TPU v7x, 32 devices: a whole 2x2x4 slice. The times are simulated.
32 devices in a mesh: gx: 4 (over z), gy: 8 (over y, x, core).
Axes of the slice: x: 2, y: 2, z: 4, core: 2. Of those that a mesh axis runs over, the one named last changes fastest.
Arguments:
- tokens: bfloat16 [33856, 768], P(('gx', 'gy')), may hold values from -6 to 6
- lengths: int32 [64], P(('gx', 'gy')), may hold values from 40 to 529, as said below
- key_mask: int32 [64, 529], P(('gx', 'gy')), may hold values 0 or 1
- ln1_gain: bfloat16 [768], P(('gx', 'gy')), may hold values from 0.5 to 1.5
- ln1_bias: bfloat16 [768], P(('gx', 'gy')), may hold values from -1.1953125 to 1.1953125
- q_weight: bfloat16 [768, 768], P(('gx', 'gy')), may hold values from -0.21875 to 0.21875
- q_bias: bfloat16 [768], P(('gx', 'gy')), may hold values from -1.1953125 to 1.1953125
- k_weight: bfloat16 [768, 768], P(('gx', 'gy')), may hold values from -0.21875 to 0.21875
- v_weight: bfloat16 [768, 768], P(('gx', 'gy')), may hold values from -0.21875 to 0.21875
- v_bias: bfloat16 [768], P(('gx', 'gy')), may hold values from -1.1953125 to 1.1953125
- o_weight: bfloat16 [768, 768], P(('gx', 'gy')), may hold values from -3.5 to 3.5
- o_bias: bfloat16 [768], P(('gx', 'gy')), may hold values from -1.1953125 to 1.1953125
- ln2_gain: bfloat16 [768], P(('gx', 'gy')), may hold values from 0.5 to 1.5
- ln2_bias: bfloat16 [768], P(('gx', 'gy')), may hold values from -1.1953125 to 1.1953125
- up_weight: bfloat16 [768, 3072], P(('gx', 'gy')), may hold values from -0.21875 to 0.21875
- up_bias: bfloat16 [3072], P(('gx', 'gy')), may hold values from -1.1953125 to 1.1953125
- down_weight: bfloat16 [3072, 768], P(('gx', 'gy')), may hold values from -0.21875 to 0.21875
- down_bias: bfloat16 [768], P(('gx', 'gy')), may hold values from -1.1953125 to 1.1953125
- out_grad: bfloat16 [33856, 768], P(('gx', 'gy')), may hold values from -6 to 6
Outputs:
- block_out: bfloat16 [33856, 768], P(('gx', 'gy'))
- grad_tokens: float32 [33856, 768], P(('gx', 'gy'))
- grad_ln1_gain: float32 [768], P(('gx', 'gy'))
- grad_ln1_bias: float32 [768], P(('gx', 'gy'))
- grad_q_weight: float32 [768, 768], P(('gx', 'gy'))
- grad_q_bias: float32 [768], P(('gx', 'gy'))
- grad_k_weight: float32 [768, 768], P(('gx', 'gy'))
- grad_v_weight: float32 [768, 768], P(('gx', 'gy'))
- grad_v_bias: float32 [768], P(('gx', 'gy'))
- grad_o_weight: float32 [768, 768], P(('gx', 'gy'))
- grad_o_bias: float32 [768], P(('gx', 'gy'))
- grad_ln2_gain: float32 [768], P(('gx', 'gy'))
- grad_ln2_bias: float32 [768], P(('gx', 'gy'))
- grad_up_weight: float32 [768, 3072], P(('gx', 'gy'))
- grad_up_bias: float32 [3072], P(('gx', 'gy'))
- grad_down_weight: float32 [3072, 768], P(('gx', 'gy'))
- grad_down_bias: float32 [768], P(('gx', 'gy'))
Inputs may be any that keep to these rules, and one draw needn't show every extreme that they name: `lengths`: most strips are nearly full, and strip 0 holds 529 filled slots.
All inputs are finite; a program needn't handle non-finite values. No bound on the sum of `key_mask` on one device may be relied on, other than what follows from the above.
Results may differ from a plain program's by a relative error of at most 0.012.
Values may be sent and summed in bfloat16 or wider, within the bound.
A program may use at most 192 MiB of HBM per device.

v0:
```python
import math

import jax
import jax.numpy as jnp
from jax import lax
from jax.sharding import PartitionSpec as P

HEAD_DIM = 64


EPSILON = 1e-06
NEG_FILL = -1e30


def layer_norm(values, gain_vec, bias_vec):
    center = values - jnp.mean(values, axis=-1, keepdims=True)
    spread = jnp.mean(center * center, axis=-1, keepdims=True)
    return center * lax.rsqrt(spread + EPSILON) * gain_vec + bias_vec


def gelu_exact(values):
    return jax.nn.gelu(values, approximate=False)


def right_mul(left_arg, right_arg):
    return jnp.dot(left_arg, right_arg, preferred_element_type=jnp.float32)


def left_mul(left_arg, right_arg):
    return lax.dot_general(
        left_arg, right_arg, (((0,), (0,)), ((), ())), preferred_element_type=jnp.float32
    )


def back_mul(left_arg, right_arg):
    return lax.dot_general(
        left_arg, right_arg, (((1,), (1,)), ((), ())), preferred_element_type=jnp.float32
    )


def collect(
    ln1_gain,
    ln1_bias,
    q_weight,
    q_bias,
    k_weight,
    v_weight,
    v_bias,
    o_weight,
    o_bias,
    ln2_gain,
    ln2_bias,
    up_weight,
    up_bias,
    down_weight,
    down_bias,
):
    return (
        lax.all_gather(ln1_gain, ("gx", "gy"), axis=0, tiled=True),
        lax.all_gather(ln1_bias, ("gx", "gy"), axis=0, tiled=True),
        lax.all_gather(q_weight, ("gx", "gy"), axis=0, tiled=True),
        lax.all_gather(q_bias, ("gx", "gy"), axis=0, tiled=True),
        lax.all_gather(k_weight, ("gx", "gy"), axis=0, tiled=True),
        lax.all_gather(v_weight, ("gx", "gy"), axis=0, tiled=True),
        lax.all_gather(v_bias, ("gx", "gy"), axis=0, tiled=True),
        lax.all_gather(o_weight, ("gx", "gy"), axis=0, tiled=True),
        lax.all_gather(o_bias, ("gx", "gy"), axis=0, tiled=True),
        lax.all_gather(ln2_gain, ("gx", "gy"), axis=0, tiled=True),
        lax.all_gather(ln2_bias, ("gx", "gy"), axis=0, tiled=True),
        lax.all_gather(up_weight, ("gx", "gy"), axis=0, tiled=True),
        lax.all_gather(up_bias, ("gx", "gy"), axis=0, tiled=True),
        lax.all_gather(down_weight, ("gx", "gy"), axis=0, tiled=True),
        lax.all_gather(down_bias, ("gx", "gy"), axis=0, tiled=True),
    )


def spread_grads(
    grad_g1,
    grad_b1,
    grad_wq,
    grad_bq,
    grad_wk,
    grad_wv,
    grad_bv,
    grad_wo,
    grad_bo,
    grad_g2,
    grad_b2,
    grad_wup,
    grad_bup,
    grad_wdown,
    grad_bdown,
):
    return (
        lax.psum_scatter(grad_g1, ("gx", "gy"), scatter_dimension=0, tiled=True),
        lax.psum_scatter(grad_b1, ("gx", "gy"), scatter_dimension=0, tiled=True),
        lax.psum_scatter(grad_wq, ("gx", "gy"), scatter_dimension=0, tiled=True),
        lax.psum_scatter(grad_bq, ("gx", "gy"), scatter_dimension=0, tiled=True),
        lax.psum_scatter(grad_wk, ("gx", "gy"), scatter_dimension=0, tiled=True),
        lax.psum_scatter(grad_wv, ("gx", "gy"), scatter_dimension=0, tiled=True),
        lax.psum_scatter(grad_bv, ("gx", "gy"), scatter_dimension=0, tiled=True),
        lax.psum_scatter(grad_wo, ("gx", "gy"), scatter_dimension=0, tiled=True),
        lax.psum_scatter(grad_bo, ("gx", "gy"), scatter_dimension=0, tiled=True),
        lax.psum_scatter(grad_g2, ("gx", "gy"), scatter_dimension=0, tiled=True),
        lax.psum_scatter(grad_b2, ("gx", "gy"), scatter_dimension=0, tiled=True),
        lax.psum_scatter(grad_wup, ("gx", "gy"), scatter_dimension=0, tiled=True),
        lax.psum_scatter(grad_bup, ("gx", "gy"), scatter_dimension=0, tiled=True),
        lax.psum_scatter(grad_wdown, ("gx", "gy"), scatter_dimension=0, tiled=True),
        lax.psum_scatter(grad_bdown, ("gx", "gy"), scatter_dimension=0, tiled=True),
    )


def shards(
    tokens,
    lengths,
    key_mask,
    ln1_gain,
    ln1_bias,
    q_weight,
    q_bias,
    k_weight,
    v_weight,
    v_bias,
    o_weight,
    o_bias,
    ln2_gain,
    ln2_bias,
    up_weight,
    up_bias,
    down_weight,
    down_bias,
    out_grad,
):
    gathered = collect(
        ln1_gain,
        ln1_bias,
        q_weight,
        q_bias,
        k_weight,
        v_weight,
        v_bias,
        o_weight,
        o_bias,
        ln2_gain,
        ln2_bias,
        up_weight,
        up_bias,
        down_weight,
        down_bias,
    )
    row_count = tokens.shape[0]
    feature_count = tokens.shape[1]
    strip_count = lengths.shape[0]
    slot_count = row_count // strip_count
    head_count = feature_count // HEAD_DIM
    score_scale = 1.0 / math.sqrt(HEAD_DIM)
    slot_ids = lax.iota(jnp.int32, slot_count)
    visible = (slot_ids[None, :] == 0) | (slot_ids[None, :] < lengths[:, None]) & (key_mask == 1)

    def split_heads(values):
        return values.reshape(strip_count, slot_count, head_count, HEAD_DIM)

    gain_one = gathered[0].astype(jnp.float32)
    bias_one = gathered[1].astype(jnp.float32)
    gain_two = gathered[9].astype(jnp.float32)
    bias_two = gathered[10].astype(jnp.float32)
    inputs = tokens.astype(jnp.float32)
    normed = layer_norm(inputs, gain_one, bias_one).astype(jnp.bfloat16)
    queries = (right_mul(normed, gathered[2]) + gathered[3].astype(jnp.float32)).astype(
        jnp.bfloat16
    )
    key_rows = right_mul(normed, gathered[4]).astype(jnp.bfloat16)
    value_rows = (right_mul(normed, gathered[5]) + gathered[6].astype(jnp.float32)).astype(
        jnp.bfloat16
    )

    def attend(pieces):
        queries_in, keys_in, values_in, visible_in = pieces
        scores = (
            jnp.einsum("qhd,khd->hqk", queries_in, keys_in, preferred_element_type=jnp.float32)
            * score_scale
        )
        scores = jnp.where(visible_in[None, None, :], scores, NEG_FILL)
        row_max = jnp.max(scores, axis=-1, keepdims=True)
        powers = jnp.exp(scores - row_max)
        row_sum = jnp.sum(powers, axis=-1, keepdims=True)
        attn_low = (powers / row_sum).astype(jnp.bfloat16)
        context = jnp.einsum(
            "hqk,khd->qhd", attn_low, values_in, preferred_element_type=jnp.float32
        )
        return (context, row_max + jnp.log(row_sum))

    context, log_sums = lax.map(
        attend, (split_heads(queries), split_heads(key_rows), split_heads(value_rows), visible)
    )
    context = context.reshape(row_count, feature_count).astype(jnp.bfloat16)
    residual = inputs + right_mul(context, gathered[7]) + gathered[8].astype(jnp.float32)
    normed2 = layer_norm(residual, gain_two, bias_two).astype(jnp.bfloat16)
    hidden = right_mul(normed2, gathered[11]) + gathered[12].astype(jnp.float32)
    active = gelu_exact(hidden).astype(jnp.bfloat16)
    mlp_out = right_mul(active, gathered[13]) + gathered[14].astype(jnp.float32)
    block_out = (residual + mlp_out).astype(jnp.bfloat16)
    regathered = collect(
        ln1_gain,
        ln1_bias,
        q_weight,
        q_bias,
        k_weight,
        v_weight,
        v_bias,
        o_weight,
        o_bias,
        ln2_gain,
        ln2_bias,
        up_weight,
        up_bias,
        down_weight,
        down_bias,
    )
    cotangent = out_grad.astype(jnp.float32)
    grad_wdown = left_mul(active, out_grad)
    grad_bdown = jnp.sum(cotangent, axis=0)
    grad_active = back_mul(out_grad, regathered[13])
    _, gelu_pull = jax.vjp(gelu_exact, hidden)
    grad_hidden = gelu_pull(grad_active)[0].astype(jnp.bfloat16)
    grad_wup = left_mul(normed2, grad_hidden)
    grad_bup = jnp.sum(grad_hidden.astype(jnp.float32), axis=0)
    grad_normed2 = back_mul(grad_hidden, regathered[11])
    _, second_pull = jax.vjp(layer_norm, residual, gain_two, bias_two)
    grad_res, grad_g2, grad_b2 = second_pull(grad_normed2)
    grad_res = cotangent + grad_res
    grad_att = grad_res.astype(jnp.bfloat16)
    grad_wo = left_mul(context, grad_att)
    grad_bo = jnp.sum(grad_att.astype(jnp.float32), axis=0)
    grad_context = back_mul(grad_att, regathered[7]).astype(jnp.bfloat16)

    def attend_back(pieces):
        queries_in, keys_in, values_in, visible_in, lse_in, grad_in = pieces
        scores = (
            jnp.einsum("qhd,khd->hqk", queries_in, keys_in, preferred_element_type=jnp.float32)
            * score_scale
        )
        scores = jnp.where(visible_in[None, None, :], scores, NEG_FILL)
        attn_probs = jnp.exp(scores - lse_in)
        attn_low = attn_probs.astype(jnp.bfloat16)
        grad_values = jnp.einsum(
            "hqk,qhd->khd", attn_low, grad_in, preferred_element_type=jnp.float32
        )
        grad_probs = jnp.einsum(
            "qhd,khd->hqk", grad_in, values_in, preferred_element_type=jnp.float32
        )
        row_inner = jnp.sum(attn_probs * grad_probs, axis=-1, keepdims=True)
        grad_scores = (attn_probs * (grad_probs - row_inner)).astype(jnp.bfloat16)
        grad_queries = (
            jnp.einsum("hqk,khd->qhd", grad_scores, keys_in, preferred_element_type=jnp.float32)
            * score_scale
        )
        grad_keys = (
            jnp.einsum("hqk,qhd->khd", grad_scores, queries_in, preferred_element_type=jnp.float32)
            * score_scale
        )
        return (
            grad_queries.astype(jnp.bfloat16),
            grad_keys.astype(jnp.bfloat16),
            grad_values.astype(jnp.bfloat16),
        )

    grad_queries, grad_keys, grad_values = lax.map(
        attend_back,
        (
            split_heads(queries),
            split_heads(key_rows),
            split_heads(value_rows),
            visible,
            log_sums,
            split_heads(grad_context),
        ),
    )
    grad_queries = grad_queries.reshape(row_count, feature_count)
    grad_keys = grad_keys.reshape(row_count, feature_count)
    grad_values = grad_values.reshape(row_count, feature_count)
    grad_wq = left_mul(normed, grad_queries)
    grad_wk = left_mul(normed, grad_keys)
    grad_wv = left_mul(normed, grad_values)
    grad_bq = jnp.sum(grad_queries.astype(jnp.float32), axis=0)
    grad_bv = jnp.sum(grad_values.astype(jnp.float32), axis=0)
    grad_normed = (
        back_mul(grad_queries, regathered[2])
        + back_mul(grad_keys, regathered[4])
        + back_mul(grad_values, regathered[5])
    )
    _, first_pull = jax.vjp(layer_norm, inputs, gain_one, bias_one)
    grad_inputs, grad_g1, grad_b1 = first_pull(grad_normed)
    grad_tokens = grad_res + grad_inputs
    shares = spread_grads(
        grad_g1,
        grad_b1,
        grad_wq,
        grad_bq,
        grad_wk,
        grad_wv,
        grad_bv,
        grad_wo,
        grad_bo,
        grad_g2,
        grad_b2,
        grad_wup,
        grad_bup,
        grad_wdown,
        grad_bdown,
    )
    return (block_out, grad_tokens) + tuple(shares)


def solution(mesh):
    return jax.shard_map(
        shards,
        mesh=mesh,
        in_specs=(
            P(("gx", "gy"), None),
            P(("gx", "gy")),
            P(("gx", "gy"), None),
            P(("gx", "gy")),
            P(("gx", "gy")),
            P(("gx", "gy"), None),
            P(("gx", "gy")),
            P(("gx", "gy"), None),
            P(("gx", "gy"), None),
            P(("gx", "gy")),
            P(("gx", "gy"), None),
            P(("gx", "gy")),
            P(("gx", "gy")),
            P(("gx", "gy")),
            P(("gx", "gy"), None),
            P(("gx", "gy")),
            P(("gx", "gy"), None),
            P(("gx", "gy")),
            P(("gx", "gy"), None),
        ),
        out_specs=(
            P(("gx", "gy"), None),
            P(("gx", "gy"), None),
            P(("gx", "gy")),
            P(("gx", "gy")),
            P(("gx", "gy"), None),
            P(("gx", "gy")),
            P(("gx", "gy"), None),
            P(("gx", "gy"), None),
            P(("gx", "gy")),
            P(("gx", "gy"), None),
            P(("gx", "gy")),
            P(("gx", "gy")),
            P(("gx", "gy")),
            P(("gx", "gy"), None),
            P(("gx", "gy")),
            P(("gx", "gy"), None),
            P(("gx", "gy")),
        ),
        check_vma=False,
    )
```

profile of v0, /device:TPU:0, one launch (start us, length us, event | category | flops | bytes accessed | tf_op | source)
XLA Modules:
  0.0 1127.2 jit_solution(7891332789321585317)
XLA Ops:
  18.9 42.9 %all-reduce.19 = (bf16[768]{0:T(1024)(128)(2,1)S(1)}, bf16[768]{0:T(1024)(128)(2,1)S(1)}, bf16[768]{0:T(1024)(128)(2,1)S(1)}, bf16[768]{0:T(1024)(128)(2,1)S(1)}...) all-reduce(bf16[768]{0:T(1024)(128)(2,1)S(1)} %dynamic-update-slice, ...), channel_id=1, replica_groups=mesh['gx'=4,'gy'=8] {'gx','gy'}, use_global_device_ids=true, to_apply=%add.2 | all-reduce | flops 9216 | bytes 36864
  67.8 3.0 convolution_convert_fusion.1
  70.9 4.5 reshape.193
  75.4 5.3 copy.75
  80.7 43.1 %all-gather.7.cloned.1.call-done = bf16[768,768]{1,0:T(8,128)(2,1)} async-done(((bf16[24,768]{1,0:T(8,128)(2,1)}), bf16[768,768]{1,0:T(8,128)(2,1)}) %all-gather.7.cloned.1.call-update) | async-done | bytes 1179664 | tf_op jit(solution)/shard_map/all_gather | solution.py:64
  123.8 4.7 fusion.64
  128.5 6.1 reshape.191
  134.6 6.2 copy.73
  140.8 38.7 %all-gather.9.cloned.1.call-done = bf16[768,768]{1,0:T(8,128)(2,1)} async-done(((bf16[24,768]{1,0:T(8,128)(2,1)}), bf16[768,768]{1,0:T(8,128)(2,1)}) %all-gather.9.cloned.1.call-update) | async-done | bytes 1179664 | tf_op jit(solution)/shard_map/all_gather | solution.py:61
  179.6 4.7 fusion.65
  184.3 6.1 reshape.192
  190.4 6.4 copy.74
  196.8 58.1 %while.26 = (s32[]{:T(128)}, bf16[2,529,12,64]{1,3,2,0:T(8,128)(2,1)}, f32[2,12,529,1]{2,1,3,0:T(8,128)S(1)}, bf16[2,529,12,64]{1,3,2,0:T(8,128)(2,1)}, pred[2,5...) while((s32[]{:T(128)}, ...), condition=%wide.region_5.6_spmd, body=%wide.region_2.5_spmd.sunk | while | flops 899962304 | bytes 54692004 | solution.py:193
  196.8 10.5 fusion.139
  207.4 9.3 fusion.140
  216.7 9.0 bitcast_dynamic-update-slice_fusion.4
  225.7 10.5 fusion.139
  236.3 9.3 fusion.140
  245.6 8.8 bitcast_dynamic-update-slice_fusion.4
  255.0 5.6 copy.76
  260.5 4.9 convert_element_type.120
  265.5 4.0 fusion.89
  270.1 30.4 %all-gather.15.cloned.1.call-done = bf16[768,3072]{1,0:T(8,128)(2,1)} async-done(((bf16[24,3072]{1,0:T(8,128)(2,1)}), bf16[768,3072]{1,0:T(8,128)(2,1)}) %all-gather.15.cloned.1.call-update) | async-done | bytes 4718608 | tf_op jit(solution)/shard_map/all_gather | solution.py:70
  300.5 38.0 %multiply_convert_fusion.3 = (bf16[1058,3072]{1,0:T(8,128)(2,1)}, f32[1058,3072]{1,0:T(8,128)}, f32[1058,3072]{1,0:T(8,128)}) fusion(f32[3072]{0:T(1024)S(1)} %copy-done.40, bf16[768,3072]{1,0:T(8,128)(2,1)} %all-gather.15.cloned.1.call-done, f32[1058,768]{1,0:T(8,128)S(1)} %get-tuple-element.237, f32[768]{0:T(1024)S(1)} %copy-done.37, ...), kind=kOutput, calls=%fused_computation.61 | convolution fusion | flops 5210844672 | bytes 40497424 | tf_op jit(solution)/shard_map/dot_general | solution.py:26
  338.5 26.7 %all-gather.17.cloned.1.call-done = bf16[3072,768]{1,0:T(8,128)(2,1)} async-done(((bf16[96,768]{1,0:T(8,128)(2,1)}), bf16[3072,768]{1,0:T(8,128)(2,1)}) %all-gather.17.cloned.1.call-update) | async-done | bytes 4718608 | tf_op jit(solution)/shard_map/all_gather | solution.py:72
  365.2 19.3 %convert_reduce_fusion = (f32[3072]{0:T(1024)}, bf16[1058,3072]{1,0:T(8,128)(2,1)}) fusion(f32[1058,3072]{1,0:T(8,128)} %get-tuple-element.229, f32[1058,3072]{1,0:T(8,128)} %get-tuple-element.238, bf16[1058,768]{1,0:T(8,128)(2,1)} %param.41, bf16[3072,768]{1,0:T(8,128)(2,1)} %all-gather.17.cloned.1.call-done), kind=kOutput, calls=%fused_computation.59 | convolution fusion | flops 5044270080 | bytes 38857728 | tf_op jit(solution)/shard_map/dot_general | solution.py:36
  384.5 10.7 multiply_reduce_fusion.1
  399.1 3.1 fusion.91
  402.6 2.8 convolution_convert_fusion
  405.4 4.5 reshape.190
  409.9 6.4 copy.80
  416.3 100.3 %while.27 = (s32[]{:T(128)}, bf16[2,529,12,64]{1,3,2,0:T(8,128)(2,1)}, bf16[2,529,12,64]{1,3,2,0:T(8,128)(2,1)}, bf16[2,529,12,64]{1,3,2,0:T(8,128)(2,1)}, bf16[...) while((s32[]{:T(128)}, ...), condition=%wide.region_12.13_spmd, body=%wide.region_10.12_spmd.sunk | while | flops 2181426688 | bytes 142791664 | solution.py:268
  416.4 10.1 fusion.149
  426.5 12.3 %multiply_reduce_fusion.5 = (f32[12,529]{1,0:T(8,128)S(1)}, f32[12,529,529]{1,2,0:T(8,128)}) fusion(f32[12,529,529]{1,2,0:T(8,128)} %fusion.149, f32[12,529]{1,0:T(8,128)S(1)} %dynamic-slice_bitcast_fusion.2, bf16[2,529,12,64]{1,3,2,0:T(8,128)(2,1)S(1)} %get-tuple-element.407, s32[]{:T(128)S(6)} %copy.124, ...), kind=kOutput, calls=%fused_computation.21.clone.1 | convolution fusion | flops 446619840 | bytes 28899216 | tf_op jit(solution)/shard_map/while/body/eval_jaxpr/qhd,khd->hqk/dot_general | solution.py:240
  438.8 11.6 %multiply_convert_fusion.5 = bf16[12,529,529]{1,2,0:T(8,128)(2,1)S(1)} fusion(f32[12,529,529]{1,2,0:T(8,128)} %get-tuple-element.355, f32[12,529,529]{1,2,0:T(8,128)} %fusion.149, f32[12,529]{1,0:T(8,128)S(1)} %get-tuple-element.356), kind=kLoop, calls=%fused_computation.20.clone.1 | loop fusion | flops 10074276 | bytes 33606312 | tf_op jit(solution)/shard_map/while/body/eval_jaxpr/convert_element_type | solution.py:253
  450.5 9.4 fusion.152
  459.9 3.7 fusion.151
  466.6 10.1 fusion.149
  476.7 12.3 %multiply_reduce_fusion.5 = (f32[12,529]{1,0:T(8,128)S(1)}, f32[12,529,529]{1,2,0:T(8,128)}) fusion(f32[12,529,529]{1,2,0:T(8,128)} %fusion.149, f32[12,529]{1,0:T(8,128)S(1)} %dynamic-slice_bitcast_fusion.2, bf16[2,529,12,64]{1,3,2,0:T(8,128)(2,1)S(1)} %get-tuple-element.407, s32[]{:T(128)S(6)} %copy.124, ...), kind=kOutput, calls=%fused_computation.21.clone.1 | convolution fusion | flops 446619840 | bytes 28899216 | tf_op jit(solution)/shard_map/while/body/eval_jaxpr/qhd,khd->hqk/dot_general | solution.py:240
  489.0 11.4 %multiply_convert_fusion.5 = bf16[12,529,529]{1,2,0:T(8,128)(2,1)S(1)} fusion(f32[12,529,529]{1,2,0:T(8,128)} %get-tuple-element.355, f32[12,529,529]{1,2,0:T(8,128)} %fusion.149, f32[12,529]{1,0:T(8,128)S(1)} %get-tuple-element.356), kind=kLoop, calls=%fused_computation.20.clone.1 | loop fusion | flops 10074276 | bytes 33606312 | tf_op jit(solution)/shard_map/while/body/eval_jaxpr/convert_element_type | solution.py:253
  500.4 9.3 fusion.152
  509.8 3.7 fusion.151
  513.4 1.8 fusion.150
  516.7 4.9 copy.84
  521.6 4.0 reshape.171
  525.7 3.8 fusion.76
  529.6 4.8 copy.83
  534.4 5.0 reshape.170
  539.3 5.3 fusion.78
  545.0 4.9 copy.82
  549.9 5.0 reshape.169
  554.9 5.4 fusion.80
  560.3 12.6 %fusion.75 = f32[768,3072]{1,0:T(8,128)} fusion(bf16[1058,3072]{1,0:T(8,128)(2,1)} %get-tuple-element.242, f32[1058,768]{1,0:T(8,128)} %copy-done.6, f32[768]{0:T(1024)S(1)} %copy-done.38, f32[768]{0:T(1024)S(1)} %copy-done.28, f32[1058]{0:T(1024)S(1)} %copy-done.26, f32[1058]{0:T(1024)S(1)} %copy-done.22), kind=kOutput, calls=%fused_computation.127 | convolution fusion | flops 4996333056 | bytes 19202320 | tf_op jit(solution)/shard_map/dot_general | solution.py:30
  573.2 11.2 fusion.92
  585.0 2.8 convert_reduce_fusion.3
  588.0 3.6 fusion.90
  593.4 2.3 fusion.85
  598.2 2.9 convert_reduce_fusion.2
  601.2 40.1 %all-reduce.18 = (f32[768]{0:T(1024)S(1)}, f32[768]{0:T(1024)S(1)}, f32[768]{0:T(1024)S(1)}, f32[768]{0:T(1024)S(1)}, f32[768]{0:T(1024)S(1)}, /*index=5*/f32[76...) all-reduce(f32[768]{0:T(1024)S(1)} %get-tuple-element.167, ...), channel_id=2, replica_groups=mesh['gx'=4,'gy'=8] {'gx','gy'}, use_global_device_ids=true, to_apply=%region_16.17.clone | all-reduce | flops 9216 | bytes 73728
  646.5 10.3 fusion.63
  656.8 75.6 %reduce-scatter.9.cloned.1.call-done = f32[24,768]{1,0:T(8,128)} async-done(((f32[768,768]{1,0:T(8,128)}), f32[24,768]{1,0:T(8,128)}) %reduce-scatter.9.cloned.1.call-update) | async-done | bytes 73744 | tf_op jit(solution)/shard_map/reduce_scatter | solution.py:99
  732.4 104.4 %reduce-scatter.7.cloned.1.call-done = f32[24,768]{1,0:T(8,128)} async-done(((f32[768,768]{1,0:T(8,128)}), f32[24,768]{1,0:T(8,128)}) %reduce-scatter.7.cloned.1.call-update) | async-done | bytes 73744 | tf_op jit(solution)/shard_map/reduce_scatter | solution.py:97
  836.8 141.6 %reduce-scatter.15.cloned.1.call-done = f32[24,3072]{1,0:T(8,128)} async-done(((f32[768,3072]{1,0:T(8,128)}), f32[24,3072]{1,0:T(8,128)}) %reduce-scatter.15.cloned.1.call-update) | async-done | bytes 294928 | tf_op jit(solution)/shard_map/reduce_scatter | solution.py:106
  978.4 141.4 %reduce-scatter.17.cloned.1.call-done = f32[96,768]{1,0:T(8,128)} async-done(((f32[3072,768]{1,0:T(8,128)}), f32[96,768]{1,0:T(8,128)}) %reduce-scatter.17.cloned.1.call-update) | async-done | bytes 294928 | tf_op jit(solution)/shard_map/reduce_scatter | solution.py:108
  (209 shorter events, 37.8 us)
Async XLA Ops:
  7.2 58.1 %copy-start.4 = (bf16[1058,768]{1,0:T(8,128)(2,1)S(1)}, bf16[1058,768]{1,0:T(8,128)(2,1)}, u32[]{:S(2)}) copy-start(bf16[1058,768]{1,0:T(8,128)(2,1)} %param.23) | copy-start | bytes 4875268
  7.2 59.4 %copy-start.42 = (s32[2,529]{1,0:T(2,128)S(1)}, s32[2,529]{1,0:T(2,128)}, u32[]{:S(2)}) copy-start(s32[2,529]{1,0:T(2,128)} %param.25) | copy-start | bytes 12700
  7.2 59.4 %copy-start.49 = (s32[2]{0:T(128)S(1)}, s32[2]{0:T(128)}, u32[]{:S(2)}) copy-start(s32[2]{0:T(128)} %param.24) | copy-start | bytes 28
  7.2 60.6 %all-gather.11.cloned.1.call-start = ((), (), s32[]{:S(2)}) async-start(), calls=%async_computation.8 | async-start | bytes 1216512 | tf_op jit(solution)/shard_map/all_gather | solution.py:63
  8.0 115.9 %all-gather.7.cloned.1.call-start = ((), (), s32[]{:S(2)}) async-start(), calls=%async_computation.6 | async-start | bytes 1216512 | tf_op jit(solution)/shard_map/all_gather | solution.py:64
  8.7 170.9 %all-gather.9.cloned.1.call-start = ((), (), s32[]{:S(2)}) async-start(), calls=%async_computation.7 | async-start | bytes 1216512 | tf_op jit(solution)/shard_map/all_gather | solution.py:61
  9.4 256.0 %all-gather.13.cloned.1.call-start = ((), (), s32[]{:S(2)}) async-start(), calls=%async_computation.9 | async-start | bytes 1216512 | tf_op jit(solution)/shard_map/all_gather | solution.py:66
  10.0 290.5 %all-gather.15.cloned.1.call-start = ((), (), s32[]{:S(2)}) async-start(), calls=%async_computation.10 | async-start | bytes 4866048 | tf_op jit(solution)/shard_map/all_gather | solution.py:70
  10.6 354.6 %all-gather.17.cloned.1.call-start = ((), (), s32[]{:S(2)}) async-start(), calls=%async_computation.11 | async-start | bytes 4866048 | tf_op jit(solution)/shard_map/all_gather | solution.py:72
  11.2 645.6 %reduce-scatter.13.cloned.1.call-start = ((), (), s32[]{:S(2)}) async-start(), calls=%async_computation.15 | async-start | bytes 2433024 | tf_op jit(solution)/shard_map/reduce_scatter | solution.py:102
  61.7 117.8 %copy-start.35 = (f32[768]{0:T(1024)}, f32[768]{0:T(1024)S(1)}, u32[]{:S(2)}) copy-start(f32[768]{0:T(1024)S(1)} %convert_element_type.111) | copy-start | bytes 9220
  61.7 117.8 %copy-start.43 = (f32[768]{0:T(1024)}, f32[768]{0:T(1024)S(1)}, u32[]{:S(2)}) copy-start(f32[768]{0:T(1024)S(1)} %convert_element_type.112) | copy-start | bytes 9220
  65.3 114.3 %copy-start.23 = (f32[1058]{0:T(1024)}, f32[1058]{0:T(1024)S(1)}, u32[]{:S(2)}) copy-start(f32[1058]{0:T(1024)S(1)} %broadcast_multiply_fusion.1) | copy-start | bytes 12700
  65.9 113.7 %copy-start.29 = (f32[1058]{0:T(1024)}, f32[1058]{0:T(1024)S(1)}, u32[]{:S(2)}) copy-start(f32[1058]{0:T(1024)S(1)} %fusion.72) | copy-start | bytes 12700
  207.4 9.3 copy-start.9
  236.3 9.3 copy-start.9
  254.9 10.5 copy-start
  254.9 10.5 copy-start.17
  254.9 10.5 copy-start.19
  254.9 10.5 copy-start.45
  269.5 125.7 %copy-start.6 = (f32[1058,768]{1,0:T(8,128)}, f32[1058,768]{1,0:T(8,128)S(1)}, u32[]{:S(2)}) copy-start(f32[1058,768]{1,0:T(8,128)S(1)} %get-tuple-element.237) | copy-start | bytes 9750532
  269.5 31.0 %copy-start.27 = (f32[768]{0:T(1024)S(1)}, f32[768]{0:T(1024)}, u32[]{:S(2)}) copy-start(f32[768]{0:T(1024)} %convert_element_type.122) | copy-start | bytes 9220
  269.5 31.0 %copy-start.37 = (f32[768]{0:T(1024)S(1)}, f32[768]{0:T(1024)}, u32[]{:S(2)}) copy-start(f32[768]{0:T(1024)} %convert_element_type.123) | copy-start | bytes 9220
  269.5 31.0 %copy-start.40 = (f32[3072]{0:T(1024)S(1)}, f32[3072]{0:T(1024)}, u32[]{:S(2)}) copy-start(f32[3072]{0:T(1024)} %convert_element_type.125) | copy-start | bytes 36868
  269.6 125.7 %copy-start.21 = (f32[1058]{0:T(1024)}, f32[1058]{0:T(1024)S(1)}, u32[]{:S(2)}) copy-start(f32[1058]{0:T(1024)S(1)} %broadcast_multiply_fusion) | copy-start | bytes 12700
  270.1 125.1 %copy-start.25 = (f32[1058]{0:T(1024)}, f32[1058]{0:T(1024)S(1)}, u32[]{:S(2)}) copy-start(f32[1058]{0:T(1024)S(1)} %fusion.73) | copy-start | bytes 12700
  395.2 1.4 copy-start.12
  396.4 1.7 copy-start.7
  396.4 1.7 copy-start.31
  396.7 2.4 copy-start.15
  402.2 254.6 %reduce-scatter.11.cloned.1.call-start = ((), (), s32[]{:S(2)}) async-start(), calls=%async_computation.14 | async-start | bytes 2433024 | tf_op jit(solution)/shard_map/reduce_scatter | solution.py:100
  409.9 6.4 copy-start.1
  409.9 6.4 copy-start.18
  409.9 6.4 copy-start.20
  416.4 10.1 copy-start.2
  438.8 11.7 %copy-start.3 = (bf16[2,529,12,64]{1,3,2,0:T(8,128)(2,1)S(1)}, bf16[2,529,12,64]{1,3,2,0:T(8,128)(2,1)}, u32[]{:S(2)}) copy-start(bf16[2,529,12,64]{1,3,2,0:T(8,128)(2,1)} %get-tuple-element.411) | copy-start | bytes 4875268 | tf_op jit(solution)/shard_map/while
  459.9 3.7 copy-start.10
  466.6 10.1 copy-start.2
  489.0 11.4 %copy-start.3 = (bf16[2,529,12,64]{1,3,2,0:T(8,128)(2,1)S(1)}, bf16[2,529,12,64]{1,3,2,0:T(8,128)(2,1)}, u32[]{:S(2)}) copy-start(bf16[2,529,12,64]{1,3,2,0:T(8,128)(2,1)} %get-tuple-element.411) | copy-start | bytes 4875268 | tf_op jit(solution)/shard_map/while
  509.8 3.7 copy-start.10
  516.6 9.0 copy-start.5
  516.6 9.0 copy-start.24
  516.7 9.0 copy-start.30
  516.7 9.0 copy-start.36
  516.7 9.0 copy-start.44
  529.5 202.9 %reduce-scatter.9.cloned.1.call-start = ((), (), s32[]{:S(2)}) async-start(), calls=%async_computation.13 | async-start | bytes 2433024 | tf_op jit(solution)/shard_map/reduce_scatter | solution.py:99
  544.7 292.1 %reduce-scatter.7.cloned.1.call-start = ((), (), s32[]{:S(2)}) async-start(), calls=%async_computation.12 | async-start | bytes 2433024 | tf_op jit(solution)/shard_map/reduce_scatter | solution.py:97
  554.8 5.4 copy-start.22
  554.8 5.5 copy-start.26
  554.8 5.5 copy-start.28
  554.9 5.5 copy-start.38
  560.2 418.1 %reduce-scatter.15.cloned.1.call-start = ((), (), s32[]{:S(2)}) async-start(), calls=%async_computation.16 | async-start | bytes 9732096 | tf_op jit(solution)/shard_map/reduce_scatter | solution.py:106
  572.9 546.9 %reduce-scatter.17.cloned.1.call-start = ((), (), s32[]{:S(2)}) async-start(), calls=%async_computation.17 | async-start | bytes 9732096 | tf_op jit(solution)/shard_map/reduce_scatter | solution.py:108
  588.0 3.6 copy-start.14
  588.0 3.6 copy-start.50
  591.7 1.7 copy-start.16
  593.4 2.4 copy-start.34
  595.7 2.0 copy-start.8
  595.7 2.5 copy-start.13
  595.7 2.5 copy-start.32
  598.2 2.9 copy-start.39
  598.2 2.9 copy-start.41
  598.2 2.9 copy-start.46
  598.2 2.9 copy-start.47
  (4 other events, 3.8 us)
Sparse Core Ops, SparseCore 0:
  10.9 56.8 all-gather.10
  70.7 53.0 all-gather.6
  126.7 52.8 all-gather.8
  182.3 52.8 all-gather.12
  237.9 62.4 all-gather.14
  303.2 61.9 all-gather.16
  402.3 97.9 reduce-scatter.12
  529.6 98.0 reduce-scatter.10
  633.6 98.7 reduce-scatter.8
  738.1 98.6 reduce-scatter.6
  843.2 135.1 reduce-scatter.14
  984.7 135.0 reduce-scatter.16
where the time goes:
time: 1130 us
  waiting for transfers between devices  607 us (54%)
  matrix products  260 us (23%)
  local copies, waits for them, and re-layouts  103 us (9%)
  blocking collectives  82.9 us (7%)
  other arithmetic  56.9 us (5%)
  between operations  15.4 us (1%)
    reduce_scatter x1, waiting for transfers between devices, spread_grads(): lax.psum_scatter(grad_wup, ('gx', 'gy'), scatter_dimension=0, tiled=True)  142 us
    reduce_scatter x1, waiting for transfers between devices, spread_grads(): lax.psum_scatter(grad_wdown, ('gx', 'gy'), scatter_dimension=0, tiled=True)  141 us
    reduce_scatter x1, waiting for transfers between devices, spread_grads(): lax.psum_scatter(grad_wq, ('gx', 'gy'), scatter_dimension=0, tiled=True)  104 us
    unnamed x2, blocking collectives  82.9 us
    reduce_scatter x1, waiting for transfers between devices, spread_grads(): lax.psum_scatter(grad_wk, ('gx', 'gy'), scatter_dimension=0, tiled=True)  75.6 us
    dot_general x6, matrix products, right_mul(): return jnp.dot(left_arg, right_arg, preferred_element_type=jnp.float32)  64.8 us
    all_gather x1, waiting for transfers between devices, collect(): lax.all_gather(v_weight, ('gx', 'gy'), axis=0, tiled=True)  43.1 us
    dot_general x6, matrix products, left_mul(): lax.dot_general(left_arg, right_arg, (((0,), (0,)), ((), ())), preferred_...  41.3 us
  transfers between devices with their start and end apart: 12, of which 9 were waited for; matrix products, arithmetic and copies ran while one was open for 34% of the time, Pallas kernels for 0%

commit v1 on v0

--- a/solution.py
+++ b/solution.py
@@ -1,8 +1,11 @@
+import functools
 import math
 
 import jax
 import jax.numpy as jnp
 from jax import lax
+from jax.experimental import pallas as pl
+from jax.experimental.pallas import tpu as pltpu
 from jax.sharding import PartitionSpec as P
 
 HEAD_DIM = 64
@@ -38,79 +41,348 @@
     )
 
 
-def collect(
-    ln1_gain,
-    ln1_bias,
-    q_weight,
-    q_bias,
-    k_weight,
-    v_weight,
-    v_bias,
-    o_weight,
-    o_bias,
-    ln2_gain,
-    ln2_bias,
-    up_weight,
-    up_bias,
-    down_weight,
-    down_bias,
-):
-    return (
-        lax.all_gather(ln1_gain, ("gx", "gy"), axis=0, tiled=True),
-        lax.all_gather(ln1_bias, ("gx", "gy"), axis=0, tiled=True),
-        lax.all_gather(q_weight, ("gx", "gy"), axis=0, tiled=True),
-        lax.all_gather(q_bias, ("gx", "gy"), axis=0, tiled=True),
-        lax.all_gather(k_weight, ("gx", "gy"), axis=0, tiled=True),
-        lax.all_gather(v_weight, ("gx", "gy"), axis=0, tiled=True),
-        lax.all_gather(v_bias, ("gx", "gy"), axis=0, tiled=True),
-        lax.all_gather(o_weight, ("gx", "gy"), axis=0, tiled=True),
-        lax.all_gather(o_bias, ("gx", "gy"), axis=0, tiled=True),
-        lax.all_gather(ln2_gain, ("gx", "gy"), axis=0, tiled=True),
-        lax.all_gather(ln2_bias, ("gx", "gy"), axis=0, tiled=True),
-        lax.all_gather(up_weight, ("gx", "gy"), axis=0, tiled=True),
-        lax.all_gather(up_bias, ("gx", "gy"), axis=0, tiled=True),
-        lax.all_gather(down_weight, ("gx", "gy"), axis=0, tiled=True),
-        lax.all_gather(down_bias, ("gx", "gy"), axis=0, tiled=True),
-    )
-
-
-def spread_grads(
-    grad_g1,
-    grad_b1,
-    grad_wq,
-    grad_bq,
-    grad_wk,
-    grad_wv,
-    grad_bv,
-    grad_wo,
-    grad_bo,
-    grad_g2,
-    grad_b2,
-    grad_wup,
-    grad_bup,
-    grad_wdown,
-    grad_bdown,
-):
-    return (
-        lax.psum_scatter(grad_g1, ("gx", "gy"), scatter_dimension=0, tiled=True),
-        lax.psum_scatter(grad_b1, ("gx", "gy"), scatter_dimension=0, tiled=True),
-        lax.psum_scatter(grad_wq, ("gx", "gy"), scatter_dimension=0, tiled=True),
-        lax.psum_scatter(grad_bq, ("gx", "gy"), scatter_dimension=0, tiled=True),
-        lax.psum_scatter(grad_wk, ("gx", "gy"), scatter_dimension=0, tiled=True),
-        lax.psum_scatter(grad_wv, ("gx", "gy"), scatter_dimension=0, tiled=True),
-        lax.psum_scatter(grad_bv, ("gx", "gy"), scatter_dimension=0, tiled=True),
-        lax.psum_scatter(grad_wo, ("gx", "gy"), scatter_dimension=0, tiled=True),
-        lax.psum_scatter(grad_bo, ("gx", "gy"), scatter_dimension=0, tiled=True),
-        lax.psum_scatter(grad_g2, ("gx", "gy"), scatter_dimension=0, tiled=True),
-        lax.psum_scatter(grad_b2, ("gx", "gy"), scatter_dimension=0, tiled=True),
-        lax.psum_scatter(grad_wup, ("gx", "gy"), scatter_dimension=0, tiled=True),
-        lax.psum_scatter(grad_bup, ("gx", "gy"), scatter_dimension=0, tiled=True),
-        lax.psum_scatter(grad_wdown, ("gx", "gy"), scatter_dimension=0, tiled=True),
-        lax.psum_scatter(grad_bdown, ("gx", "gy"), scatter_dimension=0, tiled=True),
-    )
+MESH = pl.DeviceIdType.MESH
+
+
+def grid_of(mesh):
+    z_size, plane = mesh.shape["gx"], mesh.shape["gy"] // 2
+    x_size = max(n for n in range(1, plane + 1) if plane % n == 0 and n * n <= plane)
+    return z_size, plane // x_size, x_size
+
+
+class Place:
+    def __init__(self, dims):
+        self.dims = dims
+        g = lax.axis_index("gy")
+        self.z = lax.axis_index("gx")
+        self.c = lax.rem(g, 2)
+        self.x = lax.rem(lax.div(g, 2), dims[2])
+        self.y = lax.div(g, 2 * dims[2])
+
+    def at(self, axis, step):
+        here = (self.z, self.y, self.x)[axis]
+        return lax.rem(here + step, self.dims[axis])
+
+    def device(self, axis, step):
+        where = [self.z, self.y, self.x, self.c]
+        if axis == 3:
+            where[3] = 1 - self.c
+        else:
+            where[axis] = self.at(axis, step)
+        return (where[0], (where[1] * self.dims[2] + where[2]) * 2 + where[3])
+
+    def peers(self):
+        for axis in range(3):
+            for step in range(1, self.dims[axis]):
+                yield axis, step
+        yield 3, 1
+
+    def barrier(self):
+        sem = pltpu.get_barrier_semaphore()
+        count = 0
+        for axis, step in self.peers():
+            pl.semaphore_signal(sem, inc=1, device_id=self.device(axis, step), device_id_type=MESH)
+            count += 1
+        pl.semaphore_wait(sem, count)
+
+
+class Lanes:
+    def __init__(self, place, send, recv):
+        self.place, self.send, self.recv, self.used = place, send, recv, 0
+        self.all = []
+
+    def remote(self, src, dst, axis, step):
+        n = self.used
+        self.used += 1
+        copy = pltpu.make_async_remote_copy(
+            src_ref=src, dst_ref=dst, send_sem=self.send.at[n], recv_sem=self.recv.at[n],
+            device_id=self.place.device(axis, step), device_id_type=MESH,
+        )
+        self.all.append(copy)
+        return copy
+
+
+def gather_copies(dims):
+    z, y, x = dims
+    return (z - 1) + 3 * (max(x, y) - 1) + 3 * (max(x, y) - 1) + 1
+
+
+class Gather:
+    def __init__(self, lanes, shard, buf, first, local_sem):
+        p, dims = lanes.place, lanes.place.dims
+        second = 3 - first
+        own = buf.at[p.z, p.y, p.x, p.c]
+        self.local = pltpu.make_async_copy(shard, own, local_sem)
+        self.along_z = [lanes.remote(shard, own, 0, s) for s in range(1, dims[0])]
+
+        def column(step):
+            where = [p.y, p.x]
+            where[first - 1] = p.at(first, step)
+            return buf.at[:, where[0], where[1], p.c]
+
+        def sheet(step):
+            if second == 1:
+                return buf.at[:, p.at(1, step), :, p.c]
+            return buf.at[:, :, p.at(2, step), p.c]
+
+        self.along_first = [lanes.remote(column(0), column(0), first, s) for s in range(1, dims[first])]
+        self.core_one = [lanes.remote(column(0), column(0), 3, 1)]
+        self.along_second = [lanes.remote(sheet(0), sheet(0), second, s) for s in range(1, dims[second])]
+        self.core_two = [lanes.remote(column(s), column(s), 3, 1) for s in range(1, dims[first])]
+        self.core_three = [lanes.remote(sheet(s), sheet(s), 3, 1) for s in range(1, dims[second])]
+
+    def start(self):
+        for copy in self.along_z:
+            copy.start()
+        self.local.start()
+
+    def plane_first(self):
+        self.local.wait()
+        for copy in self.along_z:
+            copy.wait_recv()
+        for copy in self.along_first + self.core_one:
+            copy.start()
+
+    def plane_second(self):
+        for copy in self.along_first:
+            copy.wait_recv()
+        for copy in self.along_second + self.core_two:
+            copy.start()
+
+    def other_core(self):
+        for copy in self.along_second:
+            copy.wait_recv()
+        for copy in self.core_three:
+            copy.start()
+
+    def arrived(self):
+        for copy in self.core_one + self.core_two + self.core_three:
+            copy.wait_recv()
+
+    def drain(self):
+        for copy in self.along_z + self.along_first + self.core_one + self.along_second + self.core_two + self.core_three:
+            copy.wait_send()
+
+
+def scatter_copies(dims):
+    z, y, x = dims
+    return 1 + (z - 1) + (y - 1) + (x - 1)
+
+
+def scatter_scratch(dims, shape, dtype, first):
+    z, y, x = dims
+    n_first, n_second = (y, x) if first == 1 else (x, y)
+    return [
+        pltpu.VMEM((z, y, x) + shape, dtype),
+        pltpu.VMEM((z, y, x) + shape, dtype),
+        pltpu.VMEM((max(n_first - 1, 1), z, n_second) + shape, dtype),
+        pltpu.VMEM((max(n_second - 1, 1), z) + shape, dtype),
+        pltpu.VMEM((max(z - 1, 1),) + shape, dtype),
+    ]
+
+
+class Scatter:
+    def __init__(self, lanes, grads, out, bufs, first, local_sem):
+        p, dims = lanes.place, lanes.place.dims
+        self.p, self.dims, self.first, self.second = p, dims, first, 3 - first
+        self.out = out
+        self.mine, self.from_core, self.from_first, self.from_second, self.from_z = bufs
+        mine = self.mine
+        self.local = pltpu.make_async_copy(grads.at[:, :, :, p.c], mine, local_sem)
+        self.over_core = lanes.remote(grads.at[:, :, :, 1 - p.c], self.from_core, 3, 1)
+
+        def sheet(step):
+            if first == 1:
+                return mine.at[:, p.at(1, step)]
+            return mine.at[:, :, p.at(2, step)]
+
+        def column(step):
+            where = [p.y, p.x]
+            where[self.second - 1] = p.at(self.second, step)
+            return mine.at[:, where[0], where[1]]
+
+        self.over_first = [lanes.remote(sheet(s), self.from_first.at[s - 1], first, s) for s in range(1, dims[first])]
+        self.over_second = [
+            lanes.remote(column(s), self.from_second.at[s - 1], self.second, s) for s in range(1, dims[self.second])
+        ]
+        self.over_z = [
+            lanes.remote(mine.at[p.at(0, s), p.y, p.x], self.from_z.at[s - 1], 0, s) for s in range(1, dims[0])
+        ]
+
+    def start(self):
+        self.over_core.start()
+        self.local.start()
+
+    def add_core(self):
+        self.local.wait()
+        self.over_core.wait_recv()
+        z, y, x = self.dims
+
+        def body(n, carry):
+            at = (lax.div(n, y * x), lax.rem(lax.div(n, x), y), lax.rem(n, x))
+            both = self.mine[at].astype(jnp.float32) + self.from_core[at].astype(jnp.float32)
+            self.mine[at] = both.astype(self.mine.dtype)
+            return carry
+
+        lax.fori_loop(0, z * y * x, body, 0)
+
+    def send_first(self):
+        for copy in self.over_first:
+            copy.start()
+
+    def add_first(self):
+        for copy in self.over_first:
+            copy.wait_recv()
+        z, wide = self.dims[0], self.dims[self.second]
+
+        def body(n, carry):
+            row, other = lax.div(n, wide), lax.rem(n, wide)
+            at = (row, self.p.y, other) if self.first == 1 else (row, other, self.p.x)
+            total = self.mine[at].astype(jnp.float32)
+            for s in range(len(self.over_first)):
+                total = total + self.from_first[s, row, other].astype(jnp.float32)
+            self.mine[at] = total.astype(self.mine.dtype)
+            return carry
+
+        lax.fori_loop(0, z * wide, body, 0)
+
+    def send_second(self):
+        for copy in self.over_second:
+            copy.start()
+
+    def add_second(self):
+        for copy in self.over_second:
+            copy.wait_recv()
+
+        def body(row, carry):
+            at = (row, self.p.y, self.p.x)
+            total = self.mine[at].astype(jnp.float32)
+            for s in range(len(self.over_second)):
+                total = total + self.from_second[s, row].astype(jnp.float32)
+            self.mine[at] = total.astype(self.mine.dtype)
+            return carry
+
+        lax.fori_loop(0, self.dims[0], body, 0)
+
+    def send_z(self):
+        for copy in self.over_z:
+            copy.start()
+
+    def finish(self):
+        for copy in self.over_z:
+            copy.wait_recv()
+        total = self.mine[self.p.z, self.p.y, self.p.x].astype(jnp.float32)
+        for s in range(len(self.over_z)):
+            total = total + self.from_z[s].astype(jnp.float32)
+        self.out[...] = total
+        for copy in [self.over_core] + self.over_first + self.over_second + self.over_z:
+            copy.wait_send()
+
+VMEM_LIMIT = 60 * 1024 * 1024
+
+
+def gather_kernel(dims, count, *refs):
+    shards, bufs, (local, send, recv) = refs[:count], refs[count : 2 * count], refs[2 * count :]
+    place = Place(dims)
+    place.barrier()
+    lanes = Lanes(place, send, recv)
+    jobs = [Gather(lanes, shards[n], bufs[n], 2 - n % 2, local.at[n]) for n in range(count)]
+    for stage in ("start", "plane_first", "plane_second", "other_core", "arrived", "drain"):
+        for job in jobs:
+            getattr(job, stage)()
+
+
+def gather_all(dims, arrays):
+    count = len(arrays)
+    copies = gather_copies(dims) * count
+    return pl.pallas_call(
+        functools.partial(gather_kernel, dims, count),
+        out_shape=[jax.ShapeDtypeStruct(dims + (2,) + a.shape, a.dtype) for a in arrays],
+        in_specs=[pl.BlockSpec(memory_space=pltpu.VMEM)] * count,
+        out_specs=[pl.BlockSpec(memory_space=pl.ANY)] * count,
+        scratch_shapes=[
+            pltpu.SemaphoreType.DMA((count,)),
+            pltpu.SemaphoreType.DMA((copies,)),
+            pltpu.SemaphoreType.DMA((copies,)),
+        ],
+        compiler_params=pltpu.CompilerParams(collective_id=0, has_side_effects=True, vmem_limit_bytes=VMEM_LIMIT),
+        name="gather",
+    )(*arrays)
+
+
+def scatter_kernel(dims, count, *refs):
+    grads, outs, scratch = refs[:count], refs[count : 2 * count], refs[2 * count :]
+    local, send, recv = scratch[-3:]
+    place = Place(dims)
+    place.barrier()
+    lanes = Lanes(place, send, recv)
+    jobs = [
+        Scatter(lanes, grads[n], outs[n], scratch[5 * n : 5 * n + 5], 1 + n % 2, local.at[n]) for n in range(count)
+    ]
+    for job in jobs:
+        job.start()
+    for add, ship in (("add_core", "send_first"), ("add_first", "send_second"), ("add_second", "send_z")):
+        for n, job in enumerate(jobs):
+            getattr(job, add)()
+            if n:
+                getattr(jobs[n - 1], ship)()
+        getattr(jobs[-1], ship)()
+    for job in jobs:
+        job.finish()
+
+
+def scatter_all(dims, arrays):
+    count = len(arrays)
+    copies = scatter_copies(dims) * count
+    scratch = []
+    for n, a in enumerate(arrays):
+        scratch += scatter_scratch(dims, a.shape[4:], a.dtype, 1 + n % 2)
+    return pl.pallas_call(
+        functools.partial(scatter_kernel, dims, count),
+        out_shape=[jax.ShapeDtypeStruct(a.shape[4:], jnp.float32) for a in arrays],
+        in_specs=[pl.BlockSpec(memory_space=pl.ANY)] * count,
+        out_specs=[pl.BlockSpec(memory_space=pltpu.VMEM)] * count,
+        scratch_shapes=scratch
+        + [
+            pltpu.SemaphoreType.DMA((count,)),
+            pltpu.SemaphoreType.DMA((copies,)),
+            pltpu.SemaphoreType.DMA((copies,)),
+        ],
+        compiler_params=pltpu.CompilerParams(collective_id=1, has_side_effects=True, vmem_limit_bytes=VMEM_LIMIT),
+        name="scatter",
+    )(*arrays)
+
+
+def lane_pad(rows, width):
+    return jnp.pad(rows, ((0, 0), (0, width - rows.shape[1])))
+
+
+def pack_vectors(vectors, wide):
+    width = 128 * -(-wide.shape[0] // 128)
+    rows = lane_pad(jnp.stack(vectors).astype(jnp.float32), width)
+    last = lane_pad(wide[None].astype(jnp.float32), width)
+    return jnp.pad(jnp.concatenate([rows, last]), ((0, 15 - len(vectors)), (0, 0)))
+
+
+def unpack_vectors(block, part, wide_part):
+    flat = block.reshape((-1,) + block.shape[-2:])
+    rows = flat[:, :8, :part].transpose(1, 0, 2).reshape(8, -1)
+    return rows, flat[:, 8, :wide_part].reshape(-1)
+
+
+def pack_vector_grads(dims, vectors, wide):
+    n = 2 * dims[0] * dims[1] * dims[2]
+    part, wide_part = vectors[0].shape[0] // n, wide.shape[0] // n
+    width = 128 * -(-wide_part // 128)
+    rows = jnp.stack(vectors).reshape(8, n, part).transpose(1, 0, 2)
+    rows = jnp.pad(rows, ((0, 0), (0, 0), (0, width - part)))
+    last = jnp.pad(wide.reshape(n, 1, wide_part), ((0, 0), (0, 0), (0, width - wide_part)))
+    block = jnp.pad(jnp.concatenate([rows, last], axis=1), ((0, 0), (0, 7), (0, 0)))
+    return block.reshape(dims + (2,) + block.shape[1:])
 
 
 def shards(
+    dims,
     tokens,
     lengths,
     key_mask,
@@ -131,23 +403,16 @@
     down_bias,
     out_grad,
 ):
-    gathered = collect(
-        ln1_gain,
-        ln1_bias,
-        q_weight,
-        q_bias,
-        k_weight,
-        v_weight,
-        v_bias,
-        o_weight,
-        o_bias,
-        ln2_gain,
-        ln2_bias,
-        up_weight,
-        up_bias,
-        down_weight,
-        down_bias,
-    )
+    weights = (q_weight, k_weight, v_weight, o_weight, up_weight, down_weight)
+    vectors = (ln1_gain, ln1_bias, q_bias, v_bias, o_bias, ln2_gain, ln2_bias, down_bias)
+    *wide, packed = gather_all(dims, list(weights) + [pack_vectors(vectors, up_bias)])
+    q_full, k_full, v_full, o_full, up_full, down_full = [w.reshape((-1,) + w.shape[-1:]) for w in wide]
+    rows, up_bias_full = unpack_vectors(packed, ln1_gain.shape[0], up_bias.shape[0])
+    gathered = (
+        rows[0], rows[1], q_full, rows[2], k_full, v_full, rows[3], o_full, rows[4], rows[5], rows[6],
+        up_full, up_bias_full, down_full, rows[7],
+    )
+    regathered = gathered
     row_count = tokens.shape[0]
     feature_count = tokens.shape[1]
     strip_count = lengths.shape[0]
@@ -200,23 +465,6 @@
     active = gelu_exact(hidden).astype(jnp.bfloat16)
     mlp_out = right_mul(active, gathered[13]) + gathered[14].astype(jnp.float32)
     block_out = (residual + mlp_out).astype(jnp.bfloat16)
-    regathered = collect(
-        ln1_gain,
-        ln1_bias,
-        q_weight,
-        q_bias,
-        k_weight,
-        v_weight,
-        v_bias,
-        o_weight,
-        o_bias,
-        ln2_gain,
-        ln2_bias,
-        up_weight,
-        up_bias,
-        down_weight,
-        down_bias,
-    )
     cotangent = out_grad.astype(jnp.float32)
     grad_wdown = left_mul(active, out_grad)
     grad_bdown = jnp.sum(cotangent, axis=0)
@@ -292,29 +540,27 @@
     _, first_pull = jax.vjp(layer_norm, inputs, gain_one, bias_one)
     grad_inputs, grad_g1, grad_b1 = first_pull(grad_normed)
     grad_tokens = grad_res + grad_inputs
-    shares = spread_grads(
-        grad_g1,
-        grad_b1,
-        grad_wq,
-        grad_bq,
-        grad_wk,
-        grad_wv,
-        grad_bv,
-        grad_wo,
-        grad_bo,
-        grad_g2,
-        grad_b2,
-        grad_wup,
-        grad_bup,
-        grad_wdown,
-        grad_bdown,
-    )
-    return (block_out, grad_tokens) + tuple(shares)
+
+    def blocks(grad, like):
+        return grad.astype(jnp.bfloat16).reshape(dims + (2,) + like.shape)
+
+    vector_grads = pack_vector_grads(
+        dims, (grad_g1, grad_b1, grad_bq, grad_bv, grad_bo, grad_g2, grad_b2, grad_bdown), grad_bup
+    )
+    full = (grad_wq, grad_wk, grad_wv, grad_wo, grad_wup, grad_wdown)
+    *sums, small = scatter_all(dims, [blocks(g, w) for g, w in zip(full, weights)] + [vector_grads])
+    sum_wq, sum_wk, sum_wv, sum_wo, sum_wup, sum_wdown = sums
+    vec = [small[n, : ln1_gain.shape[0]] for n in range(8)]
+    return (
+        block_out, grad_tokens, vec[0], vec[1], sum_wq, vec[2], sum_wk, sum_wv, vec[3], sum_wo, vec[4], vec[5], vec[6],
+        sum_wup, small[8, : up_bias.shape[0]], sum_wdown, vec[7],
+    )
 
 
 def solution(mesh):
+    dims = grid_of(mesh)
     return jax.shard_map(
-        shards,
+        functools.partial(shards, dims),
         mesh=mesh,
         in_specs=(
             P(("gx", "gy"), None),

time: 1130 us -> 615 us (0.54)
  waiting for transfers between devices: 607 us -> 0 us
  Pallas kernels: 0 us -> 202 us
  blocking collectives: 82.9 us -> 0 us
  matrix products: 260 us -> 238 us
  between operations: 15.4 us -> 1.68 us
    reduce_scatter x6 -> x0, waiting for transfers between devices: 463 us -> none  [the longest x1 142 us: spread_grads(): lax.psum_scatter(grad_wup, ('gx', 'gy'), scatter_dimension=0, tiled=True)]
    pallas_call x0 -> x2, Pallas kernels: none -> 202 us  [the longest x1 101 us: gather_all(): pl.pallas_call(functools.partial(gather_kernel, dims, count), out_shape=[...]
    all_gather x6 -> x0, waiting for transfers between devices: 140 us -> none  [the longest x1 43.1 us: collect(): lax.all_gather(v_weight, ('gx', 'gy'), axis=0, tiled=True)]
    unnamed x2 -> x0, blocking collectives: 82.9 us -> none
  transfers between devices with their start and end apart: 12 -> 0, of which waited for: 9 -> 0; matrix products, arithmetic and copies ran while one was open for 34% -> 0% of each run, Pallas kernels for 0% -> 0%
where the time goes in v1:
time: 615 us; the launch traced here: 607 us
  matrix products  238 us (39%)
  Pallas kernels  202 us (33%)
  local copies, waits for them, and re-layouts  102 us (17%)
  other arithmetic  62.2 us (10%)
    pallas_call x1, Pallas kernels, gather_all(): pl.pallas_call(functools.partial(gather_kernel, dims, count), out_shape=[...  101 us
    pallas_call x1, Pallas kernels, scatter_all(): pl.pallas_call(functools.partial(scatter_kernel, dims, count), out_shape=...  101 us
    dot_general x6, matrix products, right_mul(): return jnp.dot(left_arg, right_arg, preferred_element_type=jnp.float32)  61 us
    dot_general x6, matrix products, back_mul(): lax.dot_general(left_arg, right_arg, (((1,), (1,)), ((), ())), preferred_...  33.3 us
    dot_general x6, matrix products, left_mul(): lax.dot_general(left_arg, right_arg, (((0,), (0,)), ((), ())), preferred_...  30.3 us
    dot_general x2, matrix products, attend_back(): jnp.einsum('qhd,khd->hqk', queries_in, keys_in, preferred_element_type=jn...  24.4 us
    convert_element_type x2, other arithmetic, attend_back(): grad_scores = (attn_probs * (grad_probs - row_inner)).astype(jnp.bfloat16)  22.6 us
    dot_general x2, matrix products, attend(): jnp.einsum('qhd,khd->hqk', queries_in, keys_in, preferred_element_type=jn...  21.1 us

profile of v1, /device:TPU:0, one launch (start us, length us, event | category | flops | bytes accessed | tf_op | source)
XLA Modules:
  0.0 606.8 jit_solution(4630844016088156766)
XLA Ops:
  3.6 1.7 convert_reduce_fusion.1
  5.4 2.1 fusion.76
  7.5 101.3 %gather.1 = (bf16[4,2,2,2,24,768]{5,4,3,2,1,0:T(8,128)(2,1)}, bf16[4,2,2,2,24,768]{5,4,3,2,1,0:T(8,128)(2,1)}, bf16[4,2,2,2,24,768]{5,4,3,2,1,0:T(8,128)(2,1)}, ...) custom-call(bf16[24,768]{1,0:T(8,128)(2,1)} %refs_0_.1, ...), custom_call_target="tpu_custom_call" | custom-call | tf_op jit(solution)/shard_map/gather/pallas_call | solution.py:298
  114.5 4.3 fusion.71
  118.9 3.0 fusion.72
  121.9 1.8 convolution_convert_fusion.3
  123.7 4.5 reshape.266
  128.2 5.5 copy.57
  133.7 6.0 reshape.265
  139.7 6.2 %copy.56 = bf16[2,529,12,64]{1,3,2,0:T(8,128)(2,1)} copy(bf16[2,529,12,64]{3,2,1,0:T(8,128)(2,1)} %reshape.265) | data formatting | bytes 3250176 | tf_op jit(solution)/shard_map/while | solution.py:458
  145.9 6.0 reshape.264
  152.0 6.2 %copy.55 = bf16[2,529,12,64]{1,3,2,0:T(8,128)(2,1)} copy(bf16[2,529,12,64]{3,2,1,0:T(8,128)(2,1)} %reshape.264) | data formatting | bytes 3250176 | tf_op jit(solution)/shard_map/while | solution.py:458
  158.2 57.4 %while.26 = (s32[]{:T(128)}, bf16[2,529,12,64]{1,3,2,0:T(8,128)(2,1)}, f32[2,12,529,1]{2,1,3,0:T(8,128)S(1)}, bf16[2,529,12,64]{1,3,2,0:T(8,128)(2,1)}, pred[2,5...) while((s32[]{:T(128)}, ...), condition=%wide.region_5.6_spmd, body=%wide.region_2.5_spmd.sunk | while | flops 899962304 | bytes 54692004 | solution.py:458
  158.2 10.5 %fusion.144 = (f32[12,529]{1,0:T(8,128)S(1)}, f32[12,529,529]{1,2,0:T(8,128)}) fusion(pred[529]{0:T(1024)(128)(4,1)S(1)} %dynamic-slice_reduce_fusion.4, bf16[2,529,12,64]{1,3,2,0:T(8,128)(2,1)S(1)} %get-tuple-element.388, s32[]{:T(128)S(6)} %copy.92, bf16[2,529,12,64]{1,3,2,0:T(8,128)(2,1)} %get-tuple-element.387), kind=kOutput, calls=%fused_computation.3.clone.1 | convolution fusion | flops 439903680 | bytes 15425888 | tf_op jit(solution)/shard_map/while/body/eval_jaxpr/qhd,khd->hqk/dot_general | solution.py:445
  168.7 9.3 %fusion.145 = f32[12,529]{1,0:T(8,128)S(1)} fusion(f32[12,529,529]{1,2,0:T(8,128)} %get-tuple-element.352, f32[12,529]{1,0:T(8,128)S(1)} %get-tuple-element.353, pred[529]{0:T(1024)(128)(4,1)S(1)} %dynamic-slice_reduce_fusion.4), kind=kLoop, calls=%fused_computation.4.clone.1 | loop fusion | flops 13426020 | bytes 13483681 | tf_op jit(solution)/shard_map/while/body/eval_jaxpr/reduce_sum | solution.py:451
  178.1 8.8 %bitcast_dynamic-update-slice_fusion.4 = bf16[2,529,12,64]{1,3,2,0:T(8,128)(2,1)} fusion(bf16[2,529,12,64]{1,3,2,0:T(8,128)(2,1)} %get-tuple-element.375, s32[]{:T(128)S(6)} %copy.92, f32[12,529,529]{1,2,0:T(8,128)} %get-tuple-element.352, f32[12,529]{1,0:T(8,128)S(1)} %fusion.145, f32[12,529]{1,0:T(8,128)S(1)} %get-tuple-element.353, ...), kind=kOutput, calls=%fused_computation.6.clone.1 | convolution fusion | flops 446626240 | bytes 19158016 | tf_op jit(solution)/shard_map/while/body/eval_jaxpr/hqk,khd->qhd/dot_general | solution.py:453
  186.9 10.5 %fusion.144 = (f32[12,529]{1,0:T(8,128)S(1)}, f32[12,529,529]{1,2,0:T(8,128)}) fusion(pred[529]{0:T(1024)(128)(4,1)S(1)} %dynamic-slice_reduce_fusion.4, bf16[2,529,12,64]{1,3,2,0:T(8,128)(2,1)S(1)} %get-tuple-element.388, s32[]{:T(128)S(6)} %copy.92, bf16[2,529,12,64]{1,3,2,0:T(8,128)(2,1)} %get-tuple-element.387), kind=kOutput, calls=%fused_computation.3.clone.1 | convolution fusion | flops 439903680 | bytes 15425888 | tf_op jit(solution)/shard_map/while/body/eval_jaxpr/qhd,khd->hqk/dot_general | solution.py:445
  197.5 9.3 %fusion.145 = f32[12,529]{1,0:T(8,128)S(1)} fusion(f32[12,529,529]{1,2,0:T(8,128)} %get-tuple-element.352, f32[12,529]{1,0:T(8,128)S(1)} %get-tuple-element.353, pred[529]{0:T(1024)(128)(4,1)S(1)} %dynamic-slice_reduce_fusion.4), kind=kLoop, calls=%fused_computation.4.clone.1 | loop fusion | flops 13426020 | bytes 13483681 | tf_op jit(solution)/shard_map/while/body/eval_jaxpr/reduce_sum | solution.py:451
  206.8 8.8 %bitcast_dynamic-update-slice_fusion.4 = bf16[2,529,12,64]{1,3,2,0:T(8,128)(2,1)} fusion(bf16[2,529,12,64]{1,3,2,0:T(8,128)(2,1)} %get-tuple-element.375, s32[]{:T(128)S(6)} %copy.92, f32[12,529,529]{1,2,0:T(8,128)} %get-tuple-element.352, f32[12,529]{1,0:T(8,128)S(1)} %fusion.145, f32[12,529]{1,0:T(8,128)S(1)} %get-tuple-element.353, ...), kind=kOutput, calls=%fused_computation.6.clone.1 | convolution fusion | flops 446626240 | bytes 19158016 | tf_op jit(solution)/shard_map/while/body/eval_jaxpr/hqk,khd->qhd/dot_general | solution.py:453
  215.7 5.6 copy.58
  221.3 5.3 convert_element_type.126
  226.6 3.7 fusion.96
  231.6 38.1 %multiply_convert_fusion.3 = (bf16[1058,3072]{1,0:T(8,128)(2,1)}, f32[1058,3072]{1,0:T(8,128)}, f32[1058,3072]{1,0:T(8,128)}) fusion(f32[3072]{0:T(1024)S(1)} %copy-done.40, bf16[768,3072]{1,0:T(8,128)(2,1)} %bitcast.221, f32[1058,768]{1,0:T(8,128)S(1)} %get-tuple-element.246, f32[768]{0:T(1024)S(1)} %copy-done.43, f32[768]{0:T(1024)S(1)} %copy-done.39, ...), kind=kOutput, calls=%fused_computation.69 | convolution fusion | flops 5210844672 | bytes 40497424 | tf_op jit(solution)/shard_map/dot_general | solution.py:29
  269.7 17.2 %convert_reduce_fusion = (f32[3072]{0:T(1024)S(1)}, bf16[1058,3072]{1,0:T(8,128)(2,1)}) fusion(f32[1058,3072]{1,0:T(8,128)} %get-tuple-element.222, f32[1058,3072]{1,0:T(8,128)} %get-tuple-element.247, bf16[3072,768]{1,0:T(8,128)(2,1)} %bitcast.223, bf16[1058,768]{1,0:T(8,128)(2,1)S(1)} %copy-done.12), kind=kOutput, calls=%fused_computation.68 | convolution fusion | flops 5044270080 | bytes 38857728 | tf_op jit(solution)/shard_map/dot_general | solution.py:39
  286.9 10.0 %fusion.70 = bf16[1058,768]{1,0:T(8,128)(2,1)} fusion(f32[1058,768]{1,0:T(8,128)S(1)} %get-tuple-element.246, bf16[1058,3072]{1,0:T(8,128)(2,1)} %get-tuple-element.221, bf16[3072,768]{1,0:T(8,128)(2,1)} %bitcast.224, f32[768]{0:T(1024)S(1)} %copy-done.44), kind=kOutput, calls=%fused_computation.109 | convolution fusion | flops 4994707968 | bytes 16097280 | tf_op jit(solution)/shard_map/dot_general | solution.py:29
  296.9 8.4 %convolution_convert_fusion = bf16[3072,768]{1,0:T(8,128)(2,1)} fusion(bf16[1058,3072]{1,0:T(8,128)(2,1)S(1)} %copy-done.54, bf16[1058,768]{1,0:T(8,128)(2,1)S(1)} %copy-done.12), kind=kOutput, calls=%fused_computation.83 | convolution fusion | flops 4994629632 | bytes 12844032 | tf_op jit(solution)/shard_map/dot_general | solution.py:33
  305.4 5.9 multiply_reduce_fusion.1
  312.6 8.9 %convolution_convert_fusion.1 = bf16[768,3072]{1,0:T(8,128)(2,1)} fusion(bf16[1058,3072]{1,0:T(8,128)(2,1)S(1)} %copy-done.53, f32[1058,768]{1,0:T(8,128)S(1)} %get-tuple-element.246, f32[768]{0:T(1024)S(1)} %copy-done.43, f32[768]{0:T(1024)S(1)} %copy-done.39, f32[1058]{0:T(1024)S(1)} %fusion.82, f32[1058]{0:T(1024)S(1)} %broadcast_multiply_fusion), kind=kOutput, calls=%fused_computation.84 | convolution fusion | flops 4998692352 | bytes 14483728 | tf_op jit(solution)/shard_map/dot_general | solution.py:33
  323.5 2.1 convert_reduce_fusion.5
  325.7 2.7 convolution_convert_fusion.4
  329.1 2.9 convolution_convert_fusion.2
  332.0 4.5 reshape.263
  336.5 6.3 %copy.62 = bf16[2,529,12,64]{1,3,2,0:T(8,128)(2,1)} copy(bf16[2,529,12,64]{3,2,1,0:T(8,128)(2,1)} %reshape.263) | data formatting | bytes 3250176 | tf_op jit(solution)/shard_map/while | solution.py:516
  342.8 100.3 %while.27 = (s32[]{:T(128)}, bf16[2,529,12,64]{1,3,2,0:T(8,128)(2,1)}, bf16[2,529,12,64]{1,3,2,0:T(8,128)(2,1)}, bf16[2,529,12,64]{1,3,2,0:T(8,128)(2,1)}, bf16[...) while((s32[]{:T(128)}, ...), condition=%wide.region_12.13_spmd, body=%wide.region_10.12_spmd.sunk | while | flops 2181426688 | bytes 142791664 | solution.py:516
  343.3 10.1 %fusion.154 = f32[12,529,529]{1,2,0:T(8,128)} fusion(bf16[2,529,12,64]{1,3,2,0:T(8,128)(2,1)} %get-tuple-element.421, s32[]{:T(128)S(6)} %copy.102, bf16[2,529,12,64]{1,3,2,0:T(8,128)(2,1)} %get-tuple-element.420), kind=kOutput, calls=%fused_computation.34.clone.1 | convolution fusion | flops 429835776 | bytes 15399472 | tf_op jit(solution)/shard_map/while/body/eval_jaxpr/qhd,khd->hqk/dot_general | solution.py:497
  353.4 12.2 %multiply_reduce_fusion.5 = (f32[12,529]{1,0:T(8,128)S(1)}, f32[12,529,529]{1,2,0:T(8,128)}) fusion(f32[12,529,529]{1,2,0:T(8,128)} %fusion.154, f32[12,529]{1,0:T(8,128)S(1)} %dynamic-slice_bitcast_fusion.2, bf16[2,529,12,64]{1,3,2,0:T(8,128)(2,1)S(1)} %get-tuple-element.416, s32[]{:T(128)S(6)} %copy.102, ...), kind=kOutput, calls=%fused_computation.21.clone.1 | convolution fusion | flops 446619840 | bytes 28899216 | tf_op jit(solution)/shard_map/while/body/eval_jaxpr/qhd,khd->hqk/dot_general | solution.py:488
  365.6 11.3 %multiply_convert_fusion.5 = bf16[12,529,529]{1,2,0:T(8,128)(2,1)S(1)} fusion(f32[12,529,529]{1,2,0:T(8,128)} %get-tuple-element.364, f32[12,529,529]{1,2,0:T(8,128)} %fusion.154, f32[12,529]{1,0:T(8,128)S(1)} %get-tuple-element.365), kind=kLoop, calls=%fused_computation.20.clone.1 | loop fusion | flops 10074276 | bytes 33606312 | tf_op jit(solution)/shard_map/while/body/eval_jaxpr/convert_element_type | solution.py:501
  376.9 9.4 %fusion.157 = bf16[2,529,12,64]{1,3,2,0:T(8,128)(2,1)} fusion(bf16[2,529,12,64]{1,3,2,0:T(8,128)(2,1)} %get-tuple-element.404, s32[]{:T(128)S(6)} %copy.102, f32[12,529,529]{1,2,0:T(8,128)} %get-tuple-element.364, bf16[2,529,12,64]{1,3,2,0:T(8,128)(2,1)S(1)} %copy-done.3), kind=kOutput, calls=%fused_computation.29.clone.1 | convolution fusion | flops 433600128 | bytes 18433024 | tf_op jit(solution)/shard_map/while/body/eval_jaxpr/hqk,qhd->khd/dot_general | solution.py:494
  386.3 3.7 fusion.156
  390.0 1.8 fusion.155
  393.2 10.1 %fusion.154 = f32[12,529,529]{1,2,0:T(8,128)} fusion(bf16[2,529,12,64]{1,3,2,0:T(8,128)(2,1)} %get-tuple-element.421, s32[]{:T(128)S(6)} %copy.102, bf16[2,529,12,64]{1,3,2,0:T(8,128)(2,1)} %get-tuple-element.420), kind=kOutput, calls=%fused_computation.34.clone.1 | convolution fusion | flops 429835776 | bytes 15399472 | tf_op jit(solution)/shard_map/while/body/eval_jaxpr/qhd,khd->hqk/dot_general | solution.py:497
  403.3 12.2 %multiply_reduce_fusion.5 = (f32[12,529]{1,0:T(8,128)S(1)}, f32[12,529,529]{1,2,0:T(8,128)}) fusion(f32[12,529,529]{1,2,0:T(8,128)} %fusion.154, f32[12,529]{1,0:T(8,128)S(1)} %dynamic-slice_bitcast_fusion.2, bf16[2,529,12,64]{1,3,2,0:T(8,128)(2,1)S(1)} %get-tuple-element.416, s32[]{:T(128)S(6)} %copy.102, ...), kind=kOutput, calls=%fused_computation.21.clone.1 | convolution fusion | flops 446619840 | bytes 28899216 | tf_op jit(solution)/shard_map/while/body/eval_jaxpr/qhd,khd->hqk/dot_general | solution.py:488
  415.5 11.3 %multiply_convert_fusion.5 = bf16[12,529,529]{1,2,0:T(8,128)(2,1)S(1)} fusion(f32[12,529,529]{1,2,0:T(8,128)} %get-tuple-element.364, f32[12,529,529]{1,2,0:T(8,128)} %fusion.154, f32[12,529]{1,0:T(8,128)S(1)} %get-tuple-element.365), kind=kLoop, calls=%fused_computation.20.clone.1 | loop fusion | flops 10074276 | bytes 33606312 | tf_op jit(solution)/shard_map/while/body/eval_jaxpr/convert_element_type | solution.py:501
  426.8 9.3 %fusion.157 = bf16[2,529,12,64]{1,3,2,0:T(8,128)(2,1)} fusion(bf16[2,529,12,64]{1,3,2,0:T(8,128)(2,1)} %get-tuple-element.404, s32[]{:T(128)S(6)} %copy.102, f32[12,529,529]{1,2,0:T(8,128)} %get-tuple-element.364, bf16[2,529,12,64]{1,3,2,0:T(8,128)(2,1)S(1)} %copy-done.3), kind=kOutput, calls=%fused_computation.29.clone.1 | convolution fusion | flops 433600128 | bytes 18433024 | tf_op jit(solution)/shard_map/while/body/eval_jaxpr/hqk,qhd->khd/dot_general | solution.py:494
  436.1 3.6 fusion.156
  439.8 1.8 fusion.155
  443.1 3.6 copy.65
  446.6 2.5 reshape.253
  449.2 2.9 convert_reduce_fusion.3
  452.1 2.0 copy.64
  454.1 2.5 reshape.252
  456.7 5.0 copy.66
  461.6 4.3 reshape.254
  466.1 3.5 convolution_convert_fusion.5
  469.6 3.5 convolution_convert_fusion.7
  473.0 1.7 fusion.97
  474.8 1.7 convolution_add_fusion.5
  476.6 3.9 fusion.91
  480.5 3.4 convolution_convert_fusion.6
  484.0 3.8 fusion.75
  487.9 4.3 convert_reduce_fusion.2
  493.3 101.0 %scatter.1 = (f32[24,768]{1,0:T(8,128)}, f32[24,768]{1,0:T(8,128)}, f32[24,768]{1,0:T(8,128)}, f32[24,768]{1,0:T(8,128)}, f32[24,3072]{1,0:T(8,128)}, /*index=5*/f32[96,768]{1,0:T(8,128)}, f32[16,128]{1,0:T(8,128)}) custom-call(bf16[4,2,2,2,24,768]{5,4,3,2,1,0:T(8,128)(2,1)} %bitcast.205, bf16[4,2,2,2,24,768]{5,4,3,2,1,0:T(8,128)(2,1)} %bitcast.206, ...), custom_call_target="tpu_custom_call" | custom-call | tf_op jit(solution)/shard_map/scatter/pallas_call | solution.py:340
  603.1 1.7 copy.129
  604.8 1.7 copy.130
  (187 shorter events, 26.9 us)
Async XLA Ops:
  0.7 113.9 %copy-start.4 = (bf16[1058,768]{1,0:T(8,128)(2,1)S(1)}, bf16[1058,768]{1,0:T(8,128)(2,1)}, u32[]{:S(2)}) copy-start(bf16[1058,768]{1,0:T(8,128)(2,1)} %param.23) | copy-start | bytes 4875268
  5.4 116.5 %copy-start.23 = (f32[1058]{0:T(1024)}, f32[1058]{0:T(1024)S(1)}, u32[]{:S(2)}) copy-start(f32[1058]{0:T(1024)S(1)} %broadcast_multiply_fusion.1) | copy-start | bytes 12700
  7.4 101.4 %copy-start.29 = (f32[1058]{0:T(1024)}, f32[1058]{0:T(1024)S(1)}, u32[]{:S(2)}) copy-start(f32[1058]{0:T(1024)S(1)} %fusion.76) | copy-start | bytes 12700
  7.5 114.4 %copy-start.25 = (f32[1058]{0:T(1024)}, f32[1058]{0:T(1024)S(1)}, u32[]{:S(2)}) copy-start(f32[1058]{0:T(1024)S(1)} %fusion.81) | copy-start | bytes 12700
  112.2 9.6 %copy-start.33 = (f32[768]{0:T(1024)}, f32[768]{0:T(1024)S(1)}, u32[]{:S(2)}) copy-start(f32[768]{0:T(1024)S(1)} %mul.175) | copy-start | bytes 9220
  112.3 9.5 %copy-start.41 = (f32[768]{0:T(1024)}, f32[768]{0:T(1024)S(1)}, u32[]{:S(2)}) copy-start(f32[768]{0:T(1024)S(1)} %add.144) | copy-start | bytes 9220
  114.5 4.3 copy-start.49
  118.9 3.0 copy-start.47
  168.7 9.3 %copy-start.8 = (bf16[2,529,12,64]{1,3,2,0:T(8,128)(2,1)S(1)}, bf16[2,529,12,64]{1,3,2,0:T(8,128)(2,1)}, u32[]{:S(2)}) copy-start(bf16[2,529,12,64]{1,3,2,0:T(8,128)(2,1)} %get-tuple-element.385) | copy-start | bytes 4875268 | tf_op jit(solution)/shard_map/while
  197.5 9.3 %copy-start.8 = (bf16[2,529,12,64]{1,3,2,0:T(8,128)(2,1)S(1)}, bf16[2,529,12,64]{1,3,2,0:T(8,128)(2,1)}, u32[]{:S(2)}) copy-start(bf16[2,529,12,64]{1,3,2,0:T(8,128)(2,1)} %get-tuple-element.385) | copy-start | bytes 4875268 | tf_op jit(solution)/shard_map/while
  215.6 11.0 %copy-start = (bf16[2,529,12,64]{1,3,2,0:T(8,128)(2,1)}, bf16[2,529,12,64]{1,3,2,0:T(8,128)(2,1)S(1)}, u32[]{:S(2)}) copy-start(bf16[2,529,12,64]{1,3,2,0:T(8,128)(2,1)S(1)} %get-tuple-element.457) | copy-start | bytes 4875268
  215.6 11.0 %copy-start.19 = (f32[2,12,529,1]{2,1,3,0:T(8,128)}, f32[2,12,529,1]{2,1,3,0:T(8,128)S(1)}, u32[]{:S(2)}) copy-start(f32[2,12,529,1]{2,1,3,0:T(8,128)S(1)} %get-tuple-element.397) | copy-start | bytes 152356
  215.6 11.0 %copy-start.21 = (pred[2,529]{1,0:T(4,128)(4,1)}, pred[2,529]{1,0:T(4,128)(4,1)S(1)}, u32[]{:S(2)}) copy-start(pred[2,529]{1,0:T(4,128)(4,1)S(1)} %get-tuple-element.460) | copy-start | bytes 3178
  215.6 11.0 %copy-start.45 = (f32[768]{0:T(1024)S(1)}, f32[768]{0:T(1024)}, u32[]{:S(2)}) copy-start(f32[768]{0:T(1024)} %add.154) | copy-start | bytes 9220
  215.7 11.0 %copy-start.51 = (bf16[4,2,2,2,24,768]{5,4,3,2,1,0:T(8,128)(2,1)S(1)}, bf16[4,2,2,2,24,768]{5,4,3,2,1,0:T(8,128)(2,1)}, u32[]{:S(2)}) copy-start(bf16[4,2,2,2,24,768]{5,4,3,2,1,0:T(8,128)(2,1)} %get-tuple-element.128) | copy-start | bytes 3538948
  230.4 1.2 copy-start.39
  230.4 1.2 copy-start.40
  230.4 1.2 copy-start.43
  231.0 0.6 copy-start.31
  231.6 38.2 %copy-start.12 = (bf16[1058,768]{1,0:T(8,128)(2,1)S(1)}, bf16[1058,768]{1,0:T(8,128)(2,1)}, u32[]{:S(2)}) copy-start(bf16[1058,768]{1,0:T(8,128)(2,1)} %param.41) | copy-start | bytes 4875268
  269.7 17.2 %copy-start.44 = (f32[768]{0:T(1024)S(1)}, f32[768]{0:T(1024)}, u32[]{:S(2)}) copy-start(f32[768]{0:T(1024)} %add.164) | copy-start | bytes 9220
  286.9 10.0 %copy-start.54 = (bf16[1058,3072]{1,0:T(8,128)(2,1)S(1)}, bf16[1058,3072]{1,0:T(8,128)(2,1)}, u32[]{:S(2)}) copy-start(bf16[1058,3072]{1,0:T(8,128)(2,1)} %get-tuple-element.221) | copy-start | bytes 19501060
  296.9 8.4 %copy-start.46 = (bf16[4,2,2,2,24,3072]{5,4,3,2,1,0:T(8,128)(2,1)S(1)}, bf16[4,2,2,2,24,3072]{5,4,3,2,1,0:T(8,128)(2,1)}, u32[]{:S(2)}) copy-start(bf16[4,2,2,2,24,3072]{5,4,3,2,1,0:T(8,128)(2,1)} %get-tuple-element.129) | copy-start | bytes 14155780
  296.9 8.4 %copy-start.53 = (bf16[1058,3072]{1,0:T(8,128)(2,1)S(1)}, bf16[1058,3072]{1,0:T(8,128)(2,1)}, u32[]{:S(2)}) copy-start(bf16[1058,3072]{1,0:T(8,128)(2,1)} %get-tuple-element.251) | copy-start | bytes 19501060
  305.4 5.9 copy-start.32
  312.6 11.0 %copy-start.7 = (f32[1058,768]{1,0:T(8,128)}, f32[1058,768]{1,0:T(8,128)S(1)}, u32[]{:S(2)}) copy-start(f32[1058,768]{1,0:T(8,128)S(1)} %get-tuple-element.220) | copy-start | bytes 9750532
  321.5 4.2 copy-start.27
  323.5 2.1 copy-start.14
  325.6 2.7 copy-start.17
  325.7 3.4 copy-start.52
  336.5 6.3 %copy-start.1 = (bf16[2,529,12,64]{1,3,2,0:T(8,128)(2,1)S(1)}, bf16[2,529,12,64]{1,3,2,0:T(8,128)(2,1)}, u32[]{:S(2)}) copy-start(bf16[2,529,12,64]{1,3,2,0:T(8,128)(2,1)} %copy-done) | copy-start | bytes 4875268
  336.5 6.3 %copy-start.20 = (f32[2,12,529,1]{2,1,3,0:T(8,128)S(1)}, f32[2,12,529,1]{2,1,3,0:T(8,128)}, u32[]{:S(2)}) copy-start(f32[2,12,529,1]{2,1,3,0:T(8,128)} %copy-done.19) | copy-start | bytes 152356
  336.5 6.3 %copy-start.22 = (pred[2,529]{1,0:T(4,128)(4,1)S(1)}, pred[2,529]{1,0:T(4,128)(4,1)}, u32[]{:S(2)}) copy-start(pred[2,529]{1,0:T(4,128)(4,1)} %copy-done.21) | copy-start | bytes 3178
  343.3 10.1 %copy-start.2 = (bf16[2,529,12,64]{1,3,2,0:T(8,128)(2,1)S(1)}, bf16[2,529,12,64]{1,3,2,0:T(8,128)(2,1)}, u32[]{:S(2)}) copy-start(bf16[2,529,12,64]{1,3,2,0:T(8,128)(2,1)} %get-tuple-element.418) | copy-start | bytes 4875268 | tf_op jit(solution)/shard_map/while
  365.6 11.3 %copy-start.3 = (bf16[2,529,12,64]{1,3,2,0:T(8,128)(2,1)S(1)}, bf16[2,529,12,64]{1,3,2,0:T(8,128)(2,1)}, u32[]{:S(2)}) copy-start(bf16[2,529,12,64]{1,3,2,0:T(8,128)(2,1)} %get-tuple-element.420) | copy-start | bytes 4875268 | tf_op jit(solution)/shard_map/while
  386.3 3.7 copy-start.9
  391.8 1.3 copy-start.10
  393.1 10.1 %copy-start.2 = (bf16[2,529,12,64]{1,3,2,0:T(8,128)(2,1)S(1)}, bf16[2,529,12,64]{1,3,2,0:T(8,128)(2,1)}, u32[]{:S(2)}) copy-start(bf16[2,529,12,64]{1,3,2,0:T(8,128)(2,1)} %get-tuple-element.418) | copy-start | bytes 4875268 | tf_op jit(solution)/shard_map/while
  415.5 11.3 %copy-start.3 = (bf16[2,529,12,64]{1,3,2,0:T(8,128)(2,1)S(1)}, bf16[2,529,12,64]{1,3,2,0:T(8,128)(2,1)}, u32[]{:S(2)}) copy-start(bf16[2,529,12,64]{1,3,2,0:T(8,128)(2,1)} %get-tuple-element.420) | copy-start | bytes 4875268 | tf_op jit(solution)/shard_map/while
  436.1 3.7 copy-start.9
  441.6 1.3 copy-start.10
  449.2 2.9 copy-start.11
  456.7 9.4 %copy-start.5 = (bf16[1058,768]{1,0:T(8,128)(2,1)S(1)}, bf16[1058,768]{1,0:T(8,128)(2,1)}, u32[]{:S(2)}) copy-start(bf16[1058,768]{1,0:T(8,128)(2,1)} %param.23) | copy-start | bytes 4875268
  456.7 9.4 %copy-start.24 = (f32[1058]{0:T(1024)S(1)}, f32[1058]{0:T(1024)}, u32[]{:S(2)}) copy-start(f32[1058]{0:T(1024)} %copy-done.23) | copy-start | bytes 12700
  456.7 9.4 %copy-start.26 = (f32[1058]{0:T(1024)S(1)}, f32[1058]{0:T(1024)}, u32[]{:S(2)}) copy-start(f32[1058]{0:T(1024)} %copy-done.25) | copy-start | bytes 12700
  456.7 9.4 %copy-start.34 = (f32[768]{0:T(1024)S(1)}, f32[768]{0:T(1024)}, u32[]{:S(2)}) copy-start(f32[768]{0:T(1024)} %copy-done.33) | copy-start | bytes 9220
  456.7 9.4 %copy-start.42 = (f32[768]{0:T(1024)S(1)}, f32[768]{0:T(1024)}, u32[]{:S(2)}) copy-start(f32[768]{0:T(1024)} %copy-done.41) | copy-start | bytes 9220
  466.1 3.5 copy-start.16
  469.6 3.5 copy-start.50
  473.0 1.7 copy-start.15
  473.0 1.8 copy-start.48
  474.8 1.7 copy-start.18
  480.5 3.4 copy-start.30
  483.9 3.9 copy-start.13
  483.9 3.9 copy-start.28
  484.0 3.8 copy-start.6
  487.8 4.6 copy-start.38
  487.8 4.6 copy-start.37
  487.8 4.6 copy-start.36
  487.9 4.6 copy-start.35

commit v2 on v1

v2 whole, which is shorter than its diff:
```python
import functools
import math

import jax
import jax.numpy as jnp
from jax import lax
from jax.experimental import pallas as pl
from jax.experimental.pallas import tpu as pltpu
from jax.sharding import PartitionSpec as P

HEAD_DIM = 64
EPSILON = 1e-06
NEG_FILL = -1e30
VMEM_LIMIT = 63 * 1024 * 1024


def right_mul(left_arg, right_arg):
    return jnp.dot(left_arg, right_arg, preferred_element_type=jnp.float32)


def left_mul(left_arg, right_arg):
    return lax.dot_general(
        left_arg, right_arg, (((0,), (0,)), ((), ())), preferred_element_type=jnp.float32
    )


def back_mul(left_arg, right_arg):
    return lax.dot_general(
        left_arg, right_arg, (((1,), (1,)), ((), ())), preferred_element_type=jnp.float32
    )


MESH = pl.DeviceIdType.MESH


def grid_of(mesh):
    z_size, plane = mesh.shape["gx"], mesh.shape["gy"] // 2
    x_size = max(n for n in range(1, plane + 1) if plane % n == 0 and n * n <= plane)
    return z_size, plane // x_size, x_size


class Place:
    def __init__(self, dims):
        self.dims = dims
        g = lax.axis_index("gy")
        self.z = lax.axis_index("gx")
        self.c = lax.rem(g, 2)
        self.x = lax.rem(lax.div(g, 2), dims[2])
        self.y = lax.div(g, 2 * dims[2])

    def at(self, axis, step):
        here = (self.z, self.y, self.x)[axis]
        return lax.rem(here + step, self.dims[axis])

    def device(self, axis, step):
        where = [self.z, self.y, self.x, self.c]
        if axis == 3:
            where[3] = 1 - self.c
        else:
            where[axis] = self.at(axis, step)
        return (where[0], (where[1] * self.dims[2] + where[2]) * 2 + where[3])

    def peers(self):
        for axis in range(3):
            for step in range(1, self.dims[axis]):
                yield axis, step
        yield 3, 1

    def barrier(self):
        sem = pltpu.get_barrier_semaphore()
        count = 0
        for axis, step in self.peers():
            pl.semaphore_signal(sem, inc=1, device_id=self.device(axis, step), device_id_type=MESH)
            count += 1
        pl.semaphore_wait(sem, count)


class Lanes:
    def __init__(self, place, send, recv):
        self.place, self.send, self.recv, self.used = place, send, recv, 0
        self.all = []

    def remote(self, src, dst, axis, step):
        n = self.used
        self.used += 1
        copy = pltpu.make_async_remote_copy(
            src_ref=src, dst_ref=dst, send_sem=self.send.at[n], recv_sem=self.recv.at[n],
            device_id=self.place.device(axis, step), device_id_type=MESH,
        )
        self.all.append(copy)
        return copy


def gather_copies(dims):
    z, y, x = dims
    return (z - 1) + 3 * (max(x, y) - 1) + 3 * (max(x, y) - 1) + 1


class Gather:
    def __init__(self, lanes, shard, buf, first, local_sem):
        p, dims = lanes.place, lanes.place.dims
        second = 3 - first
        own = buf.at[p.z, p.y, p.x, p.c]
        self.local = pltpu.make_async_copy(shard, own, local_sem)
        self.along_z = [lanes.remote(shard, own, 0, s) for s in range(1, dims[0])]

        def column(step):
            where = [p.y, p.x]
            where[first - 1] = p.at(first, step)
            return buf.at[:, where[0], where[1], p.c]

        def sheet(step):
            if second == 1:
                return buf.at[:, p.at(1, step), :, p.c]
            return buf.at[:, :, p.at(2, step), p.c]

        self.along_first = [lanes.remote(column(0), column(0), first, s) for s in range(1, dims[first])]
        self.core_one = [lanes.remote(column(0), column(0), 3, 1)]
        self.along_second = [lanes.remote(sheet(0), sheet(0), second, s) for s in range(1, dims[second])]
        self.core_two = [lanes.remote(column(s), column(s), 3, 1) for s in range(1, dims[first])]
        self.core_three = [lanes.remote(sheet(s), sheet(s), 3, 1) for s in range(1, dims[second])]

    def start(self):
        for copy in self.along_z:
            copy.start()
        self.local.start()

    def plane_first(self):
        self.local.wait()
        for copy in self.along_z:
            copy.wait_recv()
        for copy in self.along_first + self.core_one:
            copy.start()

    def plane_second(self):
        for copy in self.along_first:
            copy.wait_recv()
        for copy in self.along_second + self.core_two:
            copy.start()

    def other_core(self):
        for copy in self.along_second:
            copy.wait_recv()
        for copy in self.core_three:
            copy.start()

    def arrived(self):
        for copy in self.core_one + self.core_two + self.core_three:
            copy.wait_recv()

    def drain(self):
        for copy in self.along_z + self.along_first + self.core_one + self.along_second + self.core_two + self.core_three:
            copy.wait_send()


def scatter_copies(dims):
    z, y, x = dims
    return 1 + (z - 1) + (y - 1) + (x - 1)


def scatter_scratch(dims, shape, dtype, first):
    z, y, x = dims
    n_first, n_second = (y, x) if first == 1 else (x, y)
    return [
        pltpu.VMEM((z, y, x) + shape, dtype),
        pltpu.VMEM((z, y, x) + shape, dtype),
        pltpu.VMEM((max(n_first - 1, 1), z, n_second) + shape, dtype),
        pltpu.VMEM((max(n_second - 1, 1), z) + shape, dtype),
        pltpu.VMEM((max(z - 1, 1),) + shape, dtype),
    ]


class Scatter:
    def __init__(self, lanes, grads, out, bufs, first, local_sem):
        p, dims = lanes.place, lanes.place.dims
        self.p, self.dims, self.first, self.second = p, dims, first, 3 - first
        self.out = out
        self.mine, self.from_core, self.from_first, self.from_second, self.from_z = bufs
        mine = self.mine
        self.local = pltpu.make_async_copy(grads.at[:, :, :, p.c], mine, local_sem)
        self.over_core = lanes.remote(grads.at[:, :, :, 1 - p.c], self.from_core, 3, 1)

        def sheet(step):
            if first == 1:
                return mine.at[:, p.at(1, step)]
            return mine.at[:, :, p.at(2, step)]

        def column(step):
            where = [p.y, p.x]
            where[self.second - 1] = p.at(self.second, step)
            return mine.at[:, where[0], where[1]]

        self.over_first = [lanes.remote(sheet(s), self.from_first.at[s - 1], first, s) for s in range(1, dims[first])]
        self.over_second = [
            lanes.remote(column(s), self.from_second.at[s - 1], self.second, s) for s in range(1, dims[self.second])
        ]
        self.over_z = [
            lanes.remote(mine.at[p.at(0, s), p.y, p.x], self.from_z.at[s - 1], 0, s) for s in range(1, dims[0])
        ]

    def start(self):
        self.over_core.start()
        self.local.start()

    def add_core(self):
        self.local.wait()
        self.over_core.wait_recv()
        z, y, x = self.dims

        def body(n, carry):
            at = (lax.div(n, y * x), lax.rem(lax.div(n, x), y), lax.rem(n, x))
            both = self.mine[at].astype(jnp.float32) + self.from_core[at].astype(jnp.float32)
            self.mine[at] = both.astype(self.mine.dtype)
            return carry

        lax.fori_loop(0, z * y * x, body, 0)

    def send_first(self):
        for copy in self.over_first:
            copy.start()

    def add_first(self):
        for copy in self.over_first:
            copy.wait_recv()
        z, wide = self.dims[0], self.dims[self.second]

        def body(n, carry):
            row, other = lax.div(n, wide), lax.rem(n, wide)
            at = (row, self.p.y, other) if self.first == 1 else (row, other, self.p.x)
            total = self.mine[at].astype(jnp.float32)
            for s in range(len(self.over_first)):
                total = total + self.from_first[s, row, other].astype(jnp.float32)
            self.mine[at] = total.astype(self.mine.dtype)
            return carry

        lax.fori_loop(0, z * wide, body, 0)

    def send_second(self):
        for copy in self.over_second:
            copy.start()

    def add_second(self):
        for copy in self.over_second:
            copy.wait_recv()

        def body(row, carry):
            at = (row, self.p.y, self.p.x)
            total = self.mine[at].astype(jnp.float32)
            for s in range(len(self.over_second)):
                total = total + self.from_second[s, row].astype(jnp.float32)
            self.mine[at] = total.astype(self.mine.dtype)
            return carry

        lax.fori_loop(0, self.dims[0], body, 0)

    def send_z(self):
        for copy in self.over_z:
            copy.start()

    def finish(self):
        for copy in self.over_z:
            copy.wait_recv()
        total = self.mine[self.p.z, self.p.y, self.p.x].astype(jnp.float32)
        for s in range(len(self.over_z)):
            total = total + self.from_z[s].astype(jnp.float32)
        self.out[...] = total
        for copy in [self.over_core] + self.over_first + self.over_second + self.over_z:
            copy.wait_send()


def layer_norm_parts(values):
    center = values - jnp.mean(values, axis=-1, keepdims=True)
    scale = lax.rsqrt(jnp.mean(center * center, axis=-1, keepdims=True) + EPSILON)
    return center * scale, scale


def layer_norm_back(grad, xhat, scale, gain):
    scaled = grad * gain
    inner = scaled - jnp.mean(scaled, axis=-1, keepdims=True)
    back = scale * (inner - xhat * jnp.mean(scaled * xhat, axis=-1, keepdims=True))
    return back, jnp.sum(grad * xhat, axis=0, keepdims=True), jnp.sum(grad, axis=0, keepdims=True)


def gelu_and_slope(v):
    size = jnp.abs(v)
    t = 1.0 / (1.0 + (0.3275911 * math.sqrt(0.5)) * size)
    bell = jnp.exp(-0.5 * v * v)
    poly = ((((0.5 * 1.061405429) * t - 0.5 * 1.453152027) * t + 0.5 * 1.421413741) * t - 0.5 * 0.284496736) * t
    tail = (poly + 0.5 * 0.254829592) * t * bell
    share = jnp.where(v >= 0, 1.0 - tail, tail)
    return v * share, share + (v * (1.0 / math.sqrt(2.0 * math.pi))) * bell


def ffn_kernel(
    a_rows, b_rows, ff_tile, c_rows, tile,
    tokens, context, out_grad, o_weight, up_weight, down_weight, vectors, up_bias,
    block_out, grad_res, grad_context, grad_wo, grad_wup, grad_wdown, small, grad_bup,
    normed2, active, grad_hidden, grad_att, normed2_t,
):
    rows, width = tokens.shape
    ff = up_weight.shape[1]
    o_bias, gain, bias, down_bias = vectors[4:5, :], vectors[5:6, :], vectors[6:7, :], vectors[7:8, :]
    small[...] = jnp.zeros_like(small)

    def attended(n, carry):
        at = pl.ds(pl.multiple_of(n * a_rows, a_rows), a_rows)
        residual = tokens[at, :].astype(jnp.float32) + right_mul(context[at, :], o_weight[...]) + o_bias
        grad_res[at, :] = residual
        xhat, _ = layer_norm_parts(residual)
        normed2[at, :] = (xhat * gain + bias).astype(jnp.bfloat16)
        return carry

    lax.fori_loop(0, rows // a_rows, attended, 0)

    def hidden_tile(n, carry):
        cols = pl.ds(pl.multiple_of(n * ff_tile, ff_tile), ff_tile)
        sums = jnp.zeros((1, ff_tile), jnp.float32)

        def piece(m, sums):
            at = pl.ds(pl.multiple_of(m * b_rows, b_rows), b_rows)
            hidden = right_mul(normed2[at, :], up_weight[:, cols]) + up_bias[:, cols]
            grad_active = back_mul(out_grad[at, :], down_weight[cols, :])
            value, slope = gelu_and_slope(hidden)
            active[at, cols] = value.astype(jnp.bfloat16)
            back = (slope * grad_active).astype(jnp.bfloat16)
            grad_hidden[at, cols] = back
            return sums + jnp.sum(back.astype(jnp.float32), axis=0, keepdims=True)

        grad_bup[:, cols] = lax.fori_loop(0, rows // b_rows, piece, sums)
        return carry

    lax.fori_loop(0, ff // ff_tile, hidden_tile, 0)

    def finish(n, carry):
        at = pl.ds(pl.multiple_of(n * c_rows, c_rows), c_rows)
        residual = grad_res[at, :]
        cotangent = out_grad[at, :].astype(jnp.float32)
        block_out[at, :] = (residual + right_mul(active[at, :], down_weight[...]) + down_bias).astype(jnp.bfloat16)
        grad = back_mul(grad_hidden[at, :], up_weight[...])
        xhat, scale = layer_norm_parts(residual)
        back, gain_sum, bias_sum = layer_norm_back(grad, xhat, scale, gain)
        total = cotangent + back
        grad_res[at, :] = total
        low = total.astype(jnp.bfloat16)
        grad_att[at, :] = low
        grad_context[at, :] = back_mul(low, o_weight[...]).astype(jnp.bfloat16)
        small[4:5, :] += jnp.sum(low.astype(jnp.float32), axis=0, keepdims=True)
        small[5:6, :] += gain_sum
        small[6:7, :] += bias_sum
        small[7:8, :] += jnp.sum(cotangent, axis=0, keepdims=True)
        return carry

    lax.fori_loop(0, rows // c_rows, finish, 0)

    def o_tile(n, carry):
        cols = pl.ds(pl.multiple_of(n * tile, tile), tile)
        normed2_t[cols, :] = normed2[:, cols].T
        grad_wo[cols, :] = left_mul(context[:, cols], grad_att[...]).astype(jnp.bfloat16)
        return carry

    lax.fori_loop(0, width // tile, o_tile, 0)

    def ff_tile_grads(n, carry):
        cols = pl.ds(pl.multiple_of(n * tile, tile), tile)
        grad_wdown[cols, :] = left_mul(active[:, cols], out_grad[...]).astype(jnp.bfloat16)
        grad_wup[:, cols] = right_mul(normed2_t[...], grad_hidden[:, cols]).astype(jnp.bfloat16)
        return carry

    lax.fori_loop(0, ff // tile, ff_tile_grads, 0)


def ffn(tokens, context, out_grad, o_weight, up_weight, down_weight, vectors, up_bias):
    rows, width = tokens.shape
    ff = up_weight.shape[1]
    low = functools.partial(jax.ShapeDtypeStruct, dtype=jnp.bfloat16)
    full = functools.partial(jax.ShapeDtypeStruct, dtype=jnp.float32)
    vmem = pl.BlockSpec(memory_space=pltpu.VMEM)
    return pl.pallas_call(
        functools.partial(ffn_kernel, rows, rows, 1024, rows // 2, width),
        out_shape=[
            low((rows, width)), full((rows, width)), low((rows, width)),
            low((width, width)), low((width, ff)), low((ff, width)), full((8, width)), full((1, ff)),
        ],
        in_specs=[vmem] * 8,
        out_specs=[vmem] * 8,
        scratch_shapes=[
            pltpu.VMEM((rows, width), jnp.bfloat16),
            pltpu.VMEM((rows, ff), jnp.bfloat16),
            pltpu.VMEM((rows, ff), jnp.bfloat16),
            pltpu.VMEM((rows, width), jnp.bfloat16),
            pltpu.VMEM((width, rows), jnp.bfloat16),
        ],
        compiler_params=pltpu.CompilerParams(vmem_limit_bytes=VMEM_LIMIT),
        name="ffn",
    )(tokens, context, out_grad, o_weight, up_weight, down_weight, vectors, up_bias)


def head_lanes(pair, head):
    lane = lax.broadcasted_iota(jnp.int32, pair.shape, 1)
    return jnp.where(lax.div(lane, HEAD_DIM) == head, pair, jnp.zeros_like(pair))


def attend_kernel(strips, tokens, q_weight, k_weight, v_weight, vectors, mask, normed, queries, keys, values, probs, context):
    rows, width = tokens.shape
    slots, pairs = rows // strips, width // 128
    step = pl.program_id(0)

    @pl.when(step == 0)
    def _():
        xhat, _ = layer_norm_parts(tokens[...].astype(jnp.float32))
        normed[...] = (xhat * vectors[0:1, :] + vectors[1:2, :]).astype(jnp.bfloat16)
        scale = 1.0 / math.sqrt(HEAD_DIM)
        low = (right_mul(normed[...], q_weight[...]) + vectors[2:3, :]).astype(jnp.bfloat16)
        queries[...] = low * jnp.bfloat16(scale)
        keys[...] = right_mul(normed[...], k_weight[...]).astype(jnp.bfloat16)
        values[...] = (right_mul(normed[...], v_weight[...]) + vectors[3:4, :]).astype(jnp.bfloat16)

    at = pl.ds(pl.multiple_of(lax.div(step, pairs) * slots, slots), slots)
    cols = pl.ds(pl.multiple_of(lax.rem(step, pairs) * 128, 128), 128)
    query, key, value = queries[at, cols], keys[at, cols], values[at, cols]
    hidden = mask[at, 0:1]
    total = jnp.zeros((slots, 128), jnp.float32)
    for head in range(2):
        scores = back_mul(key, head_lanes(query, head)) + hidden
        powers = jnp.exp(scores - jnp.max(scores, axis=0, keepdims=True))
        low = (powers * (1.0 / jnp.sum(powers, axis=0, keepdims=True))).astype(jnp.bfloat16)
        probs[0, head] = low
        total = total + left_mul(low, head_lanes(value, head))
    context[at, cols] = total.astype(jnp.bfloat16)


def attend(strips, tokens, q_weight, k_weight, v_weight, vectors, mask):
    rows, width = tokens.shape
    slots, pairs = rows // strips, width // 128
    low = functools.partial(jax.ShapeDtypeStruct, dtype=jnp.bfloat16)
    whole = pl.BlockSpec((rows, width), lambda n: (0, 0))
    return pl.pallas_call(
        functools.partial(attend_kernel, strips),
        grid=(strips * pairs,),
        out_shape=[low((rows, width))] * 4 + [low((strips * pairs, 2, slots, slots)), low((rows, width))],
        in_specs=[pl.BlockSpec(memory_space=pltpu.VMEM)] * 6,
        out_specs=[whole] * 4 + [pl.BlockSpec((1, 2, slots, slots), lambda n: (n, 0, 0, 0)), whole],
        compiler_params=pltpu.CompilerParams(vmem_limit_bytes=VMEM_LIMIT),
        name="attend",
    )(tokens, q_weight, k_weight, v_weight, vectors, mask)


def attend_back_kernel(
    strips, tokens, normed, queries, keys, values, probs, grad_context, grad_res, q_weight, k_weight, v_weight, vectors,
    grad_tokens, grad_wq, grad_wk, grad_wv, small,
    grad_q, grad_k, grad_v,
):
    rows, width = tokens.shape
    slots, pairs = rows // strips, width // 128
    step = pl.program_id(0)
    at = pl.ds(pl.multiple_of(lax.div(step, pairs) * slots, slots), slots)
    cols = pl.ds(pl.multiple_of(lax.rem(step, pairs) * 128, 128), 128)
    query, key, value, grad = queries[at, cols], keys[at, cols], values[at, cols], grad_context[at, cols]
    back_q = back_k = back_v = jnp.zeros((slots, 128), jnp.float32)
    for head in range(2):
        low = probs[0, head]
        own = head_lanes(grad, head)
        back_v = back_v + right_mul(low, own)
        wide = low.astype(jnp.float32)
        slope = back_mul(value, own)
        inner = jnp.sum(wide * slope, axis=0, keepdims=True)
        pull = (wide * (slope - inner)).astype(jnp.bfloat16)
        back_q = back_q + left_mul(pull, head_lanes(key, head))
        back_k = back_k + right_mul(pull, head_lanes(query, head))
    grad_q[at, cols] = (back_q * (1.0 / math.sqrt(HEAD_DIM))).astype(jnp.bfloat16)
    grad_k[at, cols] = back_k.astype(jnp.bfloat16)
    grad_v[at, cols] = back_v.astype(jnp.bfloat16)

    @pl.when(step == strips * pairs - 1)
    def _():
        turned = normed[...].T
        grad_wq[...] = right_mul(turned, grad_q[...]).astype(jnp.bfloat16)
        grad_wk[...] = right_mul(turned, grad_k[...]).astype(jnp.bfloat16)
        grad_wv[...] = right_mul(turned, grad_v[...]).astype(jnp.bfloat16)
        small[...] = jnp.zeros_like(small)
        small[2:3, :] = jnp.sum(grad_q[...].astype(jnp.float32), axis=0, keepdims=True)
        small[3:4, :] = jnp.sum(grad_v[...].astype(jnp.float32), axis=0, keepdims=True)

        def finish(n, carry):
            at = pl.ds(pl.multiple_of(n * slots, slots), slots)
            grad = back_mul(grad_q[at, :], q_weight[...]) + back_mul(grad_k[at, :], k_weight[...])
            grad = grad + back_mul(grad_v[at, :], v_weight[...])
            xhat, scale = layer_norm_parts(tokens[at, :].astype(jnp.float32))
            back, gain_sum, bias_sum = layer_norm_back(grad, xhat, scale, vectors[0:1, :])
            grad_tokens[at, :] = grad_res[at, :] + back
            small[0:1, :] += gain_sum
            small[1:2, :] += bias_sum
            return carry

        lax.fori_loop(0, strips, finish, 0)


def attend_back(strips, tokens, normed, queries, keys, values, probs, grad_context, grad_res, q_weight, k_weight, v_weight, vectors):
    rows, width = tokens.shape
    slots, pairs = rows // strips, width // 128
    low = functools.partial(jax.ShapeDtypeStruct, dtype=jnp.bfloat16)
    full = functools.partial(jax.ShapeDtypeStruct, dtype=jnp.float32)
    vmem = pl.BlockSpec(memory_space=pltpu.VMEM)
    block = pl.BlockSpec((1, 2, slots, slots), lambda n: (n, 0, 0, 0))
    return pl.pallas_call(
        functools.partial(attend_back_kernel, strips),
        grid=(strips * pairs,),
        out_shape=[full((rows, width)), low((width, width)), low((width, width)), low((width, width)), full((8, width))],
        in_specs=[vmem] * 5 + [block] + [vmem] * 6,
        out_specs=[vmem] * 5,
        scratch_shapes=[pltpu.VMEM((rows, width), jnp.bfloat16)] * 3,
        compiler_params=pltpu.CompilerParams(vmem_limit_bytes=VMEM_LIMIT),
        name="attend_back",
    )(tokens, normed, queries, keys, values, probs, grad_context, grad_res, q_weight, k_weight, v_weight, vectors)


def pieces_of(shapes):
    pieces = []
    for n, shape in enumerate(shapes):
        parts = max(1, shape[-1] // 768)
        if parts == 1 and shape[-2] > shapes[0][-2] and shape[-1] == 768:
            parts = 3
        for k in range(parts):
            size = shape[-1] // parts
            pieces.append((n, k * size, size, 1 + len(pieces) % 2))
    return pieces


def staggered(count, stages):
    return [(step - s, s) for step in range(count + stages - 1) for s in range(stages) if 0 <= step - s < count]


def gather_kernel(dims, pieces, count, *refs):
    shards, bufs, (local, send, recv) = refs[:count], refs[count : 2 * count], refs[2 * count :]
    place = Place(dims)
    place.barrier()
    lanes = Lanes(place, send, recv)
    jobs = [
        Gather(lanes, shards[n].at[:, pl.ds(at, size)], bufs[n].at[:, :, :, :, :, pl.ds(at, size)], first, local.at[k])
        for k, (n, at, size, first) in enumerate(pieces)
    ]
    for job in jobs:
        job.start()
    for n, stage in staggered(len(jobs), 3):
        getattr(jobs[n], ("plane_first", "plane_second", "other_core")[stage])()
    for job in jobs:
        job.arrived()
        job.drain()


def gather_all(dims, arrays):
    count = len(arrays)
    pieces = pieces_of([a.shape for a in arrays])
    copies = gather_copies(dims) * len(pieces)
    return pl.pallas_call(
        functools.partial(gather_kernel, dims, pieces, count),
        out_shape=[jax.ShapeDtypeStruct(dims + (2,) + a.shape, a.dtype) for a in arrays],
        in_specs=[pl.BlockSpec(memory_space=pltpu.VMEM)] * count,
        out_specs=[pl.BlockSpec(memory_space=pl.ANY)] * count,
        scratch_shapes=[
            pltpu.SemaphoreType.DMA((len(pieces),)),
            pltpu.SemaphoreType.DMA((copies,)),
            pltpu.SemaphoreType.DMA((copies,)),
        ],
        compiler_params=pltpu.CompilerParams(collective_id=0, has_side_effects=True, vmem_limit_bytes=VMEM_LIMIT),
        name="gather",
    )(*arrays)


def scatter_kernel(dims, pieces, count, *refs):
    grads, outs, scratch = refs[:count], refs[count : 2 * count], refs[2 * count :]
    local, send, recv = scratch[-3:]
    place = Place(dims)
    place.barrier()
    lanes = Lanes(place, send, recv)
    jobs = [
        Scatter(
            lanes, grads[n].at[:, :, :, :, :, pl.ds(at, size)], outs[n].at[:, pl.ds(at, size)],
            scratch[5 * k : 5 * k + 5], first, local.at[k],
        )
        for k, (n, at, size, first) in enumerate(pieces)
    ]
    for job in jobs:
        job.start()
    ship = ("send_first", "send_second", "send_z")
    waiting = None
    for n, stage in staggered(len(jobs), 3):
        getattr(jobs[n], ("add_core", "add_first", "add_second")[stage])()
        if waiting is not None:
            waiting()
        waiting = getattr(jobs[n], ship[stage])
    waiting()
    for job in jobs:
        job.finish()


def scatter_all(dims, arrays):
    count = len(arrays)
    pieces = pieces_of([a.shape[4:] for a in arrays])
    copies = scatter_copies(dims) * len(pieces)
    scratch = []
    for n, at, size, first in pieces:
        scratch += scatter_scratch(dims, (arrays[n].shape[4], size), arrays[n].dtype, first)
    return pl.pallas_call(
        functools.partial(scatter_kernel, dims, pieces, count),
        out_shape=[jax.ShapeDtypeStruct(a.shape[4:], jnp.float32) for a in arrays],
        in_specs=[pl.BlockSpec(memory_space=pl.ANY)] * count,
        out_specs=[pl.BlockSpec(memory_space=pltpu.VMEM)] * count,
        scratch_shapes=scratch
        + [
            pltpu.SemaphoreType.DMA((len(pieces),)),
            pltpu.SemaphoreType.DMA((copies,)),
            pltpu.SemaphoreType.DMA((copies,)),
        ],
        compiler_params=pltpu.CompilerParams(collective_id=1, has_side_effects=True, vmem_limit_bytes=VMEM_LIMIT),
        name="scatter",
    )(*arrays)


def lane_pad(rows, width):
    return jnp.pad(rows, ((0, 0), (0, width - rows.shape[1])))


def pack_vectors(vectors, wide):
    width = 128 * -(-wide.shape[0] // 128)
    rows = lane_pad(jnp.stack(vectors).astype(jnp.float32), width)
    last = lane_pad(wide[None].astype(jnp.float32), width)
    return jnp.pad(jnp.concatenate([rows, last]), ((0, 15 - len(vectors)), (0, 0)))


def unpack_vectors(block, part, wide_part):
    flat = block.reshape((-1,) + block.shape[-2:])
    rows = flat[:, :8, :part].transpose(1, 0, 2).reshape(8, -1)
    return rows, flat[:, 8, :wide_part].reshape(1, -1)


def pack_vector_grads(dims, vectors, wide):
    n = 2 * dims[0] * dims[1] * dims[2]
    part, wide_part = vectors.shape[1] // n, wide.shape[1] // n
    width = 128 * -(-wide_part // 128)
    rows = vectors.reshape(8, n, part).transpose(1, 0, 2)
    rows = jnp.pad(rows, ((0, 0), (0, 0), (0, width - part)))
    last = jnp.pad(wide.reshape(n, 1, wide_part), ((0, 0), (0, 0), (0, width - wide_part)))
    block = jnp.pad(jnp.concatenate([rows, last], axis=1), ((0, 0), (0, 7), (0, 0)))
    return block.reshape(dims + (2,) + block.shape[1:])


def shards(
    dims,
    tokens,
    lengths,
    key_mask,
    ln1_gain,
    ln1_bias,
    q_weight,
    q_bias,
    k_weight,
    v_weight,
    v_bias,
    o_weight,
    o_bias,
    ln2_gain,
    ln2_bias,
    up_weight,
    up_bias,
    down_weight,
    down_bias,
    out_grad,
):
    weights = (q_weight, k_weight, v_weight, o_weight, up_weight, down_weight)
    vectors = (ln1_gain, ln1_bias, q_bias, v_bias, o_bias, ln2_gain, ln2_bias, down_bias)
    *wide, packed = gather_all(dims, list(weights) + [pack_vectors(vectors, up_bias)])
    q_full, k_full, v_full, o_full, up_full, down_full = [w.reshape((-1,) + w.shape[-1:]) for w in wide]
    rows, up_bias_full = unpack_vectors(packed, ln1_gain.shape[0], up_bias.shape[0])

    row_count, width = tokens.shape
    strips = lengths.shape[0]
    slots = row_count // strips
    extra = -slots % 16

    def padded(values):
        return jnp.pad(values.reshape(strips, slots, width), ((0, 0), (0, extra), (0, 0))).reshape(-1, width)

    def cropped(values):
        return values.reshape(strips, slots + extra, width)[:, :slots].reshape(row_count, width)

    slot_ids = lax.iota(jnp.int32, slots)
    visible = (slot_ids[None, :] == 0) | (slot_ids[None, :] < lengths[:, None]) & (key_mask == 1)
    mask = jnp.where(jnp.pad(visible, ((0, 0), (0, extra))), 0.0, NEG_FILL).reshape(-1, 1)
    tokens_in, grads_in = padded(tokens), padded(out_grad)

    normed, queries, keys, values, probs, context = attend(strips, tokens_in, q_full, k_full, v_full, rows, mask)
    block_out, grad_res, grad_context, grad_wo, grad_wup, grad_wdown, small, grad_bup = ffn(
        tokens_in, context, grads_in, o_full, up_full, down_full, rows, up_bias_full
    )
    grad_tokens, grad_wq, grad_wk, grad_wv, small_two = attend_back(
        strips, tokens_in, normed, queries, keys, values, probs, grad_context, grad_res, q_full, k_full, v_full, rows
    )

    def blocks(grad, like):
        return grad.reshape(dims + (2,) + like.shape)

    vector_grads = pack_vector_grads(dims, small + small_two, grad_bup)
    full = (grad_wq, grad_wk, grad_wv, grad_wo, grad_wup, grad_wdown)
    *sums, least = scatter_all(dims, [blocks(g, w) for g, w in zip(full, weights)] + [vector_grads])
    sum_wq, sum_wk, sum_wv, sum_wo, sum_wup, sum_wdown = sums
    vec = [least[n, : ln1_gain.shape[0]] for n in range(8)]
    return (
        cropped(block_out), cropped(grad_tokens), vec[0], vec[1], sum_wq, vec[2], sum_wk, sum_wv, vec[3], sum_wo, vec[4],
        vec[5], vec[6], sum_wup, least[8, : up_bias.shape[0]], sum_wdown, vec[7],
    )


def solution(mesh):
    rows, flat = P(("gx", "gy"), None), P(("gx", "gy"))
    return jax.shard_map(
        functools.partial(shards, grid_of(mesh)),
        mesh=mesh,
        in_specs=(
            rows, flat, rows, flat, flat, rows, flat, rows, rows, flat, rows, flat, flat, flat, rows, flat, rows, flat, rows,
        ),
        out_specs=(
            rows, rows, flat, flat, rows, flat, rows, rows, flat, rows, flat, flat, flat, rows, flat, rows, flat,
        ),
        check_vma=False,
    )
```

time: 615 us -> 363 us (0.59)
  matrix products: 238 us -> 0 us
  Pallas kernels: 202 us -> 329 us
  local copies, waits for them, and re-layouts: 102 us -> 26.8 us
  other arithmetic: 62.2 us -> 2.79 us
    dot_general x32 -> x0, matrix products: 238 us -> none  [the longest x6 61 us: right_mul(): return jnp.dot(left_arg, right_arg, preferred_element_type=jnp.float32)]
    pallas_call x2 -> x5, Pallas kernels: 202 us -> 329 us  [the longest x1 101 us: scatter_all(): pl.pallas_call(functools.partial(scatter_kernel, dims, pieces, count), ou...]
    while x27 -> x0, local copies, waits for them, and re-layouts: 37.4 us -> none  [the longest x3 17.9 us: shards(): lax.map(attend, (split_heads(queries), split_heads(key_rows), split_heads...]
    reduce_sum x10 -> x0, other arithmetic: 37.3 us -> none  [the longest x2 18.6 us: attend(): row_sum = jnp.sum(powers, axis=-1, keepdims=True)]
    convert_element_type x2 -> x0, other arithmetic: 22.6 us -> none  [attend_back(): grad_scores = (attn_probs * (grad_probs - row_inner)).astype(jnp.bfloat16)]
    reshape x7, local copies, waits for them, and re-layouts: 30.4 us -> 9.02 us  [the longest x2 3.5 us: cropped(): values.reshape(strips, slots + extra, width)[:, :slots]]
    convert_element_type x2 -> x0, local copies, waits for them, and re-layouts: 10.9 us -> none  [shards(): context = context.reshape(row_count, feature_count).astype(jnp.bfloat16)]
    unnamed x115 -> x28, local copies, waits for them, and re-layouts: 10.5 us -> 4.13 us
where the time goes in v2:
time: 363 us; the launch traced here: 359 us
  Pallas kernels  329 us (91%)
  local copies, waits for them, and re-layouts  26.8 us (7%)
    pallas_call x1, Pallas kernels, scatter_all(): pl.pallas_call(functools.partial(scatter_kernel, dims, pieces, count), ou...  101 us
    pallas_call x1, Pallas kernels, gather_all(): pl.pallas_call(functools.partial(gather_kernel, dims, pieces, count), out...  85.5 us
    pallas_call x1, Pallas kernels, ffn(): pl.pallas_call(functools.partial(ffn_kernel, rows, rows, 1024, rows // 2,...  67.6 us
    pallas_call x1, Pallas kernels, attend_back(): pl.pallas_call(functools.partial(attend_back_kernel, strips), grid=(strip...  45.3 us
    pallas_call x1, Pallas kernels, attend(): pl.pallas_call(functools.partial(attend_kernel, strips), grid=(strips * p...  29.1 us

profile of v2, /device:TPU:0, one launch (start us, length us, event | category | flops | bytes accessed | tf_op | source)
XLA Modules:
  0.0 359.3 jit_solution(10674026746404408337)
XLA Ops:
  0.7 0.8 stack.35
  1.5 0.7 fusion.2
  2.1 0.6 pad_convert_fusion.refs_6_
  2.7 85.5 %gather.1 = (bf16[4,2,2,2,24,768]{5,4,3,2,1,0:T(8,128)(2,1)}, bf16[4,2,2,2,24,768]{5,4,3,2,1,0:T(8,128)(2,1)}, bf16[4,2,2,2,24,768]{5,4,3,2,1,0:T(8,128)(2,1)}, ...) custom-call(bf16[24,768]{1,0:T(8,128)(2,1)} %refs_0_.1, ...), custom_call_target="tpu_custom_call" | custom-call | tf_op jit(solution)/shard_map/gather/pallas_call | solution.py:555
  88.3 0.9 slice.52
  89.2 0.7 reshape.126.vectors
  89.9 1.8 reshape.120
  91.7 0.0 copy-start.8
  91.7 0.0 copy-start.9
  91.7 1.3 pad.39
  93.0 0.0 copy-done.8
  93.0 0.0 copy-done.9
  93.0 0.1 and_or_fusion
  93.1 1.2 reshape.146.mask
  94.3 29.1 %attend.1 = (bf16[1088,768]{1,0:T(8,128)(2,1)}, bf16[1088,768]{1,0:T(8,128)(2,1)}, bf16[1088,768]{1,0:T(8,128)(2,1)}, bf16[1088,768]{1,0:T(8,128)(2,1)}, bf16[12...) custom-call(bf16[1088,768]{1,0:T(8,128)(2,1)} %bitcast.52, bf16[768,768]{1,0:T(8,128)(2,1)} %bitcast.58, ...), custom_call_target="tpu_custom_call" | custom-call | tf_op jit(solution)/shard_map/attend/pallas_call | solution.py:437
  123.4 0.9 slice.53
  124.3 0.7 reshape_squeeze.3.up_bias
  125.0 1.8 reshape.128
  126.7 1.3 pad.45
  128.1 67.6 %ffn.1 = (bf16[1088,768]{1,0:T(8,128)(2,1)}, f32[1088,768]{1,0:T(8,128)}, bf16[1088,768]{1,0:T(8,128)(2,1)}, bf16[768,768]{1,0:T(8,128)(2,1)}, bf16[768,3072]{1,...) custom-call(bf16[1088,768]{1,0:T(8,128)(2,1)} %bitcast.53, ...), custom_call_target="tpu_custom_call" | custom-call | tf_op jit(solution)/shard_map/ffn/pallas_call | solution.py:378
  195.7 0.0 copy-start.6
  195.7 0.0 copy-start.7
  195.7 45.3 %attend_back.1 = (f32[1088,768]{1,0:T(8,128)}, bf16[768,768]{1,0:T(8,128)(2,1)}, bf16[768,768]{1,0:T(8,128)(2,1)}, bf16[768,768]{1,0:T(8,128)(2,1)}, f32[8,768]{1,0:T(8,128)}) custom-call(bf16[1088,768]{1,0:T(8,128)(2,1)} %bitcast.54, bf16[1088,768]{1,0:T(8,128)(2,1)} %get-tuple-element.59.normed, bf16[1088,768]{1,0:T(8,128)(2,1)} %get-tuple-element.60.queries, ...), custom_call_target="tpu_custom_call" | custom-call | tf_op jit(solution)/shard_map/attend_back/pallas_call | solution.py:505
  241.0 0.0 copy-done.6
  241.0 0.7 add.19
  241.7 0.1 reshape.143
  241.8 0.5 broadcast.39
  242.4 0.0 copy-done.7
  242.4 0.7 reduce.3
  243.0 0.1 reshape.144
  243.1 0.1 copy.46
  243.2 0.7 pad.48.clone
  244.0 101.2 %scatter.1 = (f32[24,768]{1,0:T(8,128)}, f32[24,768]{1,0:T(8,128)}, f32[24,768]{1,0:T(8,128)}, f32[24,768]{1,0:T(8,128)}, f32[24,3072]{1,0:T(8,128)}, /*index=5*/f32[96,768]{1,0:T(8,128)}, f32[16,128]{1,0:T(8,128)}) custom-call(bf16[4,2,2,2,24,768]{5,4,3,2,1,0:T(8,128)(2,1)} %bitcast.70, bf16[4,2,2,2,24,768]{5,4,3,2,1,0:T(8,128)(2,1)} %bitcast.71, ...), custom_call_target="tpu_custom_call" | custom-call | tf_op jit(solution)/shard_map/scatter/pallas_call | solution.py:604
  345.2 1.5 slice_bitcast_fusion
  346.7 1.2 slice_bitcast_fusion.1
  347.9 2.1 slice.55
  350.0 2.0 reshape.136
  352.0 1.5 slice.54
  353.6 0.0 copy-start.5
  353.6 0.0 copy-start.4
  353.6 0.0 copy-start.3
  353.6 0.0 copy-start.2
  353.6 0.0 copy-start.1
  353.6 0.0 copy-start
  353.6 1.5 reshape.134
  355.1 0.0 copy-done.5
  355.1 0.6 copy.55
  355.8 0.0 copy-done.4
  355.8 0.6 copy.56
  356.4 0.0 copy-done.3
  356.4 0.6 copy.57
  357.0 0.0 copy-done.2
  357.0 0.6 copy.58
  357.7 0.0 copy-done.1
  357.7 0.7 copy.59
  358.4 0.0 copy-done
  358.4 0.7 copy.60
  (4 shorter events, 0.1 us)
Async XLA Ops:
  91.7 1.3 copy-start.8
  91.7 1.3 copy-start.9
  195.7 45.3 %copy-start.6 = (f32[8,768]{1,0:T(8,128)S(1)}, f32[8,768]{1,0:T(8,128)}, u32[]{:S(2)}) copy-start(f32[8,768]{1,0:T(8,128)} %get-tuple-element.73) | copy-start | bytes 73732
  195.7 46.7 %copy-start.7 = (f32[1,3072]{1,0:T(1,128)S(1)}, f32[1,3072]{1,0:T(1,128)}, u32[]{:S(2)}) copy-start(f32[1,3072]{1,0:T(1,128)} %get-tuple-element.75) | copy-start | bytes 36868
  353.6 1.5 copy-start.5
  353.6 2.2 copy-start.4
  353.6 2.8 copy-start.3
  353.6 3.4 copy-start.2
  353.6 4.0 %copy-start.1 = (f32[24,3072]{1,0:T(8,128)S(1)}, f32[24,3072]{1,0:T(8,128)}, u32[]{:S(2)}) copy-start(f32[24,3072]{1,0:T(8,128)} %get-tuple-element.121) | copy-start | bytes 884740
  353.6 4.8 %copy-start = (f32[96,768]{1,0:T(8,128)S(1)}, f32[96,768]{1,0:T(8,128)}, u32[]{:S(2)}) copy-start(f32[96,768]{1,0:T(8,128)} %get-tuple-element.123) | copy-start | bytes 884740

commit v3 on v2

v3 whole, which is shorter than its diff:
```python
import functools
import math

import jax
import jax.numpy as jnp
from jax import lax
from jax.experimental import pallas as pl
from jax.experimental.pallas import tpu as pltpu
from jax.sharding import PartitionSpec as P

HEAD_DIM = 64
EPSILON = 1e-06
NEG_FILL = -1e30
VMEM_LIMIT = 63 * 1024 * 1024
GATHER_PACE = 2.0
SCATTER_LAG = 12.0
SCATTER_GAP = 6.0


def right_mul(left_arg, right_arg):
    return jnp.dot(left_arg, right_arg, preferred_element_type=jnp.float32)


def left_mul(left_arg, right_arg):
    return lax.dot_general(
        left_arg, right_arg, (((0,), (0,)), ((), ())), preferred_element_type=jnp.float32
    )


def back_mul(left_arg, right_arg):
    return lax.dot_general(
        left_arg, right_arg, (((1,), (1,)), ((), ())), preferred_element_type=jnp.float32
    )


MESH = pl.DeviceIdType.MESH


def grid_of(mesh):
    z_size, plane = mesh.shape["gx"], mesh.shape["gy"] // 2
    x_size = max(n for n in range(1, plane + 1) if plane % n == 0 and n * n <= plane)
    return z_size, plane // x_size, x_size


class Place:
    def __init__(self, dims):
        self.dims = dims
        g = lax.axis_index("gy")
        self.z = lax.axis_index("gx")
        self.c = lax.rem(g, 2)
        self.x = lax.rem(lax.div(g, 2), dims[2])
        self.y = lax.div(g, 2 * dims[2])

    def at(self, axis, step):
        here = (self.z, self.y, self.x)[axis]
        return lax.rem(here + step, self.dims[axis])

    def plane(self, first, step, other_step):
        a, b = self.at(first, step), self.at(3 - first, other_step)
        return (a, b) if first == 1 else (b, a)

    def device(self, axis, step):
        where = [self.z, self.y, self.x, self.c]
        if axis == 3:
            where[3] = 1 - self.c
        else:
            where[axis] = self.at(axis, step)
        return (where[0], (where[1] * self.dims[2] + where[2]) * 2 + where[3])

    def barrier(self):
        sem = pltpu.get_barrier_semaphore()
        peers = [(axis, step) for axis in range(3) for step in range(1, self.dims[axis])] + [(3, 1)]
        for axis, step in peers:
            pl.semaphore_signal(sem, inc=1, device_id=self.device(axis, step), device_id_type=MESH)
        pl.semaphore_wait(sem, len(peers))


class Lanes:
    def __init__(self, place, local, send, recv):
        self.place, self.local_sem, self.send, self.recv = place, local, send, recv
        self.used = self.local_used = 0

    def remote(self, src, dst, axis, step):
        n = self.used
        self.used += 1
        return pltpu.make_async_remote_copy(
            src_ref=src, dst_ref=dst, send_sem=self.send.at[n], recv_sem=self.recv.at[n],
            device_id=self.place.device(axis, step), device_id_type=MESH,
        )

    def local(self, src, dst):
        n = self.local_used
        self.local_used += 1
        return pltpu.make_async_copy(src, dst, self.local_sem.at[n])


def gather_copies(dims, z_last):
    z, y, x = dims
    if z_last:
        return (x * y - 1) + (z - 1) + z
    return (z - 1) + (x * y - 1) + x * y


class Gather:
    def __init__(self, lanes, shard, buf, first, z_last):
        p, dims = lanes.place, lanes.place.dims
        firsts, seconds = range(1, dims[first]), range(1, dims[3 - first])
        own = buf.at[p.z, p.y, p.x, p.c]
        local = lanes.local(shard, own)
        remote = lanes.remote

        def cell(step, other):
            y, x = p.plane(first, step, other)
            return buf.at[p.z, y, x, p.c] if z_last else buf.at[:, y, x, p.c]

        def layer(step):
            return buf.at[p.at(0, step), :, :, p.c]

        mine = shard if z_last else cell(0, 0)
        to_first = [remote(mine, cell(0, 0), first, s) for s in firsts]
        to_second = [remote(mine, cell(0, 0), 3 - first, t) for t in seconds]
        onward = [remote(cell(s, 0), cell(s, 0), 3 - first, t) for s in firsts for t in seconds]
        if z_last:
            along_z = [remote(layer(0), layer(0), 0, s) for s in range(1, dims[0])]
            cores = [remote(layer(s), layer(s), 3, 1) for s in range(dims[0])]
            self.stages = [
                ([], [], to_first + to_second + [local]),
                ([], to_first, onward),
                ([local], to_second + onward, along_z + cores[:1]),
                ([], along_z, cores[1:]),
            ]
        else:
            along_z = [remote(shard, own, 0, s) for s in range(1, dims[0])]
            core = {(s, t): remote(cell(s, t), cell(s, t), 3, 1) for s in range(dims[first]) for t in range(dims[3 - first])}
            cores = list(core.values())
            self.stages = [
                ([], [], along_z + [local]),
                ([local], along_z, to_first + to_second + [core[0, 0]]),
                ([], to_first, onward + [core[s, 0] for s in firsts]),
                ([], to_second + onward, [core[s, t] for s in range(dims[first]) for t in seconds]),
            ]
        self.handed = cores
        self.remotes = to_first + to_second + onward + along_z + cores

    def run(self, stage):
        done, arrived, starts = self.stages[stage]
        for copy in done:
            copy.wait()
        for copy in arrived:
            copy.wait_recv()
        for copy in starts:
            copy.start()

    def finish(self):
        for copy in self.handed:
            copy.wait_recv()
        for copy in self.remotes:
            copy.wait_send()


def scatter_copies(dims):
    z, y, x = dims
    return 1 + (z - 1) + (x * y - 1)


def scatter_copies(dims):
    z, y, x = dims
    return 1 + (z - 1) + (x * y - 1)


def pieces_of(shapes, narrow):
    pieces = []
    for n, shape in enumerate(shapes):
        parts = max(1, shape[-1] // 768)
        if parts == 1 and shape[-2] > narrow and shape[-1] == 768:
            parts = 3
        for k in range(parts):
            size = shape[-1] // parts
            pieces.append((n, k * size, size, 1 + len(pieces) % 2))
    return pieces


def waves(count, stages):
    return [[(b + 1 - s, s) for s in range(1, stages) if 0 <= b + 1 - s < count] for b in range(count + stages - 2)]


def gather_jobs(lanes, pieces, shards, bufs):
    return [
        Gather(lanes, shards[n].at[:, pl.ds(at, size)], bufs[n].at[:, :, :, :, :, pl.ds(at, size)], first, False)
        for n, at, size, first in pieces
    ]


def comm_semaphores(pieces, copies):
    return [
        pltpu.SemaphoreType.DMA((len(pieces),)),
        pltpu.SemaphoreType.DMA((copies * len(pieces),)),
        pltpu.SemaphoreType.DMA((copies * len(pieces),)),
    ]


def run_wave(jobs, wave):
    for n, stage in wave:
        jobs[n].run(stage)


def gather_kernel(dims, pieces, count, *refs):
    shards, bufs, sems = refs[:count], refs[count : 2 * count], refs[2 * count :]
    place = Place(dims)
    jobs = gather_jobs(Lanes(place, *sems), pieces, shards, bufs)
    place.barrier()
    for job in jobs:
        job.run(0)
    for wave in waves(len(jobs), 4):
        run_wave(jobs, wave)
    for job in jobs:
        job.finish()


def gather_all(dims, arrays):
    count = len(arrays)
    pieces = pieces_of([a.shape for a in arrays], arrays[0].shape[0])
    return pl.pallas_call(
        functools.partial(gather_kernel, dims, pieces, count),
        out_shape=[jax.ShapeDtypeStruct(dims + (2,) + a.shape, a.dtype) for a in arrays],
        in_specs=[pl.BlockSpec(memory_space=pltpu.VMEM)] * count,
        out_specs=[pl.BlockSpec(memory_space=pl.ANY)] * count,
        scratch_shapes=comm_semaphores(pieces, gather_copies(dims, False)),
        compiler_params=pltpu.CompilerParams(collective_id=0, has_side_effects=True, vmem_limit_bytes=VMEM_LIMIT),
        name="gather",
    )(*arrays)


def layer_norm_parts(values):
    center = values - jnp.mean(values, axis=-1, keepdims=True)
    scale = lax.rsqrt(jnp.mean(center * center, axis=-1, keepdims=True) + EPSILON)
    return center * scale, scale


def layer_norm_back(grad, xhat, scale, gain):
    scaled = grad * gain
    inner = scaled - jnp.mean(scaled, axis=-1, keepdims=True)
    back = scale * (inner - xhat * jnp.mean(scaled * xhat, axis=-1, keepdims=True))
    return back, jnp.sum(grad * xhat, axis=0, keepdims=True), jnp.sum(grad, axis=0, keepdims=True)


def gelu_and_slope(v):
    size = jnp.abs(v)
    t = 1.0 / (1.0 + (0.3275911 * math.sqrt(0.5)) * size)
    bell = jnp.exp(-0.5 * v * v)
    poly = ((((0.5 * 1.061405429) * t - 0.5 * 1.453152027) * t + 0.5 * 1.421413741) * t - 0.5 * 0.284496736) * t
    tail = (poly + 0.5 * 0.254829592) * t * bell
    share = jnp.where(v >= 0, 1.0 - tail, tail)
    return v * share, share + (v * (1.0 / math.sqrt(2.0 * math.pi))) * bell


def ffn_kernel(
    a_rows, b_rows, ff_tile, c_rows,
    tokens, context, out_grad, o_weight, up_weight, down_weight, vectors, up_bias,
    block_out, grad_res, grad_context, grad_wo, active, grad_hidden, normed2_t, small, grad_bup,
    normed2, grad_att,
):
    rows, width = tokens.shape
    ff = up_weight.shape[1]
    o_bias, gain, bias, down_bias = vectors[4:5, :], vectors[5:6, :], vectors[6:7, :], vectors[7:8, :]
    small[...] = jnp.zeros_like(small)

    def attended(n, carry):
        at = pl.ds(pl.multiple_of(n * a_rows, a_rows), a_rows)
        residual = tokens[at, :].astype(jnp.float32) + right_mul(context[at, :], o_weight[...]) + o_bias
        grad_res[at, :] = residual
        xhat, _ = layer_norm_parts(residual)
        normed2[at, :] = (xhat * gain + bias).astype(jnp.bfloat16)
        return carry

    lax.fori_loop(0, rows // a_rows, attended, 0)

    def hidden_tile(n, carry):
        cols = pl.ds(pl.multiple_of(n * ff_tile, ff_tile), ff_tile)
        sums = jnp.zeros((1, ff_tile), jnp.float32)

        def piece(m, sums):
            at = pl.ds(pl.multiple_of(m * b_rows, b_rows), b_rows)
            hidden = right_mul(normed2[at, :], up_weight[:, cols]) + up_bias[:, cols]
            grad_active = back_mul(out_grad[at, :], down_weight[cols, :])
            value, slope = gelu_and_slope(hidden)
            active[at, cols] = value.astype(jnp.bfloat16)
            back = (slope * grad_active).astype(jnp.bfloat16)
            grad_hidden[at, cols] = back
            return sums + jnp.sum(back.astype(jnp.float32), axis=0, keepdims=True)

        grad_bup[:, cols] = lax.fori_loop(0, rows // b_rows, piece, sums)
        return carry

    lax.fori_loop(0, ff // ff_tile, hidden_tile, 0)

    def finish(n, carry):
        at = pl.ds(pl.multiple_of(n * c_rows, c_rows), c_rows)
        residual = grad_res[at, :]
        cotangent = out_grad[at, :].astype(jnp.float32)
        block_out[at, :] = (residual + right_mul(active[at, :], down_weight[...]) + down_bias).astype(jnp.bfloat16)
        grad = back_mul(grad_hidden[at, :], up_weight[...])
        xhat, scale = layer_norm_parts(residual)
        back, gain_sum, bias_sum = layer_norm_back(grad, xhat, scale, gain)
        total = cotangent + back
        grad_res[at, :] = total
        low = total.astype(jnp.bfloat16)
        grad_att[at, :] = low
        grad_context[at, :] = back_mul(low, o_weight[...]).astype(jnp.bfloat16)
        small[4:5, :] += jnp.sum(low.astype(jnp.float32), axis=0, keepdims=True)
        small[5:6, :] += gain_sum
        small[6:7, :] += bias_sum
        small[7:8, :] += jnp.sum(cotangent, axis=0, keepdims=True)
        return carry

    lax.fori_loop(0, rows // c_rows, finish, 0)

    normed2_t[...] = normed2[...].T
    grad_wo[...] = left_mul(context[...], grad_att[...]).astype(jnp.bfloat16)


def ffn(tokens, context, out_grad, o_weight, up_weight, down_weight, vectors, up_bias):
    rows, width = tokens.shape
    ff = up_weight.shape[1]
    low = functools.partial(jax.ShapeDtypeStruct, dtype=jnp.bfloat16)
    full = functools.partial(jax.ShapeDtypeStruct, dtype=jnp.float32)
    vmem = pl.BlockSpec(memory_space=pltpu.VMEM)
    return pl.pallas_call(
        functools.partial(ffn_kernel, rows, rows, 1024, rows // 2),
        out_shape=[
            low((rows, width)), full((rows, width)), low((rows, width)),
            low((width, width)), low((rows, ff)), low((rows, ff)), low((width, rows)), full((8, width)), full((1, ff)),
        ],
        in_specs=[vmem] * 8,
        out_specs=[vmem] * 9,
        scratch_shapes=[pltpu.VMEM((rows, width), jnp.bfloat16)] * 2,
        compiler_params=pltpu.CompilerParams(vmem_limit_bytes=VMEM_LIMIT),
        name="ffn",
    )(tokens, context, out_grad, o_weight, up_weight, down_weight, vectors, up_bias)


def head_lanes(pair, head):
    lane = lax.broadcasted_iota(jnp.int32, pair.shape, 1)
    return jnp.where(lax.div(lane, HEAD_DIM) == head, pair, jnp.zeros_like(pair))


def attend_kernel(dims, pieces, count, pace, strips, tokens, q_weight, k_weight, v_weight, vectors, mask, *refs):
    shards, refs = refs[:count], refs[count:]
    (turned, queries, keys, values, probs, context), bufs, scratch = refs[:6], refs[6 : 6 + count], refs[6 + count :]
    normed, *sems = scratch
    rows, width = tokens.shape
    slots, pairs = rows // strips, width // 128
    step = pl.program_id(0)
    due, late, jobs = {}, [], []
    if count:
        place = Place(dims)
        jobs = gather_jobs(Lanes(place, *sems), pieces, shards, bufs)
        late = waves(len(jobs), 4)
        for k, wave in enumerate(list(late)):
            when = 1 + int(pace * k)
            if when < strips * pairs:
                due[when] = wave
                late = late[1:]

    @pl.when(step == 0)
    def _():
        if count:
            place.barrier()
        for job in jobs:
            job.run(0)
        xhat, _ = layer_norm_parts(tokens[...].astype(jnp.float32))
        normed[...] = (xhat * vectors[0:1, :] + vectors[1:2, :]).astype(jnp.bfloat16)
        turned[...] = normed[...].T
        scale = 1.0 / math.sqrt(HEAD_DIM)
        low = (right_mul(normed[...], q_weight[...]) + vectors[2:3, :]).astype(jnp.bfloat16)
        queries[...] = low * jnp.bfloat16(scale)
        keys[...] = right_mul(normed[...], k_weight[...]).astype(jnp.bfloat16)
        values[...] = (right_mul(normed[...], v_weight[...]) + vectors[3:4, :]).astype(jnp.bfloat16)

    for when, wave in due.items():
        pl.when(step == when)(functools.partial(run_wave, jobs, wave))

    at = pl.ds(pl.multiple_of(lax.div(step, pairs) * slots, slots), slots)
    cols = pl.ds(pl.multiple_of(lax.rem(step, pairs) * 128, 128), 128)
    query, key, value = queries[at, cols], keys[at, cols], values[at, cols]
    hidden = mask[at, 0:1]
    total = jnp.zeros((slots, 128), jnp.float32)
    for head in range(2):
        scores = back_mul(key, head_lanes(query, head)) + hidden
        powers = jnp.exp(scores - jnp.max(scores, axis=0, keepdims=True))
        low = (powers * (1.0 / jnp.sum(powers, axis=0, keepdims=True))).astype(jnp.bfloat16)
        probs[0, head] = low
        total = total + left_mul(low, head_lanes(value, head))
    context[at, cols] = total.astype(jnp.bfloat16)

    @pl.when(step == strips * pairs - 1)
    def _():
        for wave in late:
            run_wave(jobs, wave)
        for job in jobs:
            job.finish()


def attend(dims, shards, strips, tokens, q_weight, k_weight, v_weight, vectors, mask):
    rows, width = tokens.shape
    slots, pairs = rows // strips, width // 128
    low = functools.partial(jax.ShapeDtypeStruct, dtype=jnp.bfloat16)
    vmem = pl.BlockSpec(memory_space=pltpu.VMEM)
    pieces = pieces_of([s.shape for s in shards], shards[0].shape[0]) if shards else []
    exchange = dict(collective_id=2, has_side_effects=True) if shards else {}
    return pl.pallas_call(
        functools.partial(attend_kernel, dims, pieces, len(shards), GATHER_PACE, strips),
        grid=(strips * pairs,),
        out_shape=[low((width, rows))]
        + [low((rows, width))] * 3
        + [low((strips * pairs, 2, slots, slots)), low((rows, width))]
        + [low(dims + (2,) + s.shape) for s in shards],
        in_specs=[vmem] * (6 + len(shards)),
        out_specs=[vmem] * 4
        + [pl.BlockSpec((1, 2, slots, slots), lambda n: (n, 0, 0, 0)), vmem]
        + [pl.BlockSpec(memory_space=pl.ANY)] * len(shards),
        scratch_shapes=[pltpu.VMEM((rows, width), jnp.bfloat16)]
        + (comm_semaphores(pieces, gather_copies(dims, False)) if shards else []),
        compiler_params=pltpu.CompilerParams(vmem_limit_bytes=VMEM_LIMIT, **exchange),
        name="attend",
    )(tokens, q_weight, k_weight, v_weight, vectors, mask, *shards)


def attend_back_kernel(
    strips, tokens, turned, queries, keys, values, probs, grad_context, grad_res, q_weight, k_weight, v_weight, vectors,
    grad_tokens, grad_wq, grad_wk, grad_wv, small,
    grad_q, grad_k, grad_v,
):
    rows, width = tokens.shape
    slots, pairs = rows // strips, width // 128
    step = pl.program_id(0)
    at = pl.ds(pl.multiple_of(lax.div(step, pairs) * slots, slots), slots)
    cols = pl.ds(pl.multiple_of(lax.rem(step, pairs) * 128, 128), 128)
    query, key, value, grad = queries[at, cols], keys[at, cols], values[at, cols], grad_context[at, cols]
    back_q = back_k = back_v = jnp.zeros((slots, 128), jnp.float32)
    for head in range(2):
        low = probs[0, head]
        own = head_lanes(grad, head)
        back_v = back_v + right_mul(low, own)
        wide = low.astype(jnp.float32)
        slope = back_mul(value, own)
        inner = jnp.sum(wide * slope, axis=0, keepdims=True)
        pull = (wide * (slope - inner)).astype(jnp.bfloat16)
        back_q = back_q + left_mul(pull, head_lanes(key, head))
        back_k = back_k + right_mul(pull, head_lanes(query, head))
    grad_q[at, cols] = (back_q * (1.0 / math.sqrt(HEAD_DIM))).astype(jnp.bfloat16)
    grad_k[at, cols] = back_k.astype(jnp.bfloat16)
    grad_v[at, cols] = back_v.astype(jnp.bfloat16)

    @pl.when(step == strips * pairs - 1)
    def _():
        grad_wq[...] = right_mul(turned[...], grad_q[...]).astype(jnp.bfloat16)
        grad_wk[...] = right_mul(turned[...], grad_k[...]).astype(jnp.bfloat16)
        grad_wv[...] = right_mul(turned[...], grad_v[...]).astype(jnp.bfloat16)
        small[...] = jnp.zeros_like(small)
        small[2:3, :] = jnp.sum(grad_q[...].astype(jnp.float32), axis=0, keepdims=True)
        small[3:4, :] = jnp.sum(grad_v[...].astype(jnp.float32), axis=0, keepdims=True)

        def finish(n, carry):
            at = pl.ds(pl.multiple_of(n * slots, slots), slots)
            grad = back_mul(grad_q[at, :], q_weight[...]) + back_mul(grad_k[at, :], k_weight[...])
            grad = grad + back_mul(grad_v[at, :], v_weight[...])
            xhat, scale = layer_norm_parts(tokens[at, :].astype(jnp.float32))
            back, gain_sum, bias_sum = layer_norm_back(grad, xhat, scale, vectors[0:1, :])
            grad_tokens[at, :] = grad_res[at, :] + back
            small[0:1, :] += gain_sum
            small[1:2, :] += bias_sum
            return carry

        lax.fori_loop(0, strips, finish, 0)


def attend_back(strips, tokens, turned, queries, keys, values, probs, grad_context, grad_res, q_weight, k_weight, v_weight, vectors):
    rows, width = tokens.shape
    slots, pairs = rows // strips, width // 128
    low = functools.partial(jax.ShapeDtypeStruct, dtype=jnp.bfloat16)
    full = functools.partial(jax.ShapeDtypeStruct, dtype=jnp.float32)
    vmem = pl.BlockSpec(memory_space=pltpu.VMEM)
    block = pl.BlockSpec((1, 2, slots, slots), lambda n: (n, 0, 0, 0))
    return pl.pallas_call(
        functools.partial(attend_back_kernel, strips),
        grid=(strips * pairs,),
        out_shape=[full((rows, width)), low((width, width)), low((width, width)), low((width, width)), full((8, width))],
        in_specs=[vmem] * 5 + [block] + [vmem] * 6,
        out_specs=[vmem] * 5,
        scratch_shapes=[pltpu.VMEM((rows, width), jnp.bfloat16)] * 3,
        compiler_params=pltpu.CompilerParams(vmem_limit_bytes=VMEM_LIMIT),
        name="attend_back",
    )(tokens, turned, queries, keys, values, probs, grad_context, grad_res, q_weight, k_weight, v_weight, vectors)


class Reduce:
    def __init__(self, lanes, whole, bufs, first, write):
        p, dims = lanes.place, lanes.place.dims
        self.p, self.dims, self.first, self.write = p, dims, first, write
        self.firsts, self.seconds = range(1, dims[first]), range(1, dims[3 - first])
        self.from_core, self.from_far, self.from_first, self.from_second, self.from_z = bufs
        self.mine, remote = whole.at[:, :, :, p.c], lanes.remote

        def cell(step, other):
            y, x = p.plane(first, step, other)
            return whole.at[:, y, x, p.c]

        core = [remote(whole.at[:, :, :, 1 - p.c], self.from_core, 3, 1)]
        self.far = [remote(cell(s, t), self.from_far.at[s - 1, t - 1], first, s) for s in self.firsts for t in self.seconds]
        self.to_first = [remote(cell(s, 0), self.from_first.at[s - 1], first, s) for s in self.firsts]
        self.to_second = [remote(cell(0, t), self.from_second.at[t - 1], 3 - first, t) for t in self.seconds]
        along_z = [
            remote(whole.at[p.at(0, s), p.y, p.x, p.c], self.from_z.at[s - 1], 0, s) for s in range(1, dims[0])
        ]
        self.ships = [core, self.far + self.to_first, self.to_second, along_z]

    def total(self, at, terms):
        total = self.mine[at].astype(jnp.float32)
        for ref, index in terms:
            total = total + ref[index].astype(jnp.float32)
        return total

    def add(self, at, terms):
        self.mine[at] = self.total(at, terms).astype(self.mine.dtype)

    def run(self, stage):
        p, (z_size, y_size, x_size) = self.p, self.dims
        arrivals = (self.ships[0], self.far, self.to_first + self.to_second, self.ships[3])[stage - 1]
        for copy in arrivals:
            copy.wait_recv()
        if stage == 1:
            def body(n, carry):
                at = (lax.div(n, y_size * x_size), lax.rem(lax.div(n, x_size), y_size), lax.rem(n, x_size))
                self.add(at, [(self.from_core, at)])
                return carry

            lax.fori_loop(0, z_size * y_size * x_size, body, 0)
        elif stage == 2:
            for z in range(z_size):
                for t in self.seconds:
                    self.add((z,) + p.plane(self.first, 0, t), [(self.from_far, (s - 1, t - 1, z)) for s in self.firsts])
        elif stage == 3:
            for z in range(z_size):
                terms = [(self.from_first, (s - 1, z)) for s in self.firsts]
                self.add((z, p.y, p.x), terms + [(self.from_second, (t - 1, z)) for t in self.seconds])
        else:
            self.write(self.total((p.z, p.y, p.x), [(self.from_z, (s,)) for s in range(z_size - 1)]))

    def ship(self, stage):
        if stage < 4:
            for copy in self.ships[stage]:
                copy.start()

    def finish(self):
        for copies in self.ships:
            for copy in copies:
                copy.wait_send()


def reduce_scratch(dims, shape, dtype, first):
    z, y, x = dims
    f, s = max(dims[first] - 1, 1), max(dims[3 - first] - 1, 1)
    leads = [(z, y, x), (f, s, z), (f, z), (s, z), (max(z - 1, 1),)]
    return [pltpu.VMEM(lead + shape, dtype) for lead in leads]


def add_wave(jobs, wave):
    left = None
    for n, stage in wave:
        if stage:
            jobs[n].run(stage)
        if left:
            jobs[left[0]].ship(left[1])
        left = (n, stage)
    return left


FF_TILE = 384
FINISH = 4
PAIRS_PER_PIECE = 2


class Plan:
    def __init__(self, dims, strips, rows, width, ff, lag, gap):
        self.tiles, self.pairs = ff // FF_TILE, width // 128
        self.down = self.tiles
        self.attention = 2 * self.tiles
        self.finish = self.attention + strips * self.pairs
        self.steps = self.finish + FINISH
        n = 2 * dims[0] * dims[1] * dims[2]
        model, wide = width // n, ff // n
        per_up = width // FF_TILE
        lasts = [0] + [per_up * (k + 1) for k in range(ff // width)] + [self.attention] * 3
        groups = self.pairs // PAIRS_PER_PIECE
        lasts += [self.attention + strips * PAIRS_PER_PIECE * (g + 1) for g in range(groups)]
        self.wholes = [(model, width)] * (1 + ff // width) + [(wide, width)]
        self.wholes += [(3 * model, width // groups)] * groups
        self.shapes = [(model, width)] * (1 + ff // width) + [(wide, width // 3)] * 3 + [(3 * model, width // groups)] * groups
        ends = [1.4] * self.attention + [3.2] * (strips * self.pairs) + [1.6] * FINISH
        starts = [sum(ends[:k]) for k in range(self.steps)]
        events, free = [], 0.0
        for piece, step in enumerate(lasts):
            begin = max(starts[step], free)
            free = begin + gap
            events += [(starts[step], 0, piece, step)]
            events += [(begin + 2.0 + lag * (k - 1), k, piece, 0) for k in range(1, 5)]
        self.waves, self.late = {}, []
        for when, stage, piece, step in sorted(events):
            fits = [k for k in range(self.steps) if starts[k] >= when and k >= step]
            if fits:
                self.waves.setdefault(fits[0], []).append((piece, stage))
            else:
                self.late.append((piece, stage))


def backward_kernel(dims, plan, strips, *refs):
    (turned, turned_two, out_grad, q_weight, k_weight, v_weight, vectors, small_in, bup_in) = refs[:9]
    (grad_hidden, active, probs, query_b, key_b, value_b, grad_b, tokens, grad_res, wo_hbm) = refs[9:19]
    (grad_tokens, sum_q, sum_k, sum_v, sum_o, sum_up, sum_down, sum_vec) = refs[19:27]
    refs = refs[27:]
    grad_q, grad_k, grad_v, small, vec_whole = refs[:5]
    wholes, refs = refs[5 : 5 + len(plan.wholes)], refs[5 + len(plan.wholes) :]
    local, send, recv = refs[-3:]
    width, rows = turned.shape
    slots, ff_pieces, groups = rows // strips, sum_up.shape[1] // width, len(plan.wholes) - 2 - sum_up.shape[1] // width
    step = pl.program_id(0)
    place = Place(dims)
    lanes = Lanes(place, local, send, recv)
    o_copy = lanes.local(wo_hbm, wholes[0])

    model = sum_q.shape[0]
    columns = width // groups

    def write_to(ref, at, size):
        def write(total):
            ref[:, pl.ds(at, size)] = total
        return write

    def write_group(g):
        def write(total):
            for n, ref in enumerate((sum_q, sum_k, sum_v)):
                ref[:, pl.ds(g * columns, columns)] = total[n * model : (n + 1) * model]
        return write

    third = width // 3
    down_whole = wholes[1 + ff_pieces]
    views = [(wholes[0], write_to(sum_o, 0, width))]
    views += [(wholes[1 + k], write_to(sum_up, k * width, width)) for k in range(ff_pieces)]
    views += [
        (down_whole.at[:, :, :, :, :, pl.ds(k * third, third)], write_to(sum_down, k * third, third)) for k in range(3)
    ]
    views += [(wholes[2 + ff_pieces + g], write_group(g)) for g in range(groups)]
    views += [(vec_whole, write_to(sum_vec, 0, sum_vec.shape[1]))]
    jobs = [Reduce(lanes, whole, refs[5 * n : 5 * n + 5], 1 + n % 2, write) for n, (whole, write) in enumerate(views)]
    last = len(jobs) - 1

    @pl.when(step == 0)
    def _():
        place.barrier()
        o_copy.start()
        small[...] = small_in[...]
        o_copy.wait()

    for when, wave in plan.waves.items():
        pl.when(step == when)(lambda wave=wave: add_wave(jobs, wave) and None)

    def rows_to_blocks(product):
        n = 2 * dims[0] * dims[1] * dims[2]
        return product.reshape(dims + (2, product.shape[0] // n, product.shape[1])).astype(jnp.bfloat16)

    for k in range(plan.tiles):
        @pl.when(step == k)
        def _():
            piece, part = divmod(k * FF_TILE, width)
            wholes[1 + piece][:, :, :, :, :, pl.ds(part, FF_TILE)] = rows_to_blocks(right_mul(turned_two[...], grad_hidden[...]))

        @pl.when(step == plan.down + k)
        def _():
            product = left_mul(active[...], out_grad[...])
            wide = down_whole.shape[4]
            for b in range(FF_TILE // wide):
                d = k * (FF_TILE // wide) + b
                at = (d // (2 * dims[1] * dims[2]), d // (2 * dims[2]) % dims[1], d // 2 % dims[2], d % 2)
                down_whole[at] = product[b * wide : (b + 1) * wide].astype(jnp.bfloat16)

    pair, strip = lax.div(step - plan.attention, strips), lax.rem(step - plan.attention, strips)
    in_attention = (step >= plan.attention) & (step < plan.finish)

    @pl.when(in_attention)
    def _():
        at = pl.ds(pl.multiple_of(strip * slots, slots), slots)
        cols = pl.ds(pl.multiple_of(pair * 128, 128), 128)
        query, key, value, grad = query_b[...], key_b[...], value_b[...], grad_b[...]
        back_q = back_k = back_v = jnp.zeros((slots, 128), jnp.float32)
        for head in range(2):
            low = probs[0, head]
            own = head_lanes(grad, head)
            back_v = back_v + right_mul(low, own)
            wide = low.astype(jnp.float32)
            slope = back_mul(value, own)
            inner = jnp.sum(wide * slope, axis=0, keepdims=True)
            pull = (wide * (slope - inner)).astype(jnp.bfloat16)
            back_q = back_q + left_mul(pull, head_lanes(key, head))
            back_k = back_k + right_mul(pull, head_lanes(query, head))
        grad_q[at, cols] = (back_q * (1.0 / math.sqrt(HEAD_DIM))).astype(jnp.bfloat16)
        grad_k[at, cols] = back_k.astype(jnp.bfloat16)
        grad_v[at, cols] = back_v.astype(jnp.bfloat16)

    for g in range(groups):
        @pl.when(step == plan.attention + strips * PAIRS_PER_PIECE * (g + 1) - 1)
        def _():
            whole = wholes[2 + ff_pieces + g]
            for n, grad in enumerate((grad_q, grad_k, grad_v)):
                part = grad[:, pl.ds(g * columns, columns)]
                whole[:, :, :, :, pl.ds(n * model, model), :] = rows_to_blocks(right_mul(turned[...], part))
                if n != 1:
                    small[2 + n // 2 : 3 + n // 2, pl.ds(g * columns, columns)] = jnp.sum(
                        part.astype(jnp.float32), axis=0, keepdims=True
                    )

    @pl.when(step >= plan.finish)
    def _():
        size = rows // FINISH
        at = pl.ds(pl.multiple_of((step - plan.finish) * size, size), size)
        grad = back_mul(grad_q[at, :], q_weight[...]) + back_mul(grad_k[at, :], k_weight[...])
        grad = grad + back_mul(grad_v[at, :], v_weight[...])
        xhat, scale = layer_norm_parts(tokens[...].astype(jnp.float32))
        back, gain_sum, bias_sum = layer_norm_back(grad, xhat, scale, vectors[0:1, :])
        grad_tokens[...] = grad_res[...] + back
        small[0:1, :] += gain_sum
        small[1:2, :] += bias_sum

    for when, wave in plan.waves.items():
        n, stage = wave[-1]
        pl.when(step == when)(functools.partial(jobs[n].ship, stage))

    @pl.when(step == plan.steps - 1)
    def _():
        vec_whole[...] = jnp.zeros_like(vec_whole)
        wide = bup_in.shape[1] // (width // model)
        for d in range(width // model):
            at = (d // (2 * dims[1] * dims[2]), d // (2 * dims[2]) % dims[1], d // 2 % dims[2], d % 2)
            vec_whole[at + (pl.ds(0, 8), pl.ds(0, model))] = small[:, d * model : (d + 1) * model]
            vec_whole[at + (pl.ds(8, 1), pl.ds(0, wide))] = bup_in[:, d * wide : (d + 1) * wide]
        late = list(plan.late)
        spread = max(1, len(late) // 5)
        left = None
        for k in range(5):
            take = late[k * spread : (k + 1) * spread] if k < 4 else late[4 * spread :]
            left = add_wave(jobs, take + [(last, k)]) if k < 4 else add_wave(jobs, take[:-1] + [(last, k)] + take[-1:])
            jobs[left[0]].ship(left[1])
        for job in jobs:
            job.finish()


def backward(dims, strips, turned, turned_two, out_grad, q_weight, k_weight, v_weight, vectors, small, grad_bup,
             grad_hidden, active, probs, queries, keys, values, grad_context, tokens, grad_res, grad_wo):
    width, rows = turned.shape
    ff = grad_hidden.shape[1]
    slots = rows // strips
    plan = Plan(dims, strips, rows, width, ff, SCATTER_LAG, SCATTER_GAP)
    n = 2 * dims[0] * dims[1] * dims[2]
    model, wide = width // n, ff // n
    lanes_wide = 128 * -(-wide // 128)
    full = functools.partial(jax.ShapeDtypeStruct, dtype=jnp.float32)
    vmem = pl.BlockSpec(memory_space=pltpu.VMEM)

    def part(step, first, count):
        return jnp.clip(step - first, 0, count - 1)

    def strip_pair(step):
        k = part(step, plan.attention, strips * plan.pairs)
        return lax.rem(k, strips), lax.div(k, strips)

    def probs_at(step):
        strip, pair = strip_pair(step)
        return (strip * plan.pairs + pair, 0, 0, 0)

    qkv = pl.BlockSpec((slots, 128), strip_pair)
    ending = pl.BlockSpec((rows // FINISH, width), lambda step: (part(step, plan.finish, FINISH), 0))
    shapes = plan.shapes
    bufs = []
    for k, shape in enumerate(shapes):
        bufs += reduce_scratch(dims, shape, jnp.bfloat16, 1 + k % 2)
    bufs += reduce_scratch(dims, (16, lanes_wide), jnp.float32, 1 + len(shapes) % 2)
    copies = scatter_copies(dims) * (len(shapes) + 1)
    return pl.pallas_call(
        functools.partial(backward_kernel, dims, plan, strips),
        grid=(plan.steps,),
        out_shape=[full((rows, width))] + [full((model, width))] * 4 + [full((model, ff)), full((wide, width)), full((16, lanes_wide))],
        in_specs=[vmem] * 9
        + [
            pl.BlockSpec((rows, FF_TILE), lambda step: (0, part(step, 0, plan.tiles))),
            pl.BlockSpec((rows, FF_TILE), lambda step: (0, part(step, plan.down, plan.tiles))),
            pl.BlockSpec((1, 2, slots, slots), probs_at),
            qkv, qkv, qkv, qkv, ending, ending,
            pl.BlockSpec(memory_space=pl.ANY),
        ],
        out_specs=[ending] + [vmem] * 7,
        scratch_shapes=[pltpu.VMEM((rows, width), jnp.bfloat16)] * 3
        + [pltpu.VMEM((8, width), jnp.float32), pltpu.VMEM(dims + (2, 16, lanes_wide), jnp.float32)]
        + [pltpu.VMEM(dims + (2,) + shape, jnp.bfloat16) for shape in plan.wholes]
        + bufs
        + [pltpu.SemaphoreType.DMA((1,)), pltpu.SemaphoreType.DMA((copies,)), pltpu.SemaphoreType.DMA((copies,))],
        compiler_params=pltpu.CompilerParams(collective_id=3, has_side_effects=True, vmem_limit_bytes=VMEM_LIMIT),
        name="backward",
    )(turned, turned_two, out_grad, q_weight, k_weight, v_weight, vectors, small, grad_bup,
      grad_hidden, active, probs, queries, keys, values, grad_context, tokens, grad_res, grad_wo)


def lane_pad(rows, width):
    return jnp.pad(rows, ((0, 0), (0, width - rows.shape[1])))


def pack_vectors(vectors, wide):
    width = 128 * -(-wide.shape[0] // 128)
    rows = lane_pad(jnp.stack(vectors).astype(jnp.float32), width)
    last = lane_pad(wide[None].astype(jnp.float32), width)
    return jnp.pad(jnp.concatenate([rows, last]), ((0, 15 - len(vectors)), (0, 0)))


def unpack_vectors(block, part, wide_part):
    flat = block.reshape((-1,) + block.shape[-2:])
    rows = flat[:, :8, :part].transpose(1, 0, 2).reshape(8, -1)
    return rows, flat[:, 8, :wide_part].reshape(1, -1)


def shards(
    dims,
    tokens,
    lengths,
    key_mask,
    ln1_gain,
    ln1_bias,
    q_weight,
    q_bias,
    k_weight,
    v_weight,
    v_bias,
    o_weight,
    o_bias,
    ln2_gain,
    ln2_bias,
    up_weight,
    up_bias,
    down_weight,
    down_bias,
    out_grad,
):
    early_weights, late_weights = (q_weight, k_weight, v_weight), (o_weight, up_weight, down_weight)
    vectors = (ln1_gain, ln1_bias, q_bias, v_bias, o_bias, ln2_gain, ln2_bias, down_bias)
    fused = q_weight.shape[0] % 8 == 0
    axes = ("gx", "gy")

    def whole(shard):
        return lax.all_gather(shard, axes, axis=0, tiled=True)

    if fused:
        *wide, packed = gather_all(dims, list(early_weights) + [pack_vectors(vectors, up_bias)])
        q_full, k_full, v_full = [w.reshape((-1,) + w.shape[-1:]) for w in wide]
        rows, up_bias_full = unpack_vectors(packed, ln1_gain.shape[0], up_bias.shape[0])
    else:
        q_full, k_full, v_full = [whole(w) for w in early_weights]
        rows = jnp.stack([whole(v) for v in vectors]).astype(jnp.float32)
        up_bias_full = whole(up_bias).astype(jnp.float32)[None]

    row_count, width = tokens.shape
    strips = lengths.shape[0]
    slots = row_count // strips
    extra = -slots % 16

    def padded(values):
        return jnp.pad(values.reshape(strips, slots, width), ((0, 0), (0, extra), (0, 0))).reshape(-1, width)

    def cropped(values):
        return values.reshape(strips, slots + extra, width)[:, :slots].reshape(row_count, width)

    slot_ids = lax.iota(jnp.int32, slots)
    visible = (slot_ids[None, :] == 0) | (slot_ids[None, :] < lengths[:, None]) & (key_mask == 1)
    mask = jnp.where(jnp.pad(visible, ((0, 0), (0, extra))), 0.0, NEG_FILL).reshape(-1, 1)
    tokens_in, grads_in = padded(tokens), padded(out_grad)

    turned, queries, keys, values, probs, context, *late = attend(
        dims, late_weights if fused else (), strips, tokens_in, q_full, k_full, v_full, rows, mask
    )
    if fused:
        o_full, up_full, down_full = [w.reshape((-1,) + w.shape[-1:]) for w in late]
    else:
        o_full, up_full, down_full = [whole(w) for w in late_weights]
    block_out, grad_res, grad_context, grad_wo, active, grad_hidden, turned_two, small, grad_bup = ffn(
        tokens_in, context, grads_in, o_full, up_full, down_full, rows, up_bias_full
    )
    if fused:
        grad_tokens, sum_wq, sum_wk, sum_wv, sum_wo, sum_wup, sum_wdown, least = backward(
            dims, strips, turned, turned_two, grads_in, q_full, k_full, v_full, rows, small, grad_bup,
            grad_hidden, active, probs, queries, keys, values, grad_context, tokens_in, grad_res,
            grad_wo.reshape(dims + (2,) + o_weight.shape),
        )
        vec = [least[n, : ln1_gain.shape[0]] for n in range(8)]
        sum_bup = least[8, : up_bias.shape[0]]
    else:
        grad_tokens, grad_wq, grad_wk, grad_wv, small_two = attend_back(
            strips, tokens_in, turned, queries, keys, values, probs, grad_context, grad_res, q_full, k_full, v_full, rows
        )
        small = small + small_two
        full = [grad_wq, grad_wk, grad_wv, grad_wo, right_mul(turned_two, grad_hidden), left_mul(active, grads_in), grad_bup[0]]
        full = [g.astype(jnp.float32) for g in full] + [small[n] for n in range(8)]
        sum_wq, sum_wk, sum_wv, sum_wo, sum_wup, sum_wdown, sum_bup, *vec = [
            lax.psum_scatter(g, axes, scatter_dimension=0, tiled=True) for g in full
        ]
    return (
        cropped(block_out), cropped(grad_tokens), vec[0], vec[1], sum_wq, vec[2], sum_wk, sum_wv, vec[3], sum_wo, vec[4],
        vec[5], vec[6], sum_wup, sum_bup, sum_wdown, vec[7],
    )


def solution(mesh):
    rows, flat = P(("gx", "gy"), None), P(("gx", "gy"))
    return jax.shard_map(
        functools.partial(shards, grid_of(mesh)),
        mesh=mesh,
        in_specs=(
            rows, flat, rows, flat, flat, rows, flat, rows, rows, flat, rows, flat, flat, flat, rows, flat, rows, flat, rows,
        ),
        out_specs=(
            rows, rows, flat, flat, rows, flat, rows, rows, flat, rows, flat, flat, flat, rows, flat, rows, flat,
        ),
        check_vma=False,
    )
```

time: 363 us -> 296 us (0.82)
  Pallas kernels: 329 us -> 266 us
    pallas_call x1, Pallas kernels: 85.5 us -> 33.2 us  [gather_all(): pl.pallas_call(functools.partial(gather_kernel, dims, pieces, count), out...]
    pallas_call x4 -> x3, Pallas kernels: 243 us -> 233 us  [the longest x1 118 us: backward(): pl.pallas_call(functools.partial(backward_kernel, dims, plan, strips), gr...]
    unnamed x28 -> x17, local copies, waits for them, and re-layouts: 4.13 us -> 7.59 us
where the time goes in v3:
time: 296 us; the launch traced here: 295 us
  Pallas kernels  266 us (90%)
  local copies, waits for them, and re-layouts  25.7 us (9%)
    pallas_call x1, Pallas kernels, backward(): pl.pallas_call(functools.partial(backward_kernel, dims, plan, strips), gr...  118 us
    pallas_call x1, Pallas kernels, attend(): pl.pallas_call(functools.partial(attend_kernel, dims, pieces, len(shards)...  69.5 us
    pallas_call x1, Pallas kernels, ffn(): pl.pallas_call(functools.partial(ffn_kernel, rows, rows, 1024, rows // 2)...  45.3 us
    pallas_call x1, Pallas kernels, gather_all(): pl.pallas_call(functools.partial(gather_kernel, dims, pieces, count), out...  33.2 us
    unnamed x17, local copies, waits for them, and re-layouts  7.59 us

profile of v3, /device:TPU:0, one launch (start us, length us, event | category | flops | bytes accessed | tf_op | source)
XLA Modules:
  0.0 294.6 jit_solution(6912900309915356219)
XLA Ops:
  0.7 0.8 and_or_fusion
  1.4 0.8 stack.35
  2.2 0.7 fusion.2
  2.9 0.6 pad_convert_fusion.refs_3_
  3.5 1.2 reshape.114.mask
  4.7 1.8 reshape.96
  6.4 0.0 copy-start
  6.5 1.3 pad.27
  7.7 0.7 copy-done
  8.5 0.3 reshape.104
  8.8 1.3 pad.33
  10.1 33.2 %gather.1 = (bf16[4,2,2,2,24,768]{5,4,3,2,1,0:T(8,128)(2,1)}, bf16[4,2,2,2,24,768]{5,4,3,2,1,0:T(8,128)(2,1)}, bf16[4,2,2,2,24,768]{5,4,3,2,1,0:T(8,128)(2,1)}, f32[4,2,2,2,16,128]{5,4,3,2,1,0:T(8,128)}) custom-call(bf16[24,768]{1,0:T(8,128)(2,1)} %refs_0_.2, bf16[24,768]{1,0:T(8,128)(2,1)} %refs_1_.2, bf16[24,768]{1,0:T(8,128)(2,1)} %refs_2_.2, ...), custom_call_target="tpu_custom_call" | custom-call | tf_op jit(solution)/shard_map/gather/pallas_call | solution.py:223
  43.3 0.9 slice.53
  44.3 0.9 slice.52
  45.2 0.7 reshape.102.vectors.refs_6_
  45.9 0.7 reshape_squeeze.3.up_bias
  46.6 69.5 %attend.1 = (bf16[768,1088]{1,0:T(8,128)(2,1)}, bf16[1088,768]{1,0:T(8,128)(2,1)}, bf16[1088,768]{1,0:T(8,128)(2,1)}, bf16[1088,768]{1,0:T(8,128)(2,1)}, bf16[12...) custom-call(bf16[1088,768]{1,0:T(8,128)(2,1)} %bitcast.45, ...), custom_call_target="tpu_custom_call" | custom-call | tf_op jit(solution)/shard_map/attend/pallas_call | solution.py:411
  116.2 45.3 %ffn.1 = (bf16[1088,768]{1,0:T(8,128)(2,1)}, f32[1088,768]{1,0:T(8,128)}, bf16[1088,768]{1,0:T(8,128)(2,1)}, bf16[768,768]{1,0:T(8,128)(2,1)}, bf16[1088,3072]{1...) custom-call(bf16[1088,768]{1,0:T(8,128)(2,1)} %bitcast.46, ...), custom_call_target="tpu_custom_call" | custom-call | tf_op jit(solution)/shard_map/ffn/pallas_call | solution.py:328
  161.4 117.8 %backward.1 = (f32[1088,768]{1,0:T(8,128)}, f32[24,768]{1,0:T(8,128)}, f32[24,768]{1,0:T(8,128)}, f32[24,768]{1,0:T(8,128)}, f32[24,768]{1,0:T(8,128)}, /*index=...) custom-call(bf16[768,1088]{1,0:T(8,128)(2,1)} %get-tuple-element.56.refs_0_, ...), custom_call_target="tpu_custom_call" | custom-call | tf_op jit(solution)/shard_map/backward/pallas_call | solution.py:788
  279.3 1.5 slice.54
  280.8 1.5 reshape.110
  282.3 2.1 slice.55
  284.5 0.0 copy-start.4
  284.5 0.0 copy-start.3
  284.5 0.0 copy-start.2
  284.5 0.0 copy-start.1
  284.5 2.0 reshape.113
  286.5 0.0 copy-done.4
  286.5 0.5 slice_bitcast_fusion.1
  287.0 0.5 slice_bitcast_fusion
  287.6 1.5 copy.51
  289.1 0.0 copy-done.3
  289.1 0.6 copy.52
  289.7 0.0 copy-done.2
  289.7 0.6 copy.53
  290.4 0.0 copy-done.1
  290.4 0.6 copy.54
  291.0 1.7 copy.55
  292.7 1.7 copy.56
  (3 shorter events, 0.0 us)
Async XLA Ops:
  6.4 2.0 copy-start
  284.5 2.1 copy-start.4
  284.5 4.6 %copy-start.3 = (f32[24,768]{1,0:T(8,128)S(1)}, f32[24,768]{1,0:T(8,128)}, u32[]{:S(2)}) copy-start(f32[24,768]{1,0:T(8,128)} %get-tuple-element.108) | copy-start | bytes 221188
  284.5 5.3 %copy-start.2 = (f32[24,768]{1,0:T(8,128)S(1)}, f32[24,768]{1,0:T(8,128)}, u32[]{:S(2)}) copy-start(f32[24,768]{1,0:T(8,128)} %get-tuple-element.109) | copy-start | bytes 221188
  284.5 5.9 %copy-start.1 = (f32[24,768]{1,0:T(8,128)S(1)}, f32[24,768]{1,0:T(8,128)}, u32[]{:S(2)}) copy-start(f32[24,768]{1,0:T(8,128)} %get-tuple-element.111) | copy-start | bytes 221188

commit v4 on v3

--- a/solution.py
+++ b/solution.py
@@ -12,7 +12,8 @@
 EPSILON = 1e-06
 NEG_FILL = -1e30
 VMEM_LIMIT = 63 * 1024 * 1024
-GATHER_PACE = 2.0
+GATHER_LAG = 12.0
+GATHER_GAP = 5.0
 SCATTER_LAG = 12.0
 SCATTER_GAP = 6.0
 
@@ -151,16 +152,13 @@
         for copy in starts:
             copy.start()
 
-    def finish(self):
+    def arrive(self):
         for copy in self.handed:
             copy.wait_recv()
+
+    def finish(self):
         for copy in self.remotes:
             copy.wait_send()
-
-
-def scatter_copies(dims):
-    z, y, x = dims
-    return 1 + (z - 1) + (x * y - 1)
 
 
 def scatter_copies(dims):
@@ -202,33 +200,6 @@
 def run_wave(jobs, wave):
     for n, stage in wave:
         jobs[n].run(stage)
-
-
-def gather_kernel(dims, pieces, count, *refs):
-    shards, bufs, sems = refs[:count], refs[count : 2 * count], refs[2 * count :]
-    place = Place(dims)
-    jobs = gather_jobs(Lanes(place, *sems), pieces, shards, bufs)
-    place.barrier()
-    for job in jobs:
-        job.run(0)
-    for wave in waves(len(jobs), 4):
-        run_wave(jobs, wave)
-    for job in jobs:
-        job.finish()
-
-
-def gather_all(dims, arrays):
-    count = len(arrays)
-    pieces = pieces_of([a.shape for a in arrays], arrays[0].shape[0])
-    return pl.pallas_call(
-        functools.partial(gather_kernel, dims, pieces, count),
-        out_shape=[jax.ShapeDtypeStruct(dims + (2,) + a.shape, a.dtype) for a in arrays],
-        in_specs=[pl.BlockSpec(memory_space=pltpu.VMEM)] * count,
-        out_specs=[pl.BlockSpec(memory_space=pl.ANY)] * count,
-        scratch_shapes=comm_semaphores(pieces, gather_copies(dims, False)),
-        compiler_params=pltpu.CompilerParams(collective_id=0, has_side_effects=True, vmem_limit_bytes=VMEM_LIMIT),
-        name="gather",
-    )(*arrays)
 
 
 def layer_norm_parts(values):
@@ -344,42 +315,9 @@
     return jnp.where(lax.div(lane, HEAD_DIM) == head, pair, jnp.zeros_like(pair))
 
 
-def attend_kernel(dims, pieces, count, pace, strips, tokens, q_weight, k_weight, v_weight, vectors, mask, *refs):
-    shards, refs = refs[:count], refs[count:]
-    (turned, queries, keys, values, probs, context), bufs, scratch = refs[:6], refs[6 : 6 + count], refs[6 + count :]
-    normed, *sems = scratch
-    rows, width = tokens.shape
+def attend_pair(strips, step, mask, queries, keys, values, probs, context):
+    rows, width = queries.shape
     slots, pairs = rows // strips, width // 128
-    step = pl.program_id(0)
-    due, late, jobs = {}, [], []
-    if count:
-        place = Place(dims)
-        jobs = gather_jobs(Lanes(place, *sems), pieces, shards, bufs)
-        late = waves(len(jobs), 4)
-        for k, wave in enumerate(list(late)):
-            when = 1 + int(pace * k)
-            if when < strips * pairs:
-                due[when] = wave
-                late = late[1:]
-
-    @pl.when(step == 0)
-    def _():
-        if count:
-            place.barrier()
-        for job in jobs:
-            job.run(0)
-        xhat, _ = layer_norm_parts(tokens[...].astype(jnp.float32))
-        normed[...] = (xhat * vectors[0:1, :] + vectors[1:2, :]).astype(jnp.bfloat16)
-        turned[...] = normed[...].T
-        scale = 1.0 / math.sqrt(HEAD_DIM)
-        low = (right_mul(normed[...], q_weight[...]) + vectors[2:3, :]).astype(jnp.bfloat16)
-        queries[...] = low * jnp.bfloat16(scale)
-        keys[...] = right_mul(normed[...], k_weight[...]).astype(jnp.bfloat16)
-        values[...] = (right_mul(normed[...], v_weight[...]) + vectors[3:4, :]).astype(jnp.bfloat16)
-
-    for when, wave in due.items():
-        pl.when(step == when)(functools.partial(run_wave, jobs, wave))
-
     at = pl.ds(pl.multiple_of(lax.div(step, pairs) * slots, slots), slots)
     cols = pl.ds(pl.multiple_of(lax.rem(step, pairs) * 128, 128), 128)
     query, key, value = queries[at, cols], keys[at, cols], values[at, cols]
@@ -393,37 +331,41 @@
         total = total + left_mul(low, head_lanes(value, head))
     context[at, cols] = total.astype(jnp.bfloat16)
 
-    @pl.when(step == strips * pairs - 1)
+
+def attend_kernel(strips, tokens, q_weight, k_weight, v_weight, vectors, mask, turned, queries, keys, values, probs, context, normed):
+    rows, width = tokens.shape
+    slots, pairs = rows // strips, width // 128
+    step = pl.program_id(0)
+
+    @pl.when(step == 0)
     def _():
-        for wave in late:
-            run_wave(jobs, wave)
-        for job in jobs:
-            job.finish()
-
-
-def attend(dims, shards, strips, tokens, q_weight, k_weight, v_weight, vectors, mask):
+        xhat, _ = layer_norm_parts(tokens[...].astype(jnp.float32))
+        normed[...] = (xhat * vectors[0:1, :] + vectors[1:2, :]).astype(jnp.bfloat16)
+        turned[...] = normed[...].T
+        scale = 1.0 / math.sqrt(HEAD_DIM)
+        low = (right_mul(normed[...], q_weight[...]) + vectors[2:3, :]).astype(jnp.bfloat16)
+        queries[...] = low * jnp.bfloat16(scale)
+        keys[...] = right_mul(normed[...], k_weight[...]).astype(jnp.bfloat16)
+        values[...] = (right_mul(normed[...], v_weight[...]) + vectors[3:4, :]).astype(jnp.bfloat16)
+
+    attend_pair(strips, step, mask, queries, keys, values, probs, context)
+
+
+def attend(strips, tokens, q_weight, k_weight, v_weight, vectors, mask):
     rows, width = tokens.shape
     slots, pairs = rows // strips, width // 128
     low = functools.partial(jax.ShapeDtypeStruct, dtype=jnp.bfloat16)
-    vmem = pl.BlockSpec(memory_space=pltpu.VMEM)
-    pieces = pieces_of([s.shape for s in shards], shards[0].shape[0]) if shards else []
-    exchange = dict(collective_id=2, has_side_effects=True) if shards else {}
     return pl.pallas_call(
-        functools.partial(attend_kernel, dims, pieces, len(shards), GATHER_PACE, strips),
+        functools.partial(attend_kernel, strips),
         grid=(strips * pairs,),
-        out_shape=[low((width, rows))]
-        + [low((rows, width))] * 3
-        + [low((strips * pairs, 2, slots, slots)), low((rows, width))]
-        + [low(dims + (2,) + s.shape) for s in shards],
-        in_specs=[vmem] * (6 + len(shards)),
-        out_specs=[vmem] * 4
-        + [pl.BlockSpec((1, 2, slots, slots), lambda n: (n, 0, 0, 0)), vmem]
-        + [pl.BlockSpec(memory_space=pl.ANY)] * len(shards),
-        scratch_shapes=[pltpu.VMEM((rows, width), jnp.bfloat16)]
-        + (comm_semaphores(pieces, gather_copies(dims, False)) if shards else []),
-        compiler_params=pltpu.CompilerParams(vmem_limit_bytes=VMEM_LIMIT, **exchange),
+        out_shape=[low((width, rows))] + [low((rows, width))] * 3 + [low((strips * pairs, 2, slots, slots)), low((rows, width))],
+        in_specs=[pl.BlockSpec(memory_space=pltpu.VMEM)] * 6,
+        out_specs=[pl.BlockSpec(memory_space=pltpu.VMEM)] * 4
+        + [pl.BlockSpec((1, 2, slots, slots), lambda n: (n, 0, 0, 0)), pl.BlockSpec(memory_space=pltpu.VMEM)],
+        scratch_shapes=[pltpu.VMEM((rows, width), jnp.bfloat16)],
+        compiler_params=pltpu.CompilerParams(vmem_limit_bytes=VMEM_LIMIT),
         name="attend",
-    )(tokens, q_weight, k_weight, v_weight, vectors, mask, *shards)
+    )(tokens, q_weight, k_weight, v_weight, vectors, mask)
 
 
 def attend_back_kernel(
@@ -494,6 +436,110 @@
     )(tokens, turned, queries, keys, values, probs, grad_context, grad_res, q_weight, k_weight, v_weight, vectors)
 
 
+def forward_plan(sizes, early, steps, lag, gap):
+    project, attend = 5.0, 2.3
+    events, start = [], 0.0
+    for n, size in enumerate(sizes):
+        start = start + gap * size
+        events += [(start + 2.0 + lag * (k - 1), k, n) for k in range(1, 4)]
+    events.sort()
+    first = max(k for k, (_, _, n) in enumerate(events) if n < early) + 1
+    begin = events[first - 1][0] + project
+    plan, late = {0: [(n, k) for _, k, n in events[:first]]}, []
+    for when, k, n in events[first:]:
+        fits = [s for s in range(1, steps) if begin + attend * (s - 1) >= when]
+        plan.setdefault(fits[0], []).append((n, k)) if fits else late.append((n, k))
+    return plan, late
+
+
+def forward_kernel(dims, pieces, early, plan, late, strips, tokens, mask, *refs):
+    count = early + 3
+    shards, refs = refs[:count], refs[count:]
+    (turned, heads, probs, context), refs = refs[:4], refs[4:]
+    queries, keys, values = heads.at[0], heads.at[1], heads.at[2]
+    weights, (vectors, up_bias), bufs, refs = refs[: early - 1], refs[early - 1 : early + 1], refs[early + 1 : early + 4], refs[early + 4 :]
+    near, normed, sems = refs[:early], refs[early], refs[early + 1 :]
+    rows, width = tokens.shape
+    slots, pairs = rows // strips, width // 128
+    step = pl.program_id(0)
+    place = Place(dims)
+    jobs = gather_jobs(Lanes(place, *sems), pieces, shards, list(near) + list(bufs))
+
+    @pl.when(step == 0)
+    def _():
+        place.barrier()
+        for job in jobs:
+            job.run(0)
+        xhat, _ = layer_norm_parts(tokens[...].astype(jnp.float32))
+        run_wave(jobs, plan[0])
+        for job in jobs[:early]:
+            job.arrive()
+        model, wide = shards[1].shape[0], up_bias.shape[1] // (width // shards[1].shape[0])
+        for d in range(width // model):
+            at = (d // (2 * dims[1] * dims[2]), d // (2 * dims[2]) % dims[1], d // 2 % dims[2], d % 2)
+            vectors[:, d * model : (d + 1) * model] = near[0][at + (pl.ds(0, 8), pl.ds(0, model))]
+            up_bias[:, d * wide : (d + 1) * wide] = near[0][at + (pl.ds(8, 1), pl.ds(0, wide))]
+        for whole, buf in zip(weights, near[1:]):
+            whole[...] = buf[...].astype(jnp.float32).reshape(width, width).astype(jnp.bfloat16)
+        q_weight, k_weight, v_weight = weights
+        normed[...] = (xhat * vectors[0:1, :] + vectors[1:2, :]).astype(jnp.bfloat16)
+        turned[...] = normed[...].T
+        scale = 1.0 / math.sqrt(HEAD_DIM)
+        low = (right_mul(normed[...], q_weight[...]) + vectors[2:3, :]).astype(jnp.bfloat16)
+        queries[...] = low * jnp.bfloat16(scale)
+        keys[...] = right_mul(normed[...], k_weight[...]).astype(jnp.bfloat16)
+        values[...] = (right_mul(normed[...], v_weight[...]) + vectors[3:4, :]).astype(jnp.bfloat16)
+
+    for when, wave in plan.items():
+        if when:
+            pl.when(step == when)(functools.partial(run_wave, jobs, wave))
+
+    attend_pair(strips, step, mask, queries, keys, values, probs, context)
+
+    @pl.when(step == strips * pairs - 1)
+    def _():
+        run_wave(jobs, late)
+        for job in jobs[early:]:
+            job.arrive()
+        for job in jobs:
+            job.finish()
+
+
+def forward(dims, strips, tokens, mask, packed, early_shards, late_shards):
+    rows, width = tokens.shape
+    slots, pairs = rows // strips, width // 128
+    shards = [packed] + list(early_shards) + list(late_shards)
+    early = 1 + len(early_shards)
+    model = early_shards[0].shape[0]
+    ff = late_shards[1].shape[1]
+    low = functools.partial(jax.ShapeDtypeStruct, dtype=jnp.bfloat16)
+    full = functools.partial(jax.ShapeDtypeStruct, dtype=jnp.float32)
+    vmem = pl.BlockSpec(memory_space=pltpu.VMEM)
+    pieces = pieces_of([s.shape for s in shards], model)
+    sizes = [shards[n].shape[0] * size * shards[n].dtype.itemsize / (model * width * 2) for n, _, size, _ in pieces]
+    plan, late = forward_plan(sizes, early, strips * pairs, GATHER_LAG, GATHER_GAP)
+    return pl.pallas_call(
+        functools.partial(forward_kernel, dims, pieces, early, plan, late, strips),
+        grid=(strips * pairs,),
+        out_shape=[low((width, rows))]
+        + [low((3, rows, width))]
+        + [low((strips * pairs, 2, slots, slots)), low((rows, width))]
+        + [low((width, width))] * len(early_shards)
+        + [full((8, width)), full((1, ff))]
+        + [low(dims + (2,) + s.shape) for s in late_shards],
+        in_specs=[vmem] * (2 + len(shards)),
+        out_specs=[vmem] * 2
+        + [pl.BlockSpec((1, 2, slots, slots), lambda n: (n, 0, 0, 0)), vmem]
+        + [vmem] * (early + 1)
+        + [pl.BlockSpec(memory_space=pl.ANY)] * 3,
+        scratch_shapes=[pltpu.VMEM(dims + (2,) + s.shape, s.dtype) for s in shards[:early]]
+        + [pltpu.VMEM((rows, width), jnp.bfloat16)]
+        + comm_semaphores(pieces, gather_copies(dims, False)),
+        compiler_params=pltpu.CompilerParams(vmem_limit_bytes=VMEM_LIMIT, collective_id=2, has_side_effects=True),
+        name="forward",
+    )(tokens, mask, *shards)
+
+
 class Reduce:
     def __init__(self, lanes, whole, bufs, first, write):
         p, dims = lanes.place, lanes.place.dims
@@ -584,8 +630,7 @@
 class Plan:
     def __init__(self, dims, strips, rows, width, ff, lag, gap):
         self.tiles, self.pairs = ff // FF_TILE, width // 128
-        self.down = self.tiles
-        self.attention = 2 * self.tiles
+        self.attention = self.tiles
         self.finish = self.attention + strips * self.pairs
         self.steps = self.finish + FINISH
         n = 2 * dims[0] * dims[1] * dims[2]
@@ -594,10 +639,10 @@
         lasts = [0] + [per_up * (k + 1) for k in range(ff // width)] + [self.attention] * 3
         groups = self.pairs // PAIRS_PER_PIECE
         lasts += [self.attention + strips * PAIRS_PER_PIECE * (g + 1) for g in range(groups)]
-        self.wholes = [(model, width)] * (1 + ff // width) + [(wide, width)]
-        self.wholes += [(3 * model, width // groups)] * groups
+        self.wholes = [((), (model, width)), ((ff // width,), (model, width)), ((), (wide, width))]
+        self.wholes += [((groups,), (3 * model, width // groups))]
         self.shapes = [(model, width)] * (1 + ff // width) + [(wide, width // 3)] * 3 + [(3 * model, width // groups)] * groups
-        ends = [1.4] * self.attention + [3.2] * (strips * self.pairs) + [1.6] * FINISH
+        ends = [2.6] * self.attention + [3.2] * (strips * self.pairs) + [1.6] * FINISH
         starts = [sum(ends[:k]) for k in range(self.steps)]
         events, free = [], 0.0
         for piece, step in enumerate(lasts):
@@ -614,20 +659,33 @@
                 self.late.append((piece, stage))
 
 
+def by_step(step, table):
+    keys = sorted(table)
+
+    def pick(low, high):
+        if high - low == 1:
+            pl.when(step == keys[low])(table[keys[low]])
+            return
+        middle = (low + high) // 2
+        lax.cond(step < keys[middle], lambda: pick(low, middle), lambda: pick(middle, high))
+
+    pick(0, len(keys))
+
+
 def backward_kernel(dims, plan, strips, *refs):
     (turned, turned_two, out_grad, q_weight, k_weight, v_weight, vectors, small_in, bup_in) = refs[:9]
-    (grad_hidden, active, probs, query_b, key_b, value_b, grad_b, tokens, grad_res, wo_hbm) = refs[9:19]
-    (grad_tokens, sum_q, sum_k, sum_v, sum_o, sum_up, sum_down, sum_vec) = refs[19:27]
-    refs = refs[27:]
-    grad_q, grad_k, grad_v, small, vec_whole = refs[:5]
-    wholes, refs = refs[5 : 5 + len(plan.wholes)], refs[5 + len(plan.wholes) :]
+    (grad_hidden, active, probs, heads, grad_b, tokens, grad_res, wo_hbm) = refs[9:17]
+    (grad_tokens, sum_q, sum_k, sum_v, sum_o, sum_up, sum_down, sum_vec) = refs[17:25]
+    refs = refs[25:]
+    grad_q, grad_k, grad_v, small, vec_whole, o_whole, up_whole, down_whole, qkv_whole = refs[:9]
+    refs = refs[9:]
     local, send, recv = refs[-3:]
     width, rows = turned.shape
-    slots, ff_pieces, groups = rows // strips, sum_up.shape[1] // width, len(plan.wholes) - 2 - sum_up.shape[1] // width
+    slots, ff_pieces, groups = rows // strips, up_whole.shape[0], qkv_whole.shape[0]
     step = pl.program_id(0)
     place = Place(dims)
     lanes = Lanes(place, local, send, recv)
-    o_copy = lanes.local(wo_hbm, wholes[0])
+    o_copy = lanes.local(wo_hbm, o_whole)
 
     model = sum_q.shape[0]
     columns = width // groups
@@ -644,13 +702,12 @@
         return write
 
     third = width // 3
-    down_whole = wholes[1 + ff_pieces]
-    views = [(wholes[0], write_to(sum_o, 0, width))]
-    views += [(wholes[1 + k], write_to(sum_up, k * width, width)) for k in range(ff_pieces)]
+    views = [(o_whole, write_to(sum_o, 0, width))]
+    views += [(up_whole.at[k], write_to(sum_up, k * width, width)) for k in range(ff_pieces)]
     views += [
         (down_whole.at[:, :, :, :, :, pl.ds(k * third, third)], write_to(sum_down, k * third, third)) for k in range(3)
     ]
-    views += [(wholes[2 + ff_pieces + g], write_group(g)) for g in range(groups)]
+    views += [(qkv_whole.at[g], write_group(g)) for g in range(groups)]
     views += [(vec_whole, write_to(sum_vec, 0, sum_vec.shape[1]))]
     jobs = [Reduce(lanes, whole, refs[5 * n : 5 * n + 5], 1 + n % 2, write) for n, (whole, write) in enumerate(views)]
     last = len(jobs) - 1
@@ -662,27 +719,24 @@
         small[...] = small_in[...]
         o_copy.wait()
 
-    for when, wave in plan.waves.items():
-        pl.when(step == when)(lambda wave=wave: add_wave(jobs, wave) and None)
+    by_step(step, {when: lambda wave=wave: add_wave(jobs, wave) and None for when, wave in plan.waves.items()})
 
     def rows_to_blocks(product):
         n = 2 * dims[0] * dims[1] * dims[2]
         return product.reshape(dims + (2, product.shape[0] // n, product.shape[1])).astype(jnp.bfloat16)
 
-    for k in range(plan.tiles):
-        @pl.when(step == k)
-        def _():
-            piece, part = divmod(k * FF_TILE, width)
-            wholes[1 + piece][:, :, :, :, :, pl.ds(part, FF_TILE)] = rows_to_blocks(right_mul(turned_two[...], grad_hidden[...]))
-
-        @pl.when(step == plan.down + k)
-        def _():
-            product = left_mul(active[...], out_grad[...])
-            wide = down_whole.shape[4]
-            for b in range(FF_TILE // wide):
-                d = k * (FF_TILE // wide) + b
-                at = (d // (2 * dims[1] * dims[2]), d // (2 * dims[2]) % dims[1], d // 2 % dims[2], d % 2)
-                down_whole[at] = product[b * wide : (b + 1) * wide].astype(jnp.bfloat16)
+    @pl.when(step < plan.attention)
+    def _():
+        per = width // FF_TILE
+        part = pl.ds(pl.multiple_of(lax.rem(step, per) * FF_TILE, FF_TILE), FF_TILE)
+        up_whole[lax.div(step, per), :, :, :, :, :, part] = rows_to_blocks(right_mul(turned_two[...], grad_hidden[...]))
+        product = left_mul(active[...], out_grad[...])
+        wide = down_whole.shape[4]
+        for b in range(FF_TILE // wide):
+            d = step * (FF_TILE // wide) + b
+            y_x = lax.div(d, 2)
+            at = (lax.div(y_x, dims[1] * dims[2]), lax.rem(lax.div(y_x, dims[2]), dims[1]), lax.rem(y_x, dims[2]), lax.rem(d, 2))
+            down_whole[at] = product[b * wide : (b + 1) * wide].astype(jnp.bfloat16)
 
     pair, strip = lax.div(step - plan.attention, strips), lax.rem(step - plan.attention, strips)
     in_attention = (step >= plan.attention) & (step < plan.finish)
@@ -691,7 +745,7 @@
     def _():
         at = pl.ds(pl.multiple_of(strip * slots, slots), slots)
         cols = pl.ds(pl.multiple_of(pair * 128, 128), 128)
-        query, key, value, grad = query_b[...], key_b[...], value_b[...], grad_b[...]
+        query, key, value, grad = heads[0], heads[1], heads[2], grad_b[...]
         back_q = back_k = back_v = jnp.zeros((slots, 128), jnp.float32)
         for head in range(2):
             low = probs[0, head]
@@ -707,17 +761,17 @@
         grad_k[at, cols] = back_k.astype(jnp.bfloat16)
         grad_v[at, cols] = back_v.astype(jnp.bfloat16)
 
-    for g in range(groups):
-        @pl.when(step == plan.attention + strips * PAIRS_PER_PIECE * (g + 1) - 1)
-        def _():
-            whole = wholes[2 + ff_pieces + g]
-            for n, grad in enumerate((grad_q, grad_k, grad_v)):
-                part = grad[:, pl.ds(g * columns, columns)]
-                whole[:, :, :, :, pl.ds(n * model, model), :] = rows_to_blocks(right_mul(turned[...], part))
-                if n != 1:
-                    small[2 + n // 2 : 3 + n // 2, pl.ds(g * columns, columns)] = jnp.sum(
-                        part.astype(jnp.float32), axis=0, keepdims=True
-                    )
+    group_steps = strips * PAIRS_PER_PIECE
+
+    @pl.when(in_attention & (lax.rem(step - plan.attention, group_steps) == group_steps - 1))
+    def _():
+        g = lax.div(step - plan.attention, group_steps)
+        cols = pl.ds(pl.multiple_of(g * columns, columns), columns)
+        for n, grad in enumerate((grad_q, grad_k, grad_v)):
+            part = grad[:, cols]
+            qkv_whole[g, :, :, :, :, pl.ds(n * model, model), :] = rows_to_blocks(right_mul(turned[...], part))
+            if n != 1:
+                small[2 + n // 2 : 3 + n // 2, cols] = jnp.sum(part.astype(jnp.float32), axis=0, keepdims=True)
 
     @pl.when(step >= plan.finish)
     def _():
@@ -731,9 +785,7 @@
         small[0:1, :] += gain_sum
         small[1:2, :] += bias_sum
 
-    for when, wave in plan.waves.items():
-        n, stage = wave[-1]
-        pl.when(step == when)(functools.partial(jobs[n].ship, stage))
+    by_step(step, {when: functools.partial(jobs[wave[-1][0]].ship, wave[-1][1]) for when, wave in plan.waves.items()})
 
     @pl.when(step == plan.steps - 1)
     def _():
@@ -755,7 +807,7 @@
 
 
 def backward(dims, strips, turned, turned_two, out_grad, q_weight, k_weight, v_weight, vectors, small, grad_bup,
-             grad_hidden, active, probs, queries, keys, values, grad_context, tokens, grad_res, grad_wo):
+             grad_hidden, active, probs, heads, grad_context, tokens, grad_res, grad_wo):
     width, rows = turned.shape
     ff = grad_hidden.shape[1]
     slots = rows // strips
@@ -777,7 +829,6 @@
         strip, pair = strip_pair(step)
         return (strip * plan.pairs + pair, 0, 0, 0)
 
-    qkv = pl.BlockSpec((slots, 128), strip_pair)
     ending = pl.BlockSpec((rows // FINISH, width), lambda step: (part(step, plan.finish, FINISH), 0))
     shapes = plan.shapes
     bufs = []
@@ -792,21 +843,23 @@
         in_specs=[vmem] * 9
         + [
             pl.BlockSpec((rows, FF_TILE), lambda step: (0, part(step, 0, plan.tiles))),
-            pl.BlockSpec((rows, FF_TILE), lambda step: (0, part(step, plan.down, plan.tiles))),
+            pl.BlockSpec((rows, FF_TILE), lambda step: (0, part(step, 0, plan.tiles))),
             pl.BlockSpec((1, 2, slots, slots), probs_at),
-            qkv, qkv, qkv, qkv, ending, ending,
+            pl.BlockSpec((3, slots, 128), lambda step: (0,) + strip_pair(step)),
+            pl.BlockSpec((slots, 128), strip_pair),
+            ending, ending,
             pl.BlockSpec(memory_space=pl.ANY),
         ],
         out_specs=[ending] + [vmem] * 7,
         scratch_shapes=[pltpu.VMEM((rows, width), jnp.bfloat16)] * 3
         + [pltpu.VMEM((8, width), jnp.float32), pltpu.VMEM(dims + (2, 16, lanes_wide), jnp.float32)]
-        + [pltpu.VMEM(dims + (2,) + shape, jnp.bfloat16) for shape in plan.wholes]
+        + [pltpu.VMEM(lead + dims + (2,) + shape, jnp.bfloat16) for lead, shape in plan.wholes]
         + bufs
         + [pltpu.SemaphoreType.DMA((1,)), pltpu.SemaphoreType.DMA((copies,)), pltpu.SemaphoreType.DMA((copies,))],
         compiler_params=pltpu.CompilerParams(collective_id=3, has_side_effects=True, vmem_limit_bytes=VMEM_LIMIT),
         name="backward",
     )(turned, turned_two, out_grad, q_weight, k_weight, v_weight, vectors, small, grad_bup,
-      grad_hidden, active, probs, queries, keys, values, grad_context, tokens, grad_res, grad_wo)
+      grad_hidden, active, probs, heads, grad_context, tokens, grad_res, grad_wo)
 
 
 def lane_pad(rows, width):
@@ -818,12 +871,6 @@
     rows = lane_pad(jnp.stack(vectors).astype(jnp.float32), width)
     last = lane_pad(wide[None].astype(jnp.float32), width)
     return jnp.pad(jnp.concatenate([rows, last]), ((0, 15 - len(vectors)), (0, 0)))
-
-
-def unpack_vectors(block, part, wide_part):
-    flat = block.reshape((-1,) + block.shape[-2:])
-    rows = flat[:, :8, :part].transpose(1, 0, 2).reshape(8, -1)
-    return rows, flat[:, 8, :wide_part].reshape(1, -1)
 
 
 def shards(
@@ -856,15 +903,6 @@
     def whole(shard):
         return lax.all_gather(shard, axes, axis=0, tiled=True)
 
-    if fused:
-        *wide, packed = gather_all(dims, list(early_weights) + [pack_vectors(vectors, up_bias)])
-        q_full, k_full, v_full = [w.reshape((-1,) + w.shape[-1:]) for w in wide]
-        rows, up_bias_full = unpack_vectors(packed, ln1_gain.shape[0], up_bias.shape[0])
-    else:
-        q_full, k_full, v_full = [whole(w) for w in early_weights]
-        rows = jnp.stack([whole(v) for v in vectors]).astype(jnp.float32)
-        up_bias_full = whole(up_bias).astype(jnp.float32)[None]
-
     row_count, width = tokens.shape
     strips = lengths.shape[0]
     slots = row_count // strips
@@ -881,20 +919,23 @@
     mask = jnp.where(jnp.pad(visible, ((0, 0), (0, extra))), 0.0, NEG_FILL).reshape(-1, 1)
     tokens_in, grads_in = padded(tokens), padded(out_grad)
 
-    turned, queries, keys, values, probs, context, *late = attend(
-        dims, late_weights if fused else (), strips, tokens_in, q_full, k_full, v_full, rows, mask
-    )
     if fused:
+        turned, heads, probs, context, q_full, k_full, v_full, rows, up_bias_full, *late = forward(
+            dims, strips, tokens_in, mask, pack_vectors(vectors, up_bias), early_weights, late_weights
+        )
         o_full, up_full, down_full = [w.reshape((-1,) + w.shape[-1:]) for w in late]
     else:
-        o_full, up_full, down_full = [whole(w) for w in late_weights]
+        q_full, k_full, v_full, o_full, up_full, down_full = [whole(w) for w in early_weights + late_weights]
+        rows = jnp.stack([whole(v) for v in vectors]).astype(jnp.float32)
+        up_bias_full = whole(up_bias).astype(jnp.float32)[None]
+        turned, queries, keys, values, probs, context = attend(strips, tokens_in, q_full, k_full, v_full, rows, mask)
     block_out, grad_res, grad_context, grad_wo, active, grad_hidden, turned_two, small, grad_bup = ffn(
         tokens_in, context, grads_in, o_full, up_full, down_full, rows, up_bias_full
     )
     if fused:
         grad_tokens, sum_wq, sum_wk, sum_wv, sum_wo, sum_wup, sum_wdown, least = backward(
             dims, strips, turned, turned_two, grads_in, q_full, k_full, v_full, rows, small, grad_bup,
-            grad_hidden, active, probs, queries, keys, values, grad_context, tokens_in, grad_res,
+            grad_hidden, active, probs, heads, grad_context, tokens_in, grad_res,
             grad_wo.reshape(dims + (2,) + o_weight.shape),
         )
         vec = [least[n, : ln1_gain.shape[0]] for n in range(8)]

time: 296 us -> 252 us (0.85)
  Pallas kernels: 266 us -> 226 us
  local copies, waits for them, and re-layouts: 25.7 us -> 22.4 us
    pallas_call x1, Pallas kernels: 118 us -> 95.2 us  [backward(): pl.pallas_call(functools.partial(backward_kernel, dims, plan, strips), gr...]
    pallas_call x2 -> x1, Pallas kernels: 103 us -> 85.9 us  [forward(): pl.pallas_call(functools.partial(forward_kernel, dims, pieces, early, pla...]
    unnamed x17 -> x16, local copies, waits for them, and re-layouts: 7.59 us -> 7.55 us
where the time goes in v4:
time: 252 us
  Pallas kernels  226 us (90%)
  local copies, waits for them, and re-layouts  22.4 us (9%)
    pallas_call x1, Pallas kernels, backward(): pl.pallas_call(functools.partial(backward_kernel, dims, plan, strips), gr...  95.2 us
    pallas_call x1, Pallas kernels, forward(): pl.pallas_call(functools.partial(forward_kernel, dims, pieces, early, pla...  85.9 us
    pallas_call x1, Pallas kernels, ffn(): pl.pallas_call(functools.partial(ffn_kernel, rows, rows, 1024, rows // 2)...  45.3 us
    unnamed x16, local copies, waits for them, and re-layouts  7.55 us

profile of v4, /device:TPU:0, one launch (start us, length us, event | category | flops | bytes accessed | tf_op | source)
XLA Modules:
  0.0 251.7 jit_solution(9813723710796133487)
XLA Ops:
  0.7 0.8 and_or_fusion
  1.4 0.8 stack.35
  2.2 0.7 fusion.2
  2.9 0.6 pad_convert_fusion.refs_0_
  3.5 1.2 reshape.94.mask
  4.7 1.8 reshape.81
  6.4 0.0 copy-start
  6.5 1.3 pad.27
  7.8 0.7 copy-done
  8.5 0.3 reshape.84
  8.8 1.3 pad.33
  10.1 85.9 %forward.1 = (bf16[768,1088]{1,0:T(8,128)(2,1)}, bf16[3,1088,768]{2,1,0:T(8,128)(2,1)}, bf16[12,2,544,544]{3,2,1,0:T(8,128)(2,1)}, bf16[1088,768]{1,0:T(8,128)(2...) custom-call(bf16[1088,768]{1,0:T(8,128)(2,1)} %bitcast.35, ...), custom_call_target="tpu_custom_call" | custom-call | tf_op jit(solution)/shard_map/forward/pallas_call | solution.py:521
  96.0 45.3 %ffn.1 = (bf16[1088,768]{1,0:T(8,128)(2,1)}, f32[1088,768]{1,0:T(8,128)}, bf16[1088,768]{1,0:T(8,128)(2,1)}, bf16[768,768]{1,0:T(8,128)(2,1)}, bf16[1088,3072]{1...) custom-call(bf16[1088,768]{1,0:T(8,128)(2,1)} %bitcast.36, ...), custom_call_target="tpu_custom_call" | custom-call | tf_op jit(solution)/shard_map/ffn/pallas_call | solution.py:299
  141.3 95.2 %backward.1 = (f32[1088,768]{1,0:T(8,128)}, f32[24,768]{1,0:T(8,128)}, f32[24,768]{1,0:T(8,128)}, f32[24,768]{1,0:T(8,128)}, f32[24,768]{1,0:T(8,128)}, /*index=...) custom-call(bf16[768,1088]{1,0:T(8,128)(2,1)} %get-tuple-element.53.refs_0_, ...), custom_call_target="tpu_custom_call" | custom-call | tf_op jit(solution)/shard_map/backward/pallas_call | solution.py:839
  236.5 1.5 slice.44
  238.1 1.5 reshape.90
  239.6 2.1 slice.45
  241.7 0.0 copy-start.4
  241.7 0.0 copy-start.3
  241.7 0.0 copy-start.2
  241.8 0.0 copy-start.1
  241.8 2.0 reshape.93
  243.8 0.0 copy-done.4
  243.8 0.5 slice_bitcast_fusion.1
  244.3 0.5 slice_bitcast_fusion
  244.8 1.5 copy.43
  246.4 0.0 copy-done.3
  246.4 0.6 copy.44
  247.0 0.0 copy-done.2
  247.0 0.6 copy.45
  247.6 0.0 copy-done.1
  247.6 0.6 copy.46
  248.3 1.7 copy.47
  250.0 1.7 copy.48
  (2 shorter events, 0.0 us)
Async XLA Ops:
  6.4 2.0 copy-start
  241.7 2.1 copy-start.4
  241.7 4.6 %copy-start.3 = (f32[24,768]{1,0:T(8,128)S(1)}, f32[24,768]{1,0:T(8,128)}, u32[]{:S(2)}) copy-start(f32[24,768]{1,0:T(8,128)} %get-tuple-element.106) | copy-start | bytes 221188
  241.7 5.3 %copy-start.2 = (f32[24,768]{1,0:T(8,128)S(1)}, f32[24,768]{1,0:T(8,128)}, u32[]{:S(2)}) copy-start(f32[24,768]{1,0:T(8,128)} %get-tuple-element.107) | copy-start | bytes 221188
  241.8 5.9 %copy-start.1 = (f32[24,768]{1,0:T(8,128)S(1)}, f32[24,768]{1,0:T(8,128)}, u32[]{:S(2)}) copy-start(f32[24,768]{1,0:T(8,128)} %get-tuple-element.109) | copy-start | bytes 221188

commit v5 on v4

--- a/solution.py
+++ b/solution.py
@@ -227,14 +227,35 @@
 
 def ffn_kernel(
     a_rows, b_rows, ff_tile, c_rows,
-    tokens, context, out_grad, o_weight, up_weight, down_weight, vectors, up_bias,
-    block_out, grad_res, grad_context, grad_wo, active, grad_hidden, normed2_t, small, grad_bup,
-    normed2, grad_att,
+    tokens_hbm, context_hbm, out_grad_hbm, o_hbm, up_hbm, down_hbm, vectors, up_bias,
+    block_out, res_hbm, back_hbm, grad_wo, active_hbm, hidden_hbm, normed2_t, small, grad_bup,
+    normed2, grad_att, tokens, context, out_grad, o_weight, up_weight, down_weight,
+    grad_res, grad_context, active, grad_hidden, outputs, loaded, stored,
 ):
     rows, width = tokens.shape
     ff = up_weight.shape[1]
     o_bias, gain, bias, down_bias = vectors[4:5, :], vectors[5:6, :], vectors[6:7, :], vectors[7:8, :]
     small[...] = jnp.zeros_like(small)
+    loads = [
+        pltpu.make_async_copy(src, dst, loaded.at[n])
+        for n, (src, dst) in enumerate((
+            (context_hbm, context), (o_hbm, o_weight), (tokens_hbm, tokens), (out_grad_hbm, out_grad),
+        ))
+    ]
+
+    def tile_in(n, kind):
+        at = pl.ds(n * ff_tile if isinstance(n, int) else pl.multiple_of(n * ff_tile, ff_tile), ff_tile)
+        if kind:
+            return pltpu.make_async_copy(down_hbm.at[at, :], down_weight.at[at, :], loaded.at[4 + 2 * n + kind])
+        return pltpu.make_async_copy(up_hbm.at[:, at], up_weight.at[:, at], loaded.at[4 + 2 * n + kind])
+
+    for copy in loads:
+        copy.start()
+    for n in range(ff // ff_tile):
+        tile_in(n, 0).start()
+        tile_in(n, 1).start()
+    for copy in loads[:3]:
+        copy.wait()
 
     def attended(n, carry):
         at = pl.ds(pl.multiple_of(n * a_rows, a_rows), a_rows)
@@ -245,10 +266,24 @@
         return carry
 
     lax.fori_loop(0, rows // a_rows, attended, 0)
+    for copy in loads[3:]:
+        copy.wait()
+
+    def tile_out(n, kind):
+        cols = pl.ds(pl.multiple_of(n * ff_tile, ff_tile), ff_tile)
+        src, dst = ((active, active_hbm), (grad_hidden, hidden_hbm))[kind]
+        return pltpu.make_async_copy(src.at[:, cols], dst.at[:, cols], stored.at[2 * n + kind])
+
+    def strip_out(n, kind):
+        at = pl.ds(pl.multiple_of(n * c_rows, c_rows), c_rows)
+        src, dst = ((grad_res, res_hbm), (grad_context, back_hbm))[kind]
+        return pltpu.make_async_copy(src.at[at, :], dst.at[at, :], stored.at[2 * (ff // ff_tile + n) + kind])
 
     def hidden_tile(n, carry):
         cols = pl.ds(pl.multiple_of(n * ff_tile, ff_tile), ff_tile)
         sums = jnp.zeros((1, ff_tile), jnp.float32)
+        tile_in(n, 0).wait()
+        tile_in(n, 1).wait()
 
         def piece(m, sums):
             at = pl.ds(pl.multiple_of(m * b_rows, b_rows), b_rows)
@@ -261,6 +296,8 @@
             return sums + jnp.sum(back.astype(jnp.float32), axis=0, keepdims=True)
 
         grad_bup[:, cols] = lax.fori_loop(0, rows // b_rows, piece, sums)
+        tile_out(n, 0).start()
+        tile_out(n, 1).start()
         return carry
 
     lax.fori_loop(0, ff // ff_tile, hidden_tile, 0)
@@ -269,7 +306,7 @@
         at = pl.ds(pl.multiple_of(n * c_rows, c_rows), c_rows)
         residual = grad_res[at, :]
         cotangent = out_grad[at, :].astype(jnp.float32)
-        block_out[at, :] = (residual + right_mul(active[at, :], down_weight[...]) + down_bias).astype(jnp.bfloat16)
+        outputs[at, :] = (residual + right_mul(active[at, :], down_weight[...]) + down_bias).astype(jnp.bfloat16)
         grad = back_mul(grad_hidden[at, :], up_weight[...])
         xhat, scale = layer_norm_parts(residual)
         back, gain_sum, bias_sum = layer_norm_back(grad, xhat, scale, gain)
@@ -282,29 +319,52 @@
         small[5:6, :] += gain_sum
         small[6:7, :] += bias_sum
         small[7:8, :] += jnp.sum(cotangent, axis=0, keepdims=True)
+        strip_out(n, 0).start()
+        strip_out(n, 1).start()
         return carry
 
     lax.fori_loop(0, rows // c_rows, finish, 0)
 
     normed2_t[...] = normed2[...].T
     grad_wo[...] = left_mul(context[...], grad_att[...]).astype(jnp.bfloat16)
-
-
-def ffn(tokens, context, out_grad, o_weight, up_weight, down_weight, vectors, up_bias):
+    slots = block_out.shape[0] * c_rows // rows
+    for n in range(rows // c_rows):
+        block_out[n * slots : (n + 1) * slots, :] = outputs[n * c_rows : n * c_rows + slots, :]
+    for n in range(ff // ff_tile):
+        tile_out(n, 0).wait()
+        tile_out(n, 1).wait()
+    for n in range(rows // c_rows):
+        strip_out(n, 0).wait()
+        strip_out(n, 1).wait()
+
+
+def ffn(strips, row_count, tokens, context, out_grad, o_weight, up_weight, down_weight, vectors, up_bias):
     rows, width = tokens.shape
     ff = up_weight.shape[1]
     low = functools.partial(jax.ShapeDtypeStruct, dtype=jnp.bfloat16)
     full = functools.partial(jax.ShapeDtypeStruct, dtype=jnp.float32)
-    vmem = pl.BlockSpec(memory_space=pltpu.VMEM)
+    vmem, hbm = pl.BlockSpec(memory_space=pltpu.VMEM), pl.BlockSpec(memory_space=pl.ANY)
     return pl.pallas_call(
-        functools.partial(ffn_kernel, rows, rows, 1024, rows // 2),
+        functools.partial(ffn_kernel, rows, rows, 1024, rows // strips),
         out_shape=[
-            low((rows, width)), full((rows, width)), low((rows, width)),
+            low((row_count, width)), full((rows, width)), low((rows, width)),
             low((width, width)), low((rows, ff)), low((rows, ff)), low((width, rows)), full((8, width)), full((1, ff)),
         ],
-        in_specs=[vmem] * 8,
-        out_specs=[vmem] * 9,
-        scratch_shapes=[pltpu.VMEM((rows, width), jnp.bfloat16)] * 2,
+        in_specs=[hbm] * 6 + [vmem] * 2,
+        out_specs=[vmem, hbm, hbm, vmem, hbm, hbm, vmem, vmem, vmem],
+        scratch_shapes=[pltpu.VMEM((rows, width), jnp.bfloat16)] * 5
+        + [
+            pltpu.VMEM((width, width), jnp.bfloat16),
+            pltpu.VMEM((width, ff), jnp.bfloat16),
+            pltpu.VMEM((ff, width), jnp.bfloat16),
+            pltpu.VMEM((rows, width), jnp.float32),
+            pltpu.VMEM((rows, width), jnp.bfloat16),
+            pltpu.VMEM((rows, ff), jnp.bfloat16),
+            pltpu.VMEM((rows, ff), jnp.bfloat16),
+            pltpu.VMEM((rows, width), jnp.bfloat16),
+            pltpu.SemaphoreType.DMA((4 + 2 * ff // 1024,)),
+            pltpu.SemaphoreType.DMA((2 * (ff // 1024 + strips),)),
+        ],
         compiler_params=pltpu.CompilerParams(vmem_limit_bytes=VMEM_LIMIT),
         name="ffn",
     )(tokens, context, out_grad, o_weight, up_weight, down_weight, vectors, up_bias)
@@ -452,10 +512,10 @@
     return plan, late
 
 
-def forward_kernel(dims, pieces, early, plan, late, strips, tokens, mask, *refs):
+def forward_kernel(dims, pieces, early, plan, late, strips, tokens_in, grads_in, mask, *refs):
     count = early + 3
     shards, refs = refs[:count], refs[count:]
-    (turned, heads, probs, context), refs = refs[:4], refs[4:]
+    (turned, heads, probs, context, tokens, grads), refs = refs[:6], refs[6:]
     queries, keys, values = heads.at[0], heads.at[1], heads.at[2]
     weights, (vectors, up_bias), bufs, refs = refs[: early - 1], refs[early - 1 : early + 1], refs[early + 1 : early + 4], refs[early + 4 :]
     near, normed, sems = refs[:early], refs[early], refs[early + 1 :]
@@ -470,6 +530,11 @@
         place.barrier()
         for job in jobs:
             job.run(0)
+        given = tokens_in.shape[0] // strips
+        for src, dst in ((tokens_in, tokens), (grads_in, grads)):
+            dst[...] = jnp.zeros_like(dst)
+            for n in range(strips):
+                dst[n * slots : n * slots + given, :] = src[n * given : (n + 1) * given, :]
         xhat, _ = layer_norm_parts(tokens[...].astype(jnp.float32))
         run_wave(jobs, plan[0])
         for job in jobs[:early]:
@@ -505,8 +570,8 @@
             job.finish()
 
 
-def forward(dims, strips, tokens, mask, packed, early_shards, late_shards):
-    rows, width = tokens.shape
+def forward(dims, strips, tokens, grads, mask, packed, early_shards, late_shards):
+    rows, width = mask.shape[0], tokens.shape[1]
     slots, pairs = rows // strips, width // 128
     shards = [packed] + list(early_shards) + list(late_shards)
     early = 1 + len(early_shards)
@@ -523,13 +588,13 @@
         grid=(strips * pairs,),
         out_shape=[low((width, rows))]
         + [low((3, rows, width))]
-        + [low((strips * pairs, 2, slots, slots)), low((rows, width))]
+        + [low((strips * pairs, 2, slots, slots))] + [low((rows, width))] * 3
         + [low((width, width))] * len(early_shards)
         + [full((8, width)), full((1, ff))]
         + [low(dims + (2,) + s.shape) for s in late_shards],
-        in_specs=[vmem] * (2 + len(shards)),
+        in_specs=[vmem] * (3 + len(shards)),
         out_specs=[vmem] * 2
-        + [pl.BlockSpec((1, 2, slots, slots), lambda n: (n, 0, 0, 0)), vmem]
+        + [pl.BlockSpec((1, 2, slots, slots), lambda n: (n, 0, 0, 0)), vmem, vmem, vmem]
         + [vmem] * (early + 1)
         + [pl.BlockSpec(memory_space=pl.ANY)] * 3,
         scratch_shapes=[pltpu.VMEM(dims + (2,) + s.shape, s.dtype) for s in shards[:early]]
@@ -537,7 +602,7 @@
         + comm_semaphores(pieces, gather_copies(dims, False)),
         compiler_params=pltpu.CompilerParams(vmem_limit_bytes=VMEM_LIMIT, collective_id=2, has_side_effects=True),
         name="forward",
-    )(tokens, mask, *shards)
+    )(tokens, grads, mask, *shards)
 
 
 class Reduce:
@@ -677,8 +742,8 @@
     (grad_hidden, active, probs, heads, grad_b, tokens, grad_res, wo_hbm) = refs[9:17]
     (grad_tokens, sum_q, sum_k, sum_v, sum_o, sum_up, sum_down, sum_vec) = refs[17:25]
     refs = refs[25:]
-    grad_q, grad_k, grad_v, small, vec_whole, o_whole, up_whole, down_whole, qkv_whole = refs[:9]
-    refs = refs[9:]
+    grad_q, grad_k, grad_v, small, vec_whole, finished, o_whole, up_whole, down_whole, qkv_whole = refs[:10]
+    refs = refs[10:]
     local, send, recv = refs[-3:]
     width, rows = turned.shape
     slots, ff_pieces, groups = rows // strips, up_whole.shape[0], qkv_whole.shape[0]
@@ -781,10 +846,18 @@
         grad = grad + back_mul(grad_v[at, :], v_weight[...])
         xhat, scale = layer_norm_parts(tokens[...].astype(jnp.float32))
         back, gain_sum, bias_sum = layer_norm_back(grad, xhat, scale, vectors[0:1, :])
-        grad_tokens[...] = grad_res[...] + back
+        finished[...] = grad_res[...] + back
         small[0:1, :] += gain_sum
         small[1:2, :] += bias_sum
 
+    def store(n):
+        size, slots_in = rows // FINISH, grad_tokens.shape[0] // strips
+        per = FINISH // strips
+        low = (n % per) * size
+        count = min(size, slots_in - low)
+        grad_tokens[pl.ds(n // per * slots_in + low, count), :] = finished[0:count, :]
+
+    by_step(step, {plan.finish + n: functools.partial(store, n) for n in range(FINISH)})
     by_step(step, {when: functools.partial(jobs[wave[-1][0]].ship, wave[-1][1]) for when, wave in plan.waves.items()})
 
     @pl.when(step == plan.steps - 1)
@@ -806,7 +879,7 @@
             job.finish()
 
 
-def backward(dims, strips, turned, turned_two, out_grad, q_weight, k_weight, v_weight, vectors, small, grad_bup,
+def backward(dims, strips, row_count, turned, turned_two, out_grad, q_weight, k_weight, v_weight, vectors, small, grad_bup,
              grad_hidden, active, probs, heads, grad_context, tokens, grad_res, grad_wo):
     width, rows = turned.shape
     ff = grad_hidden.shape[1]
@@ -839,7 +912,7 @@
     return pl.pallas_call(
         functools.partial(backward_kernel, dims, plan, strips),
         grid=(plan.steps,),
-        out_shape=[full((rows, width))] + [full((model, width))] * 4 + [full((model, ff)), full((wide, width)), full((16, lanes_wide))],
+        out_shape=[full((row_count, width))] + [full((model, width))] * 4 + [full((model, ff)), full((wide, width)), full((16, lanes_wide))],
         in_specs=[vmem] * 9
         + [
             pl.BlockSpec((rows, FF_TILE), lambda step: (0, part(step, 0, plan.tiles))),
@@ -850,9 +923,10 @@
             ending, ending,
             pl.BlockSpec(memory_space=pl.ANY),
         ],
-        out_specs=[ending] + [vmem] * 7,
+        out_specs=[vmem] * 8,
         scratch_shapes=[pltpu.VMEM((rows, width), jnp.bfloat16)] * 3
         + [pltpu.VMEM((8, width), jnp.float32), pltpu.VMEM(dims + (2, 16, lanes_wide), jnp.float32)]
+        + [pltpu.VMEM((rows // FINISH, width), jnp.float32)]
         + [pltpu.VMEM(lead + dims + (2,) + shape, jnp.bfloat16) for lead, shape in plan.wholes]
         + bufs
         + [pltpu.SemaphoreType.DMA((1,)), pltpu.SemaphoreType.DMA((copies,)), pltpu.SemaphoreType.DMA((copies,))],
@@ -917,24 +991,24 @@
     slot_ids = lax.iota(jnp.int32, slots)
     visible = (slot_ids[None, :] == 0) | (slot_ids[None, :] < lengths[:, None]) & (key_mask == 1)
     mask = jnp.where(jnp.pad(visible, ((0, 0), (0, extra))), 0.0, NEG_FILL).reshape(-1, 1)
-    tokens_in, grads_in = padded(tokens), padded(out_grad)
 
     if fused:
-        turned, heads, probs, context, q_full, k_full, v_full, rows, up_bias_full, *late = forward(
-            dims, strips, tokens_in, mask, pack_vectors(vectors, up_bias), early_weights, late_weights
+        turned, heads, probs, context, tokens_in, grads_in, q_full, k_full, v_full, rows, up_bias_full, *late = forward(
+            dims, strips, tokens, out_grad, mask, pack_vectors(vectors, up_bias), early_weights, late_weights
         )
         o_full, up_full, down_full = [w.reshape((-1,) + w.shape[-1:]) for w in late]
     else:
+        tokens_in, grads_in = padded(tokens), padded(out_grad)
         q_full, k_full, v_full, o_full, up_full, down_full = [whole(w) for w in early_weights + late_weights]
         rows = jnp.stack([whole(v) for v in vectors]).astype(jnp.float32)
         up_bias_full = whole(up_bias).astype(jnp.float32)[None]
         turned, queries, keys, values, probs, context = attend(strips, tokens_in, q_full, k_full, v_full, rows, mask)
     block_out, grad_res, grad_context, grad_wo, active, grad_hidden, turned_two, small, grad_bup = ffn(
-        tokens_in, context, grads_in, o_full, up_full, down_full, rows, up_bias_full
+        strips, row_count, tokens_in, context, grads_in, o_full, up_full, down_full, rows, up_bias_full
     )
     if fused:
         grad_tokens, sum_wq, sum_wk, sum_wv, sum_wo, sum_wup, sum_wdown, least = backward(
-            dims, strips, turned, turned_two, grads_in, q_full, k_full, v_full, rows, small, grad_bup,
+            dims, strips, row_count, turned, turned_two, grads_in, q_full, k_full, v_full, rows, small, grad_bup,
             grad_hidden, active, probs, heads, grad_context, tokens_in, grad_res,
             grad_wo.reshape(dims + (2,) + o_weight.shape),
         )
@@ -944,6 +1018,7 @@
         grad_tokens, grad_wq, grad_wk, grad_wv, small_two = attend_back(
             strips, tokens_in, turned, queries, keys, values, probs, grad_context, grad_res, q_full, k_full, v_full, rows
         )
+        grad_tokens = cropped(grad_tokens)
         small = small + small_two
         full = [grad_wq, grad_wk, grad_wv, grad_wo, right_mul(turned_two, grad_hidden), left_mul(active, grads_in), grad_bup[0]]
         full = [g.astype(jnp.float32) for g in full] + [small[n] for n in range(8)]
@@ -951,7 +1026,7 @@
             lax.psum_scatter(g, axes, scatter_dimension=0, tiled=True) for g in full
         ]
     return (
-        cropped(block_out), cropped(grad_tokens), vec[0], vec[1], sum_wq, vec[2], sum_wk, sum_wv, vec[3], sum_wo, vec[4],
+        block_out, grad_tokens, vec[0], vec[1], sum_wq, vec[2], sum_wk, sum_wv, vec[3], sum_wo, vec[4],
         vec[5], vec[6], sum_wup, sum_bup, sum_wdown, vec[7],
     )
 

time: 252 us -> 241 us (0.956)
  local copies, waits for them, and re-layouts: 22.4 us -> 12.6 us
    reshape x4 -> x0, local copies, waits for them, and re-layouts: 5.58 us -> none  [the longest x2 3.5 us: cropped(): values.reshape(strips, slots + extra, width)[:, :slots]]
    pallas_call x1, Pallas kernels: 45.3 us -> 41.4 us  [ffn(): pl.pallas_call(functools.partial(ffn_kernel, rows, rows, 1024, rows // st...]
    slice x2 -> x0, local copies, waits for them, and re-layouts: 3.69 us -> none  [cropped(): values.reshape(strips, slots + extra, width)[:, :slots]]
    pad x2 -> x0, local copies, waits for them, and re-layouts: 2.6 us -> none  [padded(): jnp.pad(values.reshape(strips, slots, width), ((0, 0), (0, extra), (0, 0)))]
    unnamed x16 -> x19, local copies, waits for them, and re-layouts: 7.55 us -> 7.9 us
where the time goes in v5:
time: 241 us; the launch traced here: 240 us
  Pallas kernels  225 us (93%)
  local copies, waits for them, and re-layouts  12.6 us (5%)
    pallas_call x1, Pallas kernels, backward(): pl.pallas_call(functools.partial(backward_kernel, dims, plan, strips), gr...  96.2 us
    pallas_call x1, Pallas kernels, forward(): pl.pallas_call(functools.partial(forward_kernel, dims, pieces, early, pla...  87.3 us
    pallas_call x1, Pallas kernels, ffn(): pl.pallas_call(functools.partial(ffn_kernel, rows, rows, 1024, rows // st...  41.4 us
    unnamed x19, local copies, waits for them, and re-layouts  7.9 us

profile of v5, /device:TPU:0, one launch (start us, length us, event | category | flops | bytes accessed | tf_op | source)
XLA Modules:
  0.0 240.3 jit_solution(2195994658170351311)
XLA Ops:
  0.7 0.8 and_or_fusion
  1.4 0.8 stack.35
  2.2 0.7 fusion.2
  2.9 0.6 pad_convert_fusion.refs_0_
  3.5 1.2 reshape.62.mask
  4.7 87.3 %forward.1 = (bf16[768,1088]{1,0:T(8,128)(2,1)}, bf16[3,1088,768]{2,1,0:T(8,128)(2,1)}, bf16[12,2,544,544]{3,2,1,0:T(8,128)(2,1)}, bf16[1088,768]{1,0:T(8,128)(2...) custom-call(bf16[1058,768]{1,0:T(8,128)(2,1)} %tokens_in.1, ...), custom_call_target="tpu_custom_call" | custom-call | tf_op jit(solution)/shard_map/forward/pallas_call | solution.py:586
  92.0 41.4 %ffn.1 = (bf16[1058,768]{1,0:T(8,128)(2,1)}, f32[1088,768]{1,0:T(8,128)}, bf16[1088,768]{1,0:T(8,128)(2,1)}, bf16[768,768]{1,0:T(8,128)(2,1)}, bf16[1088,3072]{1...) custom-call(bf16[1088,768]{1,0:T(8,128)(2,1)} %get-tuple-element.48., ...), custom_call_target="tpu_custom_call" | custom-call | tf_op jit(solution)/shard_map/ffn/pallas_call | solution.py:347
  133.4 96.2 %backward.1 = (f32[1058,768]{1,0:T(8,128)}, f32[24,768]{1,0:T(8,128)}, f32[24,768]{1,0:T(8,128)}, f32[24,768]{1,0:T(8,128)}, f32[24,768]{1,0:T(8,128)}, /*index=...) custom-call(bf16[768,1088]{1,0:T(8,128)(2,1)} %get-tuple-element.57.refs_0_, ...), custom_call_target="tpu_custom_call" | custom-call | tf_op jit(solution)/shard_map/backward/pallas_call | solution.py:912
  229.7 1.2 slice_bitcast_fusion.1
  230.9 1.5 slice_bitcast_fusion
  232.4 0.0 copy-start.5
  232.4 0.0 copy-start.4
  232.4 0.0 copy-start.3
  232.4 0.0 copy-start.2
  232.4 0.0 copy-start.1
  232.4 0.0 copy-start
  232.4 3.9 %copy.44 = f32[1058,768]{1,0:T(8,128)} copy(f32[1058,768]{1,0:T(8,128)} %get-tuple-element.105) | data formatting | bytes 6500352
  236.4 0.0 copy-done.5
  236.4 0.6 copy.45
  237.0 0.0 copy-done.4
  237.0 0.6 copy.46
  237.6 0.0 copy-done.3
  237.6 0.6 copy.47
  238.3 0.0 copy-done.2
  238.3 0.6 copy.48
  238.9 0.0 copy-done.1
  238.9 0.7 copy.49
  239.6 0.0 copy-done
  239.6 0.7 copy.50
  (2 shorter events, 0.0 us)
Async XLA Ops:
  232.4 4.0 %copy-start.5 = (f32[24,768]{1,0:T(8,128)S(1)}, f32[24,768]{1,0:T(8,128)}, u32[]{:S(2)}) copy-start(f32[24,768]{1,0:T(8,128)} %get-tuple-element.108) | copy-start | bytes 221188
  232.4 4.6 %copy-start.4 = (f32[24,768]{1,0:T(8,128)S(1)}, f32[24,768]{1,0:T(8,128)}, u32[]{:S(2)}) copy-start(f32[24,768]{1,0:T(8,128)} %get-tuple-element.110) | copy-start | bytes 221188
  232.4 5.2 %copy-start.3 = (f32[24,768]{1,0:T(8,128)S(1)}, f32[24,768]{1,0:T(8,128)}, u32[]{:S(2)}) copy-start(f32[24,768]{1,0:T(8,128)} %get-tuple-element.111) | copy-start | bytes 221188
  232.4 5.9 %copy-start.2 = (f32[24,768]{1,0:T(8,128)S(1)}, f32[24,768]{1,0:T(8,128)}, u32[]{:S(2)}) copy-start(f32[24,768]{1,0:T(8,128)} %get-tuple-element.113) | copy-start | bytes 221188
  232.4 6.5 %copy-start.1 = (f32[24,3072]{1,0:T(8,128)S(1)}, f32[24,3072]{1,0:T(8,128)}, u32[]{:S(2)}) copy-start(f32[24,3072]{1,0:T(8,128)} %get-tuple-element.117) | copy-start | bytes 884740
  232.4 7.2 %copy-start = (f32[96,768]{1,0:T(8,128)S(1)}, f32[96,768]{1,0:T(8,128)}, u32[]{:S(2)}) copy-start(f32[96,768]{1,0:T(8,128)} %get-tuple-element.119) | copy-start | bytes 884740
